TPU v7x, 128 devices: a whole 4x4x4 slice. The times are simulated.
128 devices in a mesh: region: 16 (over y_lo, z, core), depth: 2 (over y_hi), member: 4 (over x).
Axes of the slice: x: 4, y: 4 (y_hi: 2, y_lo: 2; y = y_hi * 2 + y_lo), z: 4, core: 2. Of those that a mesh axis runs over, the one named last changes fastest.
Arguments:
- ensemble: bfloat16 [14, 384, 16384], P('depth', 'member', 'region'), may hold values from -6 to 6
- obs_weights: float32 [14], P('depth'), may hold values from -1.5 to 1.5
- obs_tiles: int32 [8192], P('region'), may hold values from 0 to 1023
- obs_values: float32 [8192], P('region'), may hold values from -8 to 8
- obs_error: float32 [8192], P('region'), may hold values from 0.2 to 2
- obs_noise: float32 [384, 8192], P('member', 'region'), may hold values from -6 to 6
Outputs:
- analysis: bfloat16 [14, 384, 16384], P('depth', 'member', 'region')
- inflation: float32 [], replicated
Inputs may be any that keep to these rules, and one draw needn't show every extreme that they name: `obs_tiles`: the tile of the observation, counted within the 1024 tiles of the region whose block holds the observation.
All inputs are finite; a program needn't handle non-finite values.
Results may differ from a plain program's by a relative error of at most 0.011.
Values may be sent and summed in bfloat16 or wider, within the bound.
No kernel may reach another device: no remote copies, remote signals or barrier semaphores. Data moves between devices by JAX's collectives and lax.ppermute only.
A program may use at most 64 MiB of HBM per device.

v0:
```python
import jax
import jax.numpy as jnp
from jax import lax
from jax.sharding import PartitionSpec as P

MEMBERS = 384
RADIUS = 1024


def sent_to_all(array, axis):
    copies = jnp.broadcast_to(array, (lax.axis_size(axis), *array.shape))
    return lax.all_to_all(copies, axis, split_axis=0, concat_axis=0, tiled=True)


def taken_together(array, axis):
    return sent_to_all(array, axis).astype(jnp.float32).sum(axis=0)


def over_copies(array, axis):
    return sent_to_all(array, axis).sum(axis=0)


def in_one(arrays, axis):
    flat, at, done = (jnp.concatenate([a.reshape(-1) for a in arrays]), 0, [])
    total = over_copies(flat, axis)
    for a in arrays:
        done.append(total[at : at + a.size].reshape(a.shape))
        at += a.size
    return tuple(done)


def extended(array, sides, width):
    for axis, dim in sides:
        peers, length = (lax.axis_size(axis), array.shape[dim])
        up = [(i, (i + 1) % peers) for i in range(peers - 1)]
        down = [(j, i) for i, j in up]
        last = lax.slice_in_dim(array, length - width, length, axis=dim)
        leading = lax.slice_in_dim(array, 0, width, axis=dim)
        before = lax.ppermute(last, axis, up)
        after = lax.ppermute(leading, axis, down)
        array = jnp.concatenate([before, array, after], axis=dim)
    return array


def sent_together(arrays, axis, dim, along):
    both = jnp.concatenate(arrays, axis=along)
    out, at, done = (lax.all_gather(both, axis, axis=dim, tiled=True), 0, [])
    for a in arrays:
        done.append(lax.slice_in_dim(out, at, at + a.shape[along], axis=along))
        at += a.shape[along]
    return tuple(done)


def in_blocks(array, dim, peers):
    before, after = (array.shape[:dim], array.shape[dim + 1 :])
    return jnp.moveaxis(array.reshape(*before, peers, -1, *after), dim, 0)


def cut_rows(length, count):
    unit = 8 if length >= 8 * count else 1
    return [length // unit * k // count * unit for k in range(1, count)]


def laid_out(parts, dim):
    parts = jnp.moveaxis(parts, 0, dim)
    dims = parts.shape
    return parts.reshape(*dims[:dim], dims[dim] * dims[dim + 1], *dims[dim + 2 :])


def exchange_in_pieces(array, axis, pieces, split_dim, concat_dim):
    parts = in_blocks(array, split_dim, lax.axis_size(axis))
    widest = max(range(1, max(2, parts.ndim - 1)), key=lambda d: parts.shape[d])
    done = []
    for section in jnp.split(parts, cut_rows(parts.shape[widest], pieces), axis=widest):
        if section.size:
            done.append(lax.all_to_all(section, axis, split_axis=0, concat_axis=0, tiled=True))
    return laid_out(jnp.concatenate(done, axis=widest), concat_dim)


def regress(
    anomalies, own_anom, state_mean, obs_anom, perturbed, factor, obs_pos, first_tile, infl_root
):
    var_count = anomalies.shape[0]
    tile_count = anomalies.shape[2]
    block = 128

    def one_block(block_index, output):
        block_start = block_index * block
        slab = lax.dynamic_slice_in_dim(anomalies, block_start, block, 2)
        own_slab = lax.dynamic_slice_in_dim(own_anom, block_start, block, 2)
        means = lax.dynamic_slice_in_dim(state_mean, block_start, block, 1)
        covariance = jnp.einsum(
            "lmt,mj->ltj", slab, obs_anom, preferred_element_type=jnp.float32
        ) / (MEMBERS - 1)
        tile_pos = (first_tile + block_start + jnp.arange(block, dtype=jnp.int32)).astype(
            jnp.float32
        )
        closeness = jnp.maximum(0.0, 1.0 - jnp.abs(tile_pos[:, None] - obs_pos[None, :]) / RADIUS)
        kalman_gain = (covariance * (closeness * closeness * factor[None, :])[None]).astype(
            jnp.bfloat16
        )
        increment = jnp.einsum(
            "ltj,mj->lmt", kalman_gain, perturbed, preferred_element_type=jnp.float32
        )
        updated = (means[:, None, :] + infl_root * own_slab.astype(jnp.float32) + increment).astype(
            jnp.bfloat16
        )
        return lax.dynamic_update_slice_in_dim(output, updated, block_start, 2)

    output = jnp.zeros((var_count, perturbed.shape[0], tile_count), jnp.bfloat16)
    return lax.fori_loop(0, tile_count // block, one_block, output)


def shards(ensemble, obs_weights, obs_tiles, obs_values, obs_error, obs_noise):
    tile_count = ensemble.shape[2]
    own_members = ensemble.shape[1]
    obs_count = obs_tiles.shape[0]
    member_sum = jnp.sum(ensemble, axis=1, dtype=jnp.float32)
    picked = jnp.take(ensemble, obs_tiles, axis=2).astype(jnp.float32)
    partial_pred = jnp.einsum("lmk,l->mk", picked, obs_weights, precision=lax.Precision.HIGHEST)
    predicted = taken_together(partial_pred.astype(jnp.bfloat16), "depth").astype(jnp.float32)
    totals = in_one(
        (member_sum, jnp.sum(predicted, axis=0), jnp.sum(predicted * predicted, axis=0)), "member"
    )
    state_mean = totals[0] / MEMBERS
    obs_mean = totals[1] / MEMBERS
    obs_dev = predicted - obs_mean[None, :]
    obs_spread = (totals[2] - MEMBERS * obs_mean * obs_mean) / (MEMBERS - 1)
    innovation = obs_values - obs_mean
    global_sums = in_one(
        (jnp.sum(innovation * innovation), jnp.sum(obs_spread + obs_error)), "region"
    )
    inflation = global_sums[0] / global_sums[1]
    infl_root = jnp.sqrt(inflation)
    factor = inflation / (inflation * obs_spread + obs_error)
    obs_anom = obs_dev.astype(jnp.bfloat16)
    perturbed = (
        innovation[None, :] + jnp.sqrt(obs_error)[None, :] * obs_noise - infl_root * obs_dev
    ).astype(jnp.bfloat16)
    first_tile = lax.axis_index("region") * tile_count
    obs_pos = (first_tile + obs_tiles).astype(jnp.float32)
    stacked = jnp.concatenate([obs_anom, perturbed], axis=0)
    widened = extended(stacked, (("region", 1),), obs_count)
    near_anom = widened[:own_members]
    near_pert = widened[own_members:]
    scalars = jnp.stack([factor, obs_pos], axis=0)
    wide_scalars = extended(scalars, (("region", 1),), obs_count)
    near_factor = wide_scalars[0]
    near_pos = wide_scalars[1]
    anomalies = (ensemble.astype(jnp.float32) - state_mean[:, None, :]).astype(jnp.bfloat16)
    all_obs_anom, all_pert = sent_together((near_anom, near_pert), "member", 0, 1)
    share = tile_count // lax.axis_size("member")
    offset = lax.axis_index("member") * share
    split_anom = exchange_in_pieces(anomalies, "member", 2, 2, 1)
    split_mean = lax.dynamic_slice_in_dim(state_mean, offset, share, 1)
    updated = regress(
        split_anom,
        split_anom,
        split_mean,
        all_obs_anom,
        all_pert,
        near_factor,
        near_pos,
        first_tile + offset,
        infl_root,
    )
    analysis = lax.all_to_all(updated, "member", split_axis=1, concat_axis=2, tiled=True)
    return (analysis, inflation)


def solution(mesh):
    return jax.shard_map(
        shards,
        mesh=mesh,
        in_specs=(
            P("depth", "member", "region"),
            P("depth"),
            P("region"),
            P("region"),
            P("region"),
            P("member", "region"),
        ),
        out_specs=(P("depth", "member", "region"), P()),
        check_vma=False,
    )
```

profile of v0, /device:TPU:96, one launch (start us, length us, event | category | flops | bytes accessed | tf_op | source)
XLA Modules:
  0.0 161.5 jit_solution(6960265160344156900)
XLA Ops:
  8.6 3.2 %copy.36 = bf16[7,96,1024]{1,0,2:T(8,128)(2,1)S(1)} copy(bf16[7,96,1024]{2,1,0:T(8,128)(2,1)} %param.8) | data formatting | bytes 2752512 | tf_op args[0]
  11.8 1.8 %gather_fusion = bf16[512,7,96]{2,1,0:T(8,128)(2,1)S(1)} fusion(bf16[7,96,1024]{1,0,2:T(8,128)(2,1)S(1)} %copy.36, s32[1024]{0:T(1024)S(1)} %pad_clamp_fusion), kind=kCustom, calls=%fused_computation | custom fusion | bytes 1378304 | tf_op jit(solution)/shard_map/jit(_take)/gather | solution.py:119
  13.6 1.8 %select_bitcast_fusion = bf16[7,96,512]{1,0,2:T(8,128)(2,1)S(1)} fusion(bf16[512,7,96]{2,1,0:T(8,128)(2,1)S(1)} %gather_fusion, pred[512]{0:T(512)(128)(4,1)S(1)} %compare_and_fusion), kind=kLoop, calls=%fused_computation.15 | loop fusion | flops 344064 | bytes 1376768 | tf_op jit(solution)/shard_map/jit(_take)/select_n | solution.py:119
  17.9 4.5 %all-to-all-start = ((bf16[2,96,512]{2,1,0:T(8,128)(2,1)}), bf16[2,96,512]{2,1,0:T(8,128)(2,1)S(1)}, u32[]{:S(2)}, u32[]{:S(2)}) async-start(bf16[2,96,512]{2,1,0:T(8,128)(2,1)} %broadcast_in_dim.41), calls=%async_computation | async-start | bytes 393216 | tf_op jit(solution)/shard_map/all_to_all | solution.py:12
  22.8 6.0 %all-to-all-done = bf16[2,96,512]{2,1,0:T(8,128)(2,1)S(1)} async-done(((bf16[2,96,512]{2,1,0:T(8,128)(2,1)}), bf16[2,96,512]{2,1,0:T(8,128)(2,1)S(1)}, u32[]{:S(2)}, u32[]{:S(2)}) %all-to-all-start) | async-done | bytes 196640 | tf_op jit(solution)/shard_map/all_to_all | solution.py:12
  28.9 10.1 %all_to_all.45 = f32[4,1,8192]{2,1,0:T(1,128)S(1)} all-to-all(f32[4,1,8192]{2,1,0:T(1,128)S(1)} %broadcast_in_dim.42), channel_id=1, replica_groups=mesh['region'=16,'depth'=2,'member'=4] {'member'}, dimensions={0} | all-to-all | bytes 262144 | tf_op jit(solution)/shard_map/all_to_all | solution.py:12
  39.7 1.4 pad_maximum_fusion.7
  41.1 8.5 %all_to_all.46 = f32[16,1,2]{2,1,0:T(1,128)S(1)} all-to-all(f32[16,1,2]{2,1,0:T(1,128)S(1)} %broadcast_in_dim.43), channel_id=1, replica_groups=mesh['region'=16,'depth'=2,'member'=4] {'region'}, dimensions={0} | all-to-all | bytes 256 | tf_op jit(solution)/shard_map/all_to_all | solution.py:12
  51.8 1.9 %collective-permute-start.1 = (bf16[192,512]{1,0:T(8,128)(2,1)S(1)}, bf16[192,512]{1,0:T(8,128)(2,1)S(1)}, u32[]{:S(2)}, u32[]{:S(2)}) collective-permute-start(bf16[192,512]{1,0:T(8,128)(2,1)S(1)} %pad_maximum_fusion.3), channel_id=1, source_target_pairs={{8,0},{16,8},{24,16},{32,24},{40,32},{48,40},{56,48},{64,56},{72,6... | collective-permute-start | bytes 589832 | tf_op jit(solution)/shard_map/ppermute | solution.py:40
  53.7 2.4 %collective-permute-start = (bf16[192,512]{1,0:T(8,128)(2,1)S(1)}, bf16[192,512]{1,0:T(8,128)(2,1)S(1)}, u32[]{:S(2)}, u32[]{:S(2)}) collective-permute-start(bf16[192,512]{1,0:T(8,128)(2,1)S(1)} %pad_maximum_fusion.3), channel_id=1, source_target_pairs={{0,8},{8,16},{16,24},{24,32},{32,40},{40,48},{48,56},{56,64},{64,7... | collective-permute-start | bytes 589832 | tf_op jit(solution)/shard_map/ppermute | solution.py:39
  56.9 3.8 %collective-permute-done = bf16[192,512]{1,0:T(8,128)(2,1)S(1)} collective-permute-done((bf16[192,512]{1,0:T(8,128)(2,1)S(1)}, bf16[192,512]{1,0:T(8,128)(2,1)S(1)}, u32[]{:S(2)}, u32[]{:S(2)}) %collective-permute-start) | collective-permute-done | bytes 196640 | tf_op jit(solution)/shard_map/ppermute | solution.py:39
  64.6 3.5 %all-to-all-start.3 = ((bf16[4,7,48,256]{3,2,1,0:T(8,128)(2,1)}), bf16[4,7,48,256]{3,2,1,0:T(8,128)(2,1)S(1)}, u32[]{:S(2)}, u32[]{:S(2)}) async-start(bf16[4,7,48,256]{3,2,1,0:T(8,128)(2,1)} %copy.39), calls=%async_computation.3 | async-start | bytes 1376256 | tf_op jit(solution)/shard_map/all_to_all | solution.py:76
  68.1 1.9 %collective-permute-start.3 = (f32[2,512]{1,0:T(2,128)S(1)}, f32[2,512]{1,0:T(2,128)S(1)}, u32[]{:S(2)}, u32[]{:S(2)}) collective-permute-start(f32[2,512]{1,0:T(2,128)S(1)} %pad_maximum_fusion.6), channel_id=1, source_target_pairs={{8,0},{16,8},{24,16},{32,24},{40,32},{48,40},{56,48},{64,56},{72,6... | collective-permute-start | bytes 12296 | tf_op jit(solution)/shard_map/ppermute | solution.py:40
  70.0 3.1 %collective-permute-start.2 = (f32[2,512]{1,0:T(2,128)S(1)}, f32[2,512]{1,0:T(2,128)S(1)}, u32[]{:S(2)}, u32[]{:S(2)}) collective-permute-start(f32[2,512]{1,0:T(2,128)S(1)} %pad_maximum_fusion.6), channel_id=1, source_target_pairs={{0,8},{8,16},{16,24},{24,32},{32,40},{40,48},{48,56},{56,64},{64,7... | collective-permute-start | bytes 12296 | tf_op jit(solution)/shard_map/ppermute | solution.py:39
  74.1 11.2 %all-to-all-done.3 = bf16[4,7,48,256]{3,2,1,0:T(8,128)(2,1)S(1)} async-done(((bf16[4,7,48,256]{3,2,1,0:T(8,128)(2,1)}), bf16[4,7,48,256]{3,2,1,0:T(8,128)(2,1)S(1)}, u32[]{:S(2)}, u32[]{:S(2)}) %all-to-all-start.3) | async-done | bytes 688160 | tf_op jit(solution)/shard_map/all_to_all | solution.py:76
  85.3 3.5 %all-to-all-start.4 = ((bf16[4,7,48,256]{3,2,1,0:T(8,128)(2,1)}), bf16[4,7,48,256]{3,2,1,0:T(8,128)(2,1)S(1)}, u32[]{:S(2)}, u32[]{:S(2)}) async-start(bf16[4,7,48,256]{3,2,1,0:T(8,128)(2,1)} %copy.40), calls=%async_computation.4 | async-start | bytes 1376256 | tf_op jit(solution)/shard_map/all_to_all | solution.py:76
  88.9 18.1 %all-to-all-done.4 = bf16[4,7,48,256]{3,2,1,0:T(8,128)(2,1)S(1)} async-done(((bf16[4,7,48,256]{3,2,1,0:T(8,128)(2,1)}), bf16[4,7,48,256]{3,2,1,0:T(8,128)(2,1)S(1)}, u32[]{:S(2)}, u32[]{:S(2)}) %all-to-all-start.4) | async-done | bytes 688160 | tf_op jit(solution)/shard_map/all_to_all | solution.py:76
  107.3 3.2 %fusion.10 = (bf16[384,1536]{1,0:T(8,128)(2,1)}, bf16[384,1536]{1,0:T(8,128)(2,1)}) fusion(bf16[384,3072]{1,0:T(8,128)(2,1)} %all-gather.2.cloned.1.call-done), kind=kLoop, calls=%fused_computation.43 | loop fusion | bytes 4718592 | tf_op jit(solution)/shard_map/slice | solution.py:49
  111.7 12.9 %while.13 = (s32[]{:T(128)}, bf16[7,384,256]{1,2,0:T(8,128)(2,1)}, f32[7,256]{1,0:T(8,128)S(1)}, f32[]{:T(128)}, bf16[7,384,256]{2,1,0:T(8,128)(2,1)S(1)}, /*ind...) while((s32[]{:T(128)}, bf16[7,384,256]{1,2,0:T(8,128)(2,1)}, ...), condition=%wide.region_9.10_spmd, body=%wide.region_8.9_spmd.sunk | while | flops 2119975168 | bytes 8799963 | solution.py:111
  112.6 5.6 %fusion.21 = bf16[7,384,256]{1,2,0:T(8,128)(2,1)} fusion(bf16[7,384,256]{1,2,0:T(8,128)(2,1)} %get-tuple-element.341, s32[]{:T(128)S(6)} %select_n.31, bf16[7,384,128]{1,2,0:T(8,128)(2,1)S(1)} %copy.62, bf16[384,1536]{1,0:T(8,128)(2,1)} %get-tuple-element.364, f32[128,1536]{1,0:T(8,128)S(1)} %multiply_multiply_fusion.2, ...), kind=kOutput, calls=%fused_computation.4.clone.1 | convolution fusion | flops 2118402048 | bytes 5215744 | tf_op jit(solution)/shard_map/while/body/eval_jaxpr/ltj,mj->lmt/dot_general | solution.py:102
  119.0 5.6 %fusion.21 = bf16[7,384,256]{1,2,0:T(8,128)(2,1)} fusion(bf16[7,384,256]{1,2,0:T(8,128)(2,1)} %get-tuple-element.341, s32[]{:T(128)S(6)} %select_n.31, bf16[7,384,128]{1,2,0:T(8,128)(2,1)S(1)} %copy.62, bf16[384,1536]{1,0:T(8,128)(2,1)} %get-tuple-element.364, f32[128,1536]{1,0:T(8,128)S(1)} %multiply_multiply_fusion.2, ...), kind=kOutput, calls=%fused_computation.4.clone.1 | convolution fusion | flops 2118402048 | bytes 5215744 | tf_op jit(solution)/shard_map/while/body/eval_jaxpr/ltj,mj->lmt/dot_general | solution.py:102
  124.6 2.3 %copy.44 = bf16[7,384,256]{2,0,1:T(8,128)(2,1)S(1)} copy(bf16[7,384,256]{1,2,0:T(8,128)(2,1)} %get-tuple-element.171) | data formatting | bytes 2752512 | tf_op jit(solution)/shard_map/while | solution.py:111
  126.9 23.6 %all_to_all.47 = bf16[7,384,256]{2,0,1:T(8,128)(2,1)S(1)} all-to-all(bf16[7,384,256]{2,0,1:T(8,128)(2,1)S(1)} %copy.44), channel_id=1, replica_groups=mesh['region'=16,'depth'=2,'member'=4] {'member'}, dimensions={1} | all-to-all | bytes 2752512 | tf_op jit(solution)/shard_map/all_to_all | solution.py:167
  151.7 1.8 %all_to_all.38 = bf16[7,96,1024]{2,1,0:T(8,128)(2,1)} reshape(bf16[7,96,4,256]{3,2,1,0:T(4,128)(2,1)S(1)} %copy.46) | data formatting | bytes 2752512 | tf_op jit(solution)/shard_map/all_to_all | solution.py:167
  (69 shorter events, 15.7 us)
Async XLA Ops:
  7.2 9.3 %copy-start = (f32[7]{0:T(128)S(1)}, f32[7]{0:T(128)}, u32[]{:S(2)}) copy-start(f32[7]{0:T(128)} %param.9) | copy-start | bytes 88
  16.4 6.0 %copy-start.1 = (bf16[7,96,1024]{2,1,0:T(8,128)(2,1)S(1)}, bf16[7,96,1024]{2,1,0:T(8,128)(2,1)}, u32[]{:S(2)}) copy-start(bf16[7,96,1024]{2,1,0:T(8,128)(2,1)} %param.8) | copy-start | bytes 4128772
  17.9 10.8 %all-to-all-start = ((bf16[2,96,512]{2,1,0:T(8,128)(2,1)}), bf16[2,96,512]{2,1,0:T(8,128)(2,1)S(1)}, u32[]{:S(2)}, u32[]{:S(2)}) async-start(bf16[2,96,512]{2,1,0:T(8,128)(2,1)} %broadcast_in_dim.41), calls=%async_computation | async-start | bytes 393216 | tf_op jit(solution)/shard_map/all_to_all | solution.py:12
  22.4 16.7 %copy-start.3 = (f32[512]{0:T(512)S(1)}, f32[512]{0:T(512)}, u32[]{:S(2)}) copy-start(f32[512]{0:T(512)} %param.12) | copy-start | bytes 6148
  22.4 16.7 %copy-start.4 = (f32[512]{0:T(512)S(1)}, f32[512]{0:T(512)}, u32[]{:S(2)}) copy-start(f32[512]{0:T(512)} %param.11) | copy-start | bytes 6148
  22.4 29.3 %copy-start.2 = (f32[96,512]{1,0:T(8,128)S(1)}, f32[96,512]{1,0:T(8,128)}, u32[]{:S(2)}) copy-start(f32[96,512]{1,0:T(8,128)} %param.13) | copy-start | bytes 589828
  22.4 84.9 %all-gather.2.cloned.1.call-start = ((), (), s32[]{:S(2)}) async-start(), calls=%async_computation.6 | async-start | bytes 2949120 | tf_op jit(solution)/shard_map/all_gather | solution.py:47
  51.8 5.1 %collective-permute-start.1 = (bf16[192,512]{1,0:T(8,128)(2,1)S(1)}, bf16[192,512]{1,0:T(8,128)(2,1)S(1)}, u32[]{:S(2)}, u32[]{:S(2)}) collective-permute-start(bf16[192,512]{1,0:T(8,128)(2,1)S(1)} %pad_maximum_fusion.3), channel_id=1, source_target_pairs={{8,0},{16,8},{24,16},{32,24},{40,32},{48,40},{56,48},{64,56},{72,6... | collective-permute-start | bytes 589832 | tf_op jit(solution)/shard_map/ppermute | solution.py:40
  53.7 7.0 %collective-permute-start = (bf16[192,512]{1,0:T(8,128)(2,1)S(1)}, bf16[192,512]{1,0:T(8,128)(2,1)S(1)}, u32[]{:S(2)}, u32[]{:S(2)}) collective-permute-start(bf16[192,512]{1,0:T(8,128)(2,1)S(1)} %pad_maximum_fusion.3), channel_id=1, source_target_pairs={{0,8},{8,16},{16,24},{24,32},{32,40},{40,48},{48,56},{56,64},{64,7... | collective-permute-start | bytes 589832 | tf_op jit(solution)/shard_map/ppermute | solution.py:39
  64.6 20.7 %all-to-all-start.3 = ((bf16[4,7,48,256]{3,2,1,0:T(8,128)(2,1)}), bf16[4,7,48,256]{3,2,1,0:T(8,128)(2,1)S(1)}, u32[]{:S(2)}, u32[]{:S(2)}) async-start(bf16[4,7,48,256]{3,2,1,0:T(8,128)(2,1)} %copy.39), calls=%async_computation.3 | async-start | bytes 1376256 | tf_op jit(solution)/shard_map/all_to_all | solution.py:76
  68.1 20.7 %collective-permute-start.3 = (f32[2,512]{1,0:T(2,128)S(1)}, f32[2,512]{1,0:T(2,128)S(1)}, u32[]{:S(2)}, u32[]{:S(2)}) collective-permute-start(f32[2,512]{1,0:T(2,128)S(1)} %pad_maximum_fusion.6), channel_id=1, source_target_pairs={{8,0},{16,8},{24,16},{32,24},{40,32},{48,40},{56,48},{64,56},{72,6... | collective-permute-start | bytes 12296 | tf_op jit(solution)/shard_map/ppermute | solution.py:40
  70.0 18.8 %collective-permute-start.2 = (f32[2,512]{1,0:T(2,128)S(1)}, f32[2,512]{1,0:T(2,128)S(1)}, u32[]{:S(2)}, u32[]{:S(2)}) collective-permute-start(f32[2,512]{1,0:T(2,128)S(1)} %pad_maximum_fusion.6), channel_id=1, source_target_pairs={{0,8},{8,16},{16,24},{24,32},{32,40},{40,48},{48,56},{56,64},{64,7... | collective-permute-start | bytes 12296 | tf_op jit(solution)/shard_map/ppermute | solution.py:39
  85.3 21.7 %all-to-all-start.4 = ((bf16[4,7,48,256]{3,2,1,0:T(8,128)(2,1)}), bf16[4,7,48,256]{3,2,1,0:T(8,128)(2,1)S(1)}, u32[]{:S(2)}, u32[]{:S(2)}) async-start(bf16[4,7,48,256]{3,2,1,0:T(8,128)(2,1)} %copy.40), calls=%async_computation.4 | async-start | bytes 1376256 | tf_op jit(solution)/shard_map/all_to_all | solution.py:76
Sparse Core Ops, SparseCore 0:
  61.8 43.3 all-gather.1
where the time goes:
time: 162 us
  blocking collectives  42.3 us (26%)
  waiting for transfers between devices  39.9 us (25%)
  local copies, waits for them, and re-layouts  21.7 us (13%)
  starting transfers between devices  20.8 us (13%)
  between operations  16.9 us (10%)
  matrix products  12 us (7%)
  other arithmetic  7.83 us (5%)
    all_to_all x2, waiting for transfers between devices, exchange_in_pieces(): lax.all_to_all(section, axis, split_axis=0, concat_axis=0, tiled=True)  29.4 us
    all_to_all x1, blocking collectives, shards(): lax.all_to_all(updated, 'member', split_axis=1, concat_axis=2, tiled=True)  23.6 us
    all_to_all x2, blocking collectives, sent_to_all(): return lax.all_to_all(copies, axis, split_axis=0, concat_axis=0, tiled=True)  18.6 us
    dot_general x2, matrix products, one_block(): jnp.einsum('ltj,mj->lmt', kalman_gain, perturbed, preferred_element_type=...  11.2 us
    all_to_all x2, starting transfers between devices, exchange_in_pieces(): lax.all_to_all(section, axis, split_axis=0, concat_axis=0, tiled=True)  6.98 us
    all_to_all x1, waiting for transfers between devices, sent_to_all(): return lax.all_to_all(copies, axis, split_axis=0, concat_axis=0, tiled=True)  5.97 us
    ppermute x2, starting transfers between devices, extended(): before = lax.ppermute(last, axis, up)  5.52 us
    all_to_all x1, starting transfers between devices, sent_to_all(): return lax.all_to_all(copies, axis, split_axis=0, concat_axis=0, tiled=True)  4.46 us
  transfers between devices with their start and end apart: 8, of which 5 were waited for; matrix products, arithmetic and copies ran while one was open for 3% of the time, Pallas kernels for 0%

commit v1 on v0

v1 whole, which is shorter than its diff:
```python
import functools

import jax
import jax.numpy as jnp
from jax import lax
from jax.experimental import pallas as pl
from jax.experimental.pallas import tpu as pltpu
from jax.sharding import PartitionSpec as P

RADIUS = 1024
F32 = jnp.float32
BF16 = jnp.bfloat16


def params(**more):
    return pltpu.CompilerParams(vmem_limit_bytes=56 * 2**20, **more)


def whole():
    return pl.BlockSpec(memory_space=pltpu.VMEM)


def scalars():
    return pl.BlockSpec(memory_space=pltpu.SMEM)


def shape_of(shape, dtype=BF16):
    return jax.ShapeDtypeStruct(shape, dtype)


def split_rows(value):
    first = value.astype(BF16)
    rest = value - first.astype(F32)
    second = rest.astype(BF16)
    third = (rest - second.astype(F32)).astype(BF16)
    return [first, second, third]


def pack_body(weights, ensemble, tiles, blocks, predicted, total):
    step = pl.program_id(0)
    var_count, _, width = ensemble.shape
    blocks[0] = ensemble[...]
    mixed = weights[0] * ensemble[0].astype(F32)
    for l in range(1, var_count):
        mixed = mixed + weights[l] * ensemble[l].astype(F32)
    high = mixed.astype(BF16)
    low = (mixed - high.astype(F32)).astype(BF16)
    rows = lax.broadcasted_iota(jnp.int32, (width, tiles.shape[1]), 0)
    chosen = jnp.where(tiles[...] - step * width == rows, 1.0, 0.0).astype(BF16)
    picked = jnp.dot(high, chosen, preferred_element_type=F32)
    picked = picked + jnp.dot(low, chosen, preferred_element_type=F32)

    @pl.when(step == 0)
    def _():
        total[...] = picked

    @pl.when(step > 0)
    def _():
        total[...] += picked

    @pl.when(step == pl.num_programs(0) - 1)
    def _():
        predicted[...] = total[...].astype(BF16)


def pack(ensemble, weights, tiles, peers):
    var_count, own, tile_count = ensemble.shape
    width = tile_count // peers
    obs = tiles.shape[1]
    return pl.pallas_call(
        pack_body,
        grid=(peers,),
        in_specs=[
            scalars(),
            pl.BlockSpec((var_count, own, width), lambda j: (0, 0, j)),
            pl.BlockSpec((1, obs), lambda j: (0, 0)),
        ],
        out_specs=[
            pl.BlockSpec((1, var_count, own, width), lambda j: (j, 0, 0, 0)),
            pl.BlockSpec((own, obs), lambda j: (0, 0)),
        ],
        out_shape=[shape_of((peers, var_count, own, width)), shape_of((own, obs))],
        scratch_shapes=[pltpu.VMEM((own, obs), F32)],
        compiler_params=params(),
        name="pack",
    )(weights, ensemble, tiles)


def join_body(mine, other, noise, error, out):
    own = mine.shape[0]
    predicted = (mine[...].astype(F32) + other[...].astype(F32)).astype(BF16)
    scaled = (jnp.sqrt(error[...]) * noise[...]).astype(BF16)
    for j in range(out.shape[0]):
        out[j, :own] = predicted
        out[j, own:] = scaled


def join(mine, other, noise, error, peers):
    own, obs = mine.shape
    return pl.pallas_call(
        join_body,
        in_specs=[whole()] * 4,
        out_specs=whole(),
        out_shape=shape_of((peers, 2 * own, obs)),
        compiler_params=params(),
        name="join",
    )(mine, other, noise, error)


def stats_body(gathered, values, error, tiles, packet, sums):
    peers, double, obs = gathered.shape
    own = double // 2
    members = peers * own
    total = jnp.zeros((1, obs), F32)
    for j in range(peers):
        total = total + jnp.sum(gathered[j, :own].astype(F32), axis=0, keepdims=True)
    mean = total / members
    square = jnp.zeros((1, obs), F32)
    for j in range(peers):
        dev = gathered[j, :own].astype(F32) - mean
        square = square + jnp.sum(dev * dev, axis=0, keepdims=True)
        packet[j * own : (j + 1) * own] = dev.astype(BF16)
        packet[members + j * own : members + (j + 1) * own] = gathered[j, own:]
    spread = square / (members - 1)
    innovation = values[...] - mean
    place = tiles[...]
    rows = split_rows(innovation) + split_rows(error[...]) + split_rows(spread)
    rows += [(place // 32).astype(F32).astype(BF16), (place % 32).astype(F32).astype(BF16)]
    rows += [jnp.zeros((1, obs), BF16)] * (16 - len(rows))
    packet[2 * members :] = jnp.concatenate(rows, axis=0)
    above = jnp.sum(innovation * innovation)
    below = jnp.sum(spread + error[...])
    lane = lax.broadcasted_iota(jnp.int32, sums.shape, 1)
    sums[...] = jnp.where(lane == 0, above, jnp.where(lane == 1, below, 0.0))


def stats(gathered, values, error, tiles, regions):
    peers, double, obs = gathered.shape
    return pl.pallas_call(
        stats_body,
        in_specs=[whole()] * 4,
        out_specs=[whole(), whole()],
        out_shape=[shape_of((peers * double + 16, obs)), shape_of((regions, 128), F32)],
        compiler_params=params(),
        name="stats",
    )(gathered, values, error, tiles)


def prepare_body(offset, left, mine, right, sums, anom_t, perturbed, taper, inflation_out, *, tile_count):
    total, obs = mine.shape
    members = (total - 16) // 2
    width = taper.shape[1]
    folded = jnp.sum(sums[...], axis=0, keepdims=True)
    inflation = folded[:, 0:1] / folded[:, 1:2]
    root = jnp.sqrt(inflation)
    inflation_out[...] = jnp.broadcast_to(inflation, inflation_out.shape)
    tile = (offset[0] + lax.broadcasted_iota(jnp.int32, (1, width), 1)).astype(F32)
    for n, packet in enumerate((left, mine, right)):
        anom = packet[:members]
        anom_t[n * obs : (n + 1) * obs] = anom.T
        rows = packet[2 * members :].astype(F32)
        innovation = rows[0:1] + rows[1:2] + rows[2:3]
        error = rows[3:4] + rows[4:5] + rows[5:6]
        spread = rows[6:7] + rows[7:8] + rows[8:9]
        place = rows[9:10] * 32.0 + rows[10:11] + (n - 1.0) * tile_count
        scaled = packet[members : 2 * members].astype(F32)
        perturbed[:, n * obs : (n + 1) * obs] = (
            innovation + scaled - root * anom.astype(F32)
        ).astype(BF16)
        bottom = inflation * spread + error
        factor = jnp.where(error > 0.0, inflation / jnp.where(error > 0.0, bottom, 1.0), 0.0)
        factor = factor / (members - 1)
        columns = jnp.concatenate([place, factor, jnp.zeros((6, obs), F32)], axis=0).T
        near = jnp.maximum(0.0, 1.0 - jnp.abs(tile - columns[:, 0:1]) / RADIUS)
        taper[n * obs : (n + 1) * obs] = near * near * columns[:, 1:2]


def prepare(offset, left, mine, right, sums, width, tile_count):
    total, obs = mine.shape
    members = (total - 16) // 2
    return pl.pallas_call(
        functools.partial(prepare_body, tile_count=tile_count),
        in_specs=[scalars()] + [whole()] * 4,
        out_specs=[whole()] * 4,
        out_shape=[
            shape_of((3 * obs, members)),
            shape_of((members, 3 * obs)),
            shape_of((3 * obs, width), F32),
            shape_of((8, 128), F32),
        ],
        compiler_params=params(),
        name="prepare",
    )(offset, left, mine, right, sums)


def regress_body(states, anom_t, perturbed, taper, inflation, out, gain, *, first, count):
    peers, _, own, width = states.shape
    members = peers * own
    root = jnp.sqrt(inflation[0:1, 0:1])
    obs = taper.shape[0]
    block = 512

    def one(l, carry):
        state = states[:, first + l].astype(F32).reshape(members, width)
        mean = jnp.sum(state, axis=0, keepdims=True) / members
        anom = (state - mean).astype(BF16)
        for k in range(0, obs, block):
            covariance = jnp.dot(anom_t[k : k + block], anom, preferred_element_type=F32)
            gain[k : k + block] = (covariance * taper[k : k + block]).astype(BF16)
        increment = jnp.dot(perturbed[...], gain[...], preferred_element_type=F32)
        result = mean + root * anom.astype(F32) + increment
        out[:, l] = result.astype(BF16).reshape(peers, own, width)
        return carry

    lax.fori_loop(0, count, one, 0)


def regress(states, anom_t, perturbed, taper, inflation, first, count):
    peers, _, own, width = states.shape
    return pl.pallas_call(
        functools.partial(regress_body, first=first, count=count),
        in_specs=[whole()] * 5,
        out_specs=whole(),
        out_shape=shape_of((peers, count, own, width)),
        scratch_shapes=[pltpu.VMEM(taper.shape, BF16)],
        compiler_params=params(),
        name=f"regress{first}",
    )(states, anom_t, perturbed, taper, inflation)


def place_body(first, second, out):
    count = first.shape[1]
    out[:count] = first[0]
    out[count:] = second[0]


def place(first, second):
    peers, count, own, width = first.shape
    rest = second.shape[1]
    return pl.pallas_call(
        place_body,
        grid=(peers,),
        in_specs=[
            pl.BlockSpec((1, count, own, width), lambda j: (j, 0, 0, 0)),
            pl.BlockSpec((1, rest, own, width), lambda j: (j, 0, 0, 0)),
        ],
        out_specs=pl.BlockSpec((count + rest, own, width), lambda j: (0, 0, j)),
        out_shape=shape_of((count + rest, own, peers * width)),
        compiler_params=params(),
        name="place",
    )(first, second)


def exchanged(blocks, axis):
    return lax.all_to_all(blocks, axis, split_axis=0, concat_axis=0, tiled=True)


def shards(ensemble, obs_weights, obs_tiles, obs_values, obs_error, obs_noise):
    peers = lax.axis_size("member")
    regions = lax.axis_size("region")
    width = ensemble.shape[2] // peers
    tiles, values, error = (a[None, :] for a in (obs_tiles, obs_values, obs_error))
    blocks, partial = pack(ensemble, obs_weights, tiles, peers)
    other = lax.ppermute(partial, "depth", [(0, 1), (1, 0)])
    states = exchanged(blocks, "member")
    gathered = exchanged(join(partial, other, obs_noise, error, peers), "member")
    packet, sums = stats(gathered, values, error, tiles, regions)
    up = [(i, i + 1) for i in range(regions - 1)]
    left = lax.ppermute(packet, "region", up)
    right = lax.ppermute(packet, "region", [(j, i) for i, j in up])
    all_sums = exchanged(sums, "region")
    offset = (lax.axis_index("member") * width).astype(jnp.int32)[None]
    anom_t, perturbed, taper, inflation = prepare(
        offset, left, packet, right, all_sums, width, ensemble.shape[2]
    )
    count = ensemble.shape[0]
    half = (count + 1) // 2
    parts = []
    for first, size in ((0, half), (half, count - half)):
        updated = regress(states, anom_t, perturbed, taper, inflation, first, size)
        parts.append(exchanged(updated, "member"))
    return (place(*parts), inflation[0, 0])


def solution(mesh):
    return jax.shard_map(
        shards,
        mesh=mesh,
        in_specs=(
            P("depth", "member", "region"),
            P("depth"),
            P("region"),
            P("region"),
            P("region"),
            P("member", "region"),
        ),
        out_specs=(P("depth", "member", "region"), P()),
        check_vma=False,
    )
```

time: 162 us -> 111 us (0.69)
  Pallas kernels: 0 us -> 31.4 us
  local copies, waits for them, and re-layouts: 21.7 us -> 3.81 us
  blocking collectives: 42.3 us -> 25.3 us
  between operations: 16.9 us -> 0.69 us
  matrix products: 12 us -> 0 us
  waiting for transfers between devices: 39.9 us -> 29 us
  other arithmetic: 7.83 us -> 0 us
    pallas_call x0 -> x7, Pallas kernels: none -> 31.4 us  [the longest x2 15 us: regress(): pl.pallas_call(functools.partial(regress_body, first=first, count=count),...]
    all_to_all x3, waiting for transfers between devices: 35.3 us -> 14.6 us  [exchanged(): return lax.all_to_all(blocks, axis, split_axis=0, concat_axis=0, tiled=True)]
    all_to_all x3 -> x2, blocking collectives: 42.3 us -> 25.3 us  [exchanged(): return lax.all_to_all(blocks, axis, split_axis=0, concat_axis=0, tiled=True)]
    dot_general x3 -> x0, matrix products: 12 us -> none  [the longest x2 11.2 us: one_block(): jnp.einsum('ltj,mj->lmt', kalman_gain, perturbed, preferred_element_type=...]
    ppermute x4 -> x3, waiting for transfers between devices: 4.58 us -> 14.4 us  [the longest x1 7.37 us: shards(): right = lax.ppermute(packet, 'region', [(j, i) for i, j in up])]
    all_to_all x2 -> x0, local copies, waits for them, and re-layouts: 3.01 us -> none  [shards(): lax.all_to_all(updated, 'member', split_axis=1, concat_axis=2, tiled=True)]
    slice x4 -> x1, local copies, waits for them, and re-layouts: 3.81 us -> 1.19 us  [shards(): return (place(*parts), inflation[0, 0])]
    concatenate x7 -> x0, other arithmetic: 2.47 us -> none  [the longest x2 1.37 us: in_one(): flat, at, done = (jnp.concatenate([a.reshape(-1) for a in arrays]), 0, [])]
  transfers between devices with their start and end apart: 8 -> 6, of which waited for: 5 -> 5; matrix products, arithmetic and copies ran while one was open for 3% -> 1% of each run, Pallas kernels for 0% -> 11%
where the time goes in v1:
time: 111 us; the launch traced here: 110 us
  Pallas kernels  31.4 us (28%)
  waiting for transfers between devices  29 us (26%)
  blocking collectives  25.3 us (23%)
  starting transfers between devices  19.3 us (17%)
  local copies, waits for them, and re-layouts  3.81 us (3%)
    all_to_all x2, blocking collectives, exchanged(): return lax.all_to_all(blocks, axis, split_axis=0, concat_axis=0, tiled=True)  25.3 us
    pallas_call x2, Pallas kernels, regress(): pl.pallas_call(functools.partial(regress_body, first=first, count=count),...  15 us
    all_to_all x3, waiting for transfers between devices, exchanged(): return lax.all_to_all(blocks, axis, split_axis=0, concat_axis=0, tiled=True)  14.6 us
    all_to_all x3, starting transfers between devices, exchanged(): return lax.all_to_all(blocks, axis, split_axis=0, concat_axis=0, tiled=True)  11.8 us
    ppermute x1, waiting for transfers between devices, shards(): right = lax.ppermute(packet, 'region', [(j, i) for i, j in up])  7.37 us
    pallas_call x1, Pallas kernels, prepare(): pl.pallas_call(functools.partial(prepare_body, tile_count=tile_count), in...  4.43 us
    pallas_call x1, Pallas kernels, pack(): pl.pallas_call(pack_body, grid=(peers,), in_specs=[scalars(), pl.BlockSpe...  4.18 us
    ppermute x1, waiting for transfers between devices, shards(): left = lax.ppermute(packet, 'region', up)  3.93 us
  transfers between devices with their start and end apart: 6, of which 5 were waited for; matrix products, arithmetic and copies ran while one was open for 1% of the time, Pallas kernels for 11%

profile of v1, /device:TPU:96, one launch (start us, length us, event | category | flops | bytes accessed | tf_op | source)
XLA Modules:
  0.0 109.5 jit_solution(3872396116821963621)
XLA Ops:
  0.6 4.2 %pack.1 = (bf16[4,7,96,256]{3,2,1,0:T(8,128)(2,1)}, bf16[96,512]{1,0:T(8,128)(2,1)}) custom-call(f32[7]{0:T(128)} %weights.1, bf16[7,96,1024]{2,1,0:T(8,128)(2,1)} %ensemble.1, s32[1,512]{1,0:T(1,128)} %bitcast.10), custom_call_target="tpu_custom_call" | custom-call | tf_op jit(solution)/shard_map/pack/pallas_call | solution.py:70
  4.8 3.2 %collective-permute-start = (bf16[96,512]{1,0:T(8,128)(2,1)}, bf16[96,512]{1,0:T(8,128)(2,1)S(1)}, u32[]{:S(2)}, u32[]{:S(2)}) collective-permute-start(bf16[96,512]{1,0:T(8,128)(2,1)} %get-tuple-element.11.mine), channel_id=1, source_target_pairs={{0,4},{4,0},{1,5},{5,1},{2,6},{6,2},{3,7},{7,3},{8,12},{12,8},{9,1... | collective-permute-start | bytes 294920 | tf_op jit(solution)/shard_map/ppermute | solution.py:264
  8.0 3.1 %collective-permute-done.other = bf16[96,512]{1,0:T(8,128)(2,1)S(1)} collective-permute-done((bf16[96,512]{1,0:T(8,128)(2,1)}, bf16[96,512]{1,0:T(8,128)(2,1)S(1)}, u32[]{:S(2)}, u32[]{:S(2)}) %collective-permute-start) | collective-permute-done | bytes 98336 | tf_op jit(solution)/shard_map/ppermute | solution.py:264
  11.1 0.6 copy-done.5
  11.8 2.0 %join.1 = bf16[4,192,512]{2,1,0:T(8,128)(2,1)} custom-call(bf16[96,512]{1,0:T(8,128)(2,1)} %get-tuple-element.11.mine, bf16[96,512]{1,0:T(8,128)(2,1)} %copy-done.5, f32[96,512]{1,0:T(8,128)} %noise.1, f32[1,512]{1,0:T(1,128)} %bitcast.12), custom_call_target="tpu_custom_call" | custom-call | tf_op jit(solution)/shard_map/join/pallas_call | solution.py:100
  13.8 15.7 %all_to_all.31.gathered = bf16[4,192,512]{2,1,0:T(8,128)(2,1)} all-to-all(bf16[4,192,512]{2,1,0:T(8,128)(2,1)} %join.1), channel_id=1, replica_groups=mesh['region'=16,'depth'=2,'member'=4] {'member'}, dimensions={0} | all-to-all | bytes 1572864 | tf_op jit(solution)/shard_map/all_to_all | solution.py:255
  29.4 2.3 %stats.1 = (bf16[784,512]{1,0:T(8,128)(2,1)}, f32[16,128]{1,0:T(8,128)}) custom-call(bf16[4,192,512]{2,1,0:T(8,128)(2,1)} %all_to_all.31.gathered, f32[1,512]{1,0:T(1,128)} %bitcast.15, f32[1,512]{1,0:T(1,128)} %bitcast.13, s32[1,512]{1,0:T(1,128)} %bitcast.11), custom_call_target="tpu_custom_call" | custom-call | tf_op jit(solution)/shard_map/stats/pallas_call | solution.py:139
  31.8 9.6 %all_to_all.32 = f32[16,1,128]{2,1,0:T(1,128)} all-to-all(f32[16,1,128]{2,1,0:T(1,128)} %bitcast.14), channel_id=1, replica_groups=mesh['region'=16,'depth'=2,'member'=4] {'region'}, dimensions={0} | all-to-all | bytes 16384 | tf_op jit(solution)/shard_map/all_to_all | solution.py:255
  41.4 3.7 %all-to-all-start = ((bf16[4,7,96,256]{3,2,1,0:T(8,128)(2,1)}), bf16[4,7,96,256]{3,2,1,0:T(8,128)(2,1)S(1)}, u32[]{:S(2)}, u32[]{:S(2)}) async-start(bf16[4,7,96,256]{3,2,1,0:T(8,128)(2,1)} %get-tuple-element.10), calls=%async_computation | async-start | bytes 2752512 | tf_op jit(solution)/shard_map/all_to_all | solution.py:255
  45.1 2.1 %collective-permute-start.2 = (bf16[784,512]{1,0:T(8,128)(2,1)S(1)}, bf16[784,512]{1,0:T(8,128)(2,1)S(1)}, u32[]{:S(2)}, u32[]{:S(2)}) collective-permute-start(bf16[784,512]{1,0:T(8,128)(2,1)S(1)} %copy-done.3), channel_id=1, source_target_pairs={{8,0},{16,8},{24,16},{32,24},{40,32},{48,40},{56,48},{64,56},{72,6... | collective-permute-start | bytes 2408456 | tf_op jit(solution)/shard_map/ppermute | solution.py:270
  47.1 2.3 %collective-permute-start.1 = (bf16[784,512]{1,0:T(8,128)(2,1)S(1)}, bf16[784,512]{1,0:T(8,128)(2,1)}, u32[]{:S(2)}, u32[]{:S(2)}) collective-permute-start(bf16[784,512]{1,0:T(8,128)(2,1)S(1)} %copy-done.3), channel_id=1, source_target_pairs={{0,8},{8,16},{16,24},{24,32},{32,40},{40,48},{48,56},{56,64},{64,7... | collective-permute-start | bytes 2408456 | tf_op jit(solution)/shard_map/ppermute | solution.py:269
  49.4 7.4 %collective-permute-done.2.right = bf16[784,512]{1,0:T(8,128)(2,1)S(1)} collective-permute-done((bf16[784,512]{1,0:T(8,128)(2,1)S(1)}, bf16[784,512]{1,0:T(8,128)(2,1)S(1)}, u32[]{:S(2)}, u32[]{:S(2)}) %collective-permute-start.2) | collective-permute-done | bytes 802848 | tf_op jit(solution)/shard_map/ppermute | solution.py:270
  56.8 3.9 %collective-permute-done.1.left = bf16[784,512]{1,0:T(8,128)(2,1)} collective-permute-done((bf16[784,512]{1,0:T(8,128)(2,1)S(1)}, bf16[784,512]{1,0:T(8,128)(2,1)}, u32[]{:S(2)}, u32[]{:S(2)}) %collective-permute-start.1) | collective-permute-done | bytes 802848 | tf_op jit(solution)/shard_map/ppermute | solution.py:269
  60.7 4.4 %prepare.1 = (bf16[1536,384]{1,0:T(8,128)(2,1)}, bf16[384,1536]{1,0:T(8,128)(2,1)}, f32[1536,256]{1,0:T(8,128)}, f32[8,128]{1,0:T(8,128)}) custom-call(s32[1]{0:T(128)} %bitcast.1.offset, bf16[784,512]{1,0:T(8,128)(2,1)} %collective-permute-done.1.left, bf16[784,512]{1,0:T(8,128)(2,1)} %get-tuple-element.12.mine, bf16[784,512]{1,0:T(8,128)(2,1)} %copy-done.4, ...), custom_call_target="tpu_custom_call" | custom-call | tf_op jit(solution)/shard_map/prepare/pallas_call | solution.py:181
  65.2 1.1 copy-done
  66.3 6.9 %regress4.1 = bf16[4,3,96,256]{3,2,1,0:T(8,128)(2,1)} custom-call(bf16[4,7,96,256]{3,2,1,0:T(8,128)(2,1)} %copy-done, bf16[1536,384]{1,0:T(8,128)(2,1)} %get-tuple-element.14.anom_t, bf16[384,1536]{1,0:T(8,128)(2,1)} %get-tuple-element.15.perturbed, f32[1536,256]{1,0:T(8,128)} %get-tuple-element.16.taper, f32[8,128]{1,0:T(8,128)} %get-tuple-element.17.inflation), custom_call_target="tpu_custom_call" | custom-call | tf_op jit(solution)/shard_map/regress4/pallas_call | solution.py:220
  73.1 4.6 %all-to-all-start.4 = ((bf16[4,3,96,256]{3,2,1,0:T(8,128)(2,1)}), bf16[4,3,96,256]{3,2,1,0:T(8,128)(2,1)S(1)}, u32[]{:S(2)}, u32[]{:S(2)}) async-start(bf16[4,3,96,256]{3,2,1,0:T(8,128)(2,1)} %regress4.1), calls=%async_computation.4 | async-start | bytes 1179648 | tf_op jit(solution)/shard_map/all_to_all | solution.py:255
  77.7 8.1 %regress0.1 = bf16[4,4,96,256]{3,2,1,0:T(8,128)(2,1)} custom-call(bf16[4,7,96,256]{3,2,1,0:T(8,128)(2,1)} %copy-done, bf16[1536,384]{1,0:T(8,128)(2,1)} %get-tuple-element.14.anom_t, bf16[384,1536]{1,0:T(8,128)(2,1)} %get-tuple-element.15.perturbed, f32[1536,256]{1,0:T(8,128)} %get-tuple-element.16.taper, f32[8,128]{1,0:T(8,128)} %get-tuple-element.17.inflation), custom_call_target="tpu_custom_call" | custom-call | tf_op jit(solution)/shard_map/regress0/pallas_call | solution.py:220
  85.8 3.2 %all-to-all-done.4.second = bf16[4,3,96,256]{3,2,1,0:T(8,128)(2,1)S(1)} async-done(((bf16[4,3,96,256]{3,2,1,0:T(8,128)(2,1)}), bf16[4,3,96,256]{3,2,1,0:T(8,128)(2,1)S(1)}, u32[]{:S(2)}, u32[]{:S(2)}) %all-to-all-start.4) | async-done | bytes 589856 | tf_op jit(solution)/shard_map/all_to_all | solution.py:255
  89.0 3.5 %all-to-all-start.3 = ((bf16[4,4,96,256]{3,2,1,0:T(8,128)(2,1)}), bf16[4,4,96,256]{3,2,1,0:T(8,128)(2,1)S(1)}, u32[]{:S(2)}, u32[]{:S(2)}) async-start(bf16[4,4,96,256]{3,2,1,0:T(8,128)(2,1)} %regress0.1), calls=%async_computation.3 | async-start | bytes 1572864 | tf_op jit(solution)/shard_map/all_to_all | solution.py:255
  92.5 1.2 %slice.3 = f32[1,1]{1,0:T(1,128)} slice(f32[8,128]{1,0:T(8,128)} %get-tuple-element.17.inflation), slice={[0:1], [0:1]} | slice | bytes 8 | tf_op jit(solution)/shard_map/slice | solution.py:282
  93.7 11.3 %all-to-all-done.3.first = bf16[4,4,96,256]{3,2,1,0:T(8,128)(2,1)S(1)} async-done(((bf16[4,4,96,256]{3,2,1,0:T(8,128)(2,1)}), bf16[4,4,96,256]{3,2,1,0:T(8,128)(2,1)S(1)}, u32[]{:S(2)}, u32[]{:S(2)}) %all-to-all-start.3) | async-done | bytes 786464 | tf_op jit(solution)/shard_map/all_to_all | solution.py:255
  105.1 0.9 copy-done.1
  106.0 3.5 %place.1 = bf16[7,96,1024]{2,1,0:T(8,128)(2,1)} custom-call(bf16[4,4,96,256]{3,2,1,0:T(8,128)(2,1)} %copy-done.1, bf16[4,3,96,256]{3,2,1,0:T(8,128)(2,1)} %copy-done.2), custom_call_target="tpu_custom_call" | custom-call | tf_op jit(solution)/shard_map/place/pallas_call | solution.py:240
  (10 shorter events, 0.0 us)
Async XLA Ops:
  4.8 6.3 %collective-permute-start = (bf16[96,512]{1,0:T(8,128)(2,1)}, bf16[96,512]{1,0:T(8,128)(2,1)S(1)}, u32[]{:S(2)}, u32[]{:S(2)}) collective-permute-start(bf16[96,512]{1,0:T(8,128)(2,1)} %get-tuple-element.11.mine), channel_id=1, source_target_pairs={{0,4},{4,0},{1,5},{5,1},{2,6},{6,2},{3,7},{7,3},{8,12},{12,8},{9,1... | collective-permute-start | bytes 294920 | tf_op jit(solution)/shard_map/ppermute | solution.py:264
  11.1 0.6 copy-start.5
  41.4 3.7 %copy-start.3 = (bf16[784,512]{1,0:T(8,128)(2,1)S(1)}, bf16[784,512]{1,0:T(8,128)(2,1)}, u32[]{:S(2)}) copy-start(bf16[784,512]{1,0:T(8,128)(2,1)} %get-tuple-element.12.mine) | copy-start | bytes 2408452
  41.4 23.8 %all-to-all-start = ((bf16[4,7,96,256]{3,2,1,0:T(8,128)(2,1)}), bf16[4,7,96,256]{3,2,1,0:T(8,128)(2,1)S(1)}, u32[]{:S(2)}, u32[]{:S(2)}) async-start(bf16[4,7,96,256]{3,2,1,0:T(8,128)(2,1)} %get-tuple-element.10), calls=%async_computation | async-start | bytes 2752512 | tf_op jit(solution)/shard_map/all_to_all | solution.py:255
  45.1 11.7 %collective-permute-start.2 = (bf16[784,512]{1,0:T(8,128)(2,1)S(1)}, bf16[784,512]{1,0:T(8,128)(2,1)S(1)}, u32[]{:S(2)}, u32[]{:S(2)}) collective-permute-start(bf16[784,512]{1,0:T(8,128)(2,1)S(1)} %copy-done.3), channel_id=1, source_target_pairs={{8,0},{16,8},{24,16},{32,24},{40,32},{48,40},{56,48},{64,56},{72,6... | collective-permute-start | bytes 2408456 | tf_op jit(solution)/shard_map/ppermute | solution.py:270
  47.1 13.6 %collective-permute-start.1 = (bf16[784,512]{1,0:T(8,128)(2,1)S(1)}, bf16[784,512]{1,0:T(8,128)(2,1)}, u32[]{:S(2)}, u32[]{:S(2)}) collective-permute-start(bf16[784,512]{1,0:T(8,128)(2,1)S(1)} %copy-done.3), channel_id=1, source_target_pairs={{0,8},{8,16},{16,24},{24,32},{32,40},{40,48},{48,56},{56,64},{64,7... | collective-permute-start | bytes 2408456 | tf_op jit(solution)/shard_map/ppermute | solution.py:269
  56.8 3.9 %copy-start.4 = (bf16[784,512]{1,0:T(8,128)(2,1)}, bf16[784,512]{1,0:T(8,128)(2,1)S(1)}, u32[]{:S(2)}) copy-start(bf16[784,512]{1,0:T(8,128)(2,1)S(1)} %collective-permute-done.2.right) | copy-start | bytes 2408452
  65.2 1.1 copy-start
  73.1 15.9 %all-to-all-start.4 = ((bf16[4,3,96,256]{3,2,1,0:T(8,128)(2,1)}), bf16[4,3,96,256]{3,2,1,0:T(8,128)(2,1)S(1)}, u32[]{:S(2)}, u32[]{:S(2)}) async-start(bf16[4,3,96,256]{3,2,1,0:T(8,128)(2,1)} %regress4.1), calls=%async_computation.4 | async-start | bytes 1179648 | tf_op jit(solution)/shard_map/all_to_all | solution.py:255
  89.0 16.0 %copy-start.2 = (bf16[4,3,96,256]{3,2,1,0:T(8,128)(2,1)}, bf16[4,3,96,256]{3,2,1,0:T(8,128)(2,1)S(1)}, u32[]{:S(2)}) copy-start(bf16[4,3,96,256]{3,2,1,0:T(8,128)(2,1)S(1)} %all-to-all-done.4.second) | copy-start | bytes 1769476
  89.0 16.0 %all-to-all-start.3 = ((bf16[4,4,96,256]{3,2,1,0:T(8,128)(2,1)}), bf16[4,4,96,256]{3,2,1,0:T(8,128)(2,1)S(1)}, u32[]{:S(2)}, u32[]{:S(2)}) async-start(bf16[4,4,96,256]{3,2,1,0:T(8,128)(2,1)} %regress0.1), calls=%async_computation.3 | async-start | bytes 1572864 | tf_op jit(solution)/shard_map/all_to_all | solution.py:255
  105.1 0.9 copy-start.1

commit v2 on v1

v2 whole, which is shorter than its diff:
```python
import functools

import jax
import jax.numpy as jnp
from jax import lax
from jax.experimental import pallas as pl
from jax.experimental.pallas import tpu as pltpu
from jax.sharding import PartitionSpec as P


RADIUS = 1024
F32 = jnp.float32
BF16 = jnp.bfloat16


def params(megabytes=12):
    return pltpu.CompilerParams(vmem_limit_bytes=megabytes * 2**20)


def whole():
    return pl.BlockSpec(memory_space=pltpu.VMEM)


def scalars():
    return pl.BlockSpec(memory_space=pltpu.SMEM)


def anywhere():
    return pl.BlockSpec(memory_space=pl.ANY)


def shape_of(shape, dtype=BF16):
    return pltpu.VMEM(shape, dtype)


def in_vmem(values):
    return [pltpu.with_memory_space_constraint(v, pltpu.VMEM) for v in values]


def split_rows(value):
    first = value.astype(BF16)
    rest = value - first.astype(F32)
    second = rest.astype(BF16)
    third = (rest - second.astype(F32)).astype(BF16)
    return [first, second, third]


def tile_block(me, s, width):
    return pl.multiple_of(jnp.bitwise_xor(me, s) * width, width)


def pack_body(me, weights, ensemble, tiles, *rest):
    *blocks, predicted, arrived = rest
    peers = len(blocks)
    var_count, _, width = blocks[0].shape
    starts = [tile_block(me[0], s, width) for s in range(peers)]
    loads = [
        pltpu.make_async_copy(
            ensemble.at[:, :, pl.ds(starts[s], width)], blocks[s], arrived.at[s]
        )
        for s in range(peers)
    ]
    for load in loads:
        load.start()
    rows = lax.broadcasted_iota(jnp.int32, (width, tiles.shape[1]), 0)
    total = jnp.zeros(predicted.shape, F32)
    for s in range(peers):
        chosen = jnp.where(tiles[...] - starts[s] == rows, 1.0, 0.0).astype(BF16)
        loads[s].wait()
        mixed = weights[0] * blocks[s][0].astype(F32)
        for l in range(1, var_count):
            mixed = mixed + weights[l] * blocks[s][l].astype(F32)
        high = mixed.astype(BF16)
        low = (mixed - high.astype(F32)).astype(BF16)
        total = total + jnp.dot(high, chosen, preferred_element_type=F32)
        total = total + jnp.dot(low, chosen, preferred_element_type=F32)
    predicted[...] = total.astype(BF16)


def pack(me, ensemble, weights, tiles, peers):
    var_count, own, tile_count = ensemble.shape
    width = tile_count // peers
    obs = tiles.shape[1]
    return pl.pallas_call(
        pack_body,
        in_specs=[scalars(), scalars(), anywhere(), whole()],
        out_specs=[whole()] * (peers + 1),
        out_shape=[shape_of((var_count, own, width))] * peers + [shape_of((own, obs))],
        scratch_shapes=[pltpu.SemaphoreType.DMA((peers,))],
        compiler_params=params(),
        name="pack",
    )(me, weights, pltpu.with_memory_space_constraint(ensemble, pltpu.HBM), tiles)


def join_body(mine, other, noise, error, out):
    own = mine.shape[0]
    predicted = (mine[...].astype(F32) + other[...].astype(F32)).astype(BF16)
    scaled = (jnp.sqrt(error[...]) * noise[...]).astype(BF16)
    for j in range(out.shape[0]):
        out[j, :own] = predicted
        out[j, own:] = scaled


def join(mine, other, noise, error, peers):
    own, obs = mine.shape
    return pl.pallas_call(
        join_body,
        in_specs=[whole()] * 4,
        out_specs=whole(),
        out_shape=shape_of((peers, 2 * own, obs)),
        compiler_params=params(),
        name="join",
    )(mine, other, noise, error)


def stats_body(me, gathered, values, error, tiles, packet, sums):
    peers, double, obs = gathered.shape
    own = double // 2
    members = peers * own
    total = jnp.zeros((1, obs), F32)
    for j in range(peers):
        total = total + jnp.sum(gathered[j, :own].astype(F32), axis=0, keepdims=True)
    mean = total / members
    square = jnp.zeros((1, obs), F32)
    for j in range(peers):
        dev = gathered[j, :own].astype(F32) - mean
        square = square + jnp.sum(dev * dev, axis=0, keepdims=True)
    for s in range(peers):
        j = jnp.bitwise_xor(me[0], s)
        dev = gathered[j, :own].astype(F32) - mean
        packet[s * own : (s + 1) * own] = dev.astype(BF16)
        packet[members + s * own : members + (s + 1) * own] = gathered[j, own:]
    spread = square / (members - 1)
    innovation = values[...] - mean
    place = tiles[...]
    rows = split_rows(innovation) + split_rows(error[...]) + split_rows(spread)
    rows += [(place // 32).astype(F32).astype(BF16), (place % 32).astype(F32).astype(BF16)]
    rows += [jnp.zeros((1, obs), BF16)] * (16 - len(rows))
    packet[2 * members :] = jnp.concatenate(rows, axis=0)
    above = jnp.sum(innovation * innovation)
    below = jnp.sum(spread + error[...])
    lane = lax.broadcasted_iota(jnp.int32, sums.shape, 1)
    sums[...] = jnp.where(lane == 0, above, jnp.where(lane == 1, below, 0.0))


def stats(me, gathered, values, error, tiles, regions):
    peers, double, obs = gathered.shape
    return pl.pallas_call(
        stats_body,
        in_specs=[scalars()] + [whole()] * 4,
        out_specs=[whole(), whole()],
        out_shape=[shape_of((peers * double + 16, obs)), shape_of((regions, 128), F32)],
        compiler_params=params(),
        name="stats",
    )(me, gathered, values, error, tiles)


def scalar_rows(packet, members):
    rows = packet[2 * members :].astype(F32)
    innovation = rows[0:1] + rows[1:2] + rows[2:3]
    error = rows[3:4] + rows[4:5] + rows[5:6]
    spread = rows[6:7] + rows[7:8] + rows[8:9]
    return innovation, error, spread, rows[9:10] * 32.0 + rows[10:11]


def gains_body(offset, *refs, tile_count, peers):
    states, packets = refs[:peers], refs[peers : peers + 3]
    gain, anomalies, means, anom_t, taper = refs[peers + 3 :]
    var_count, own, width = states[0].shape
    members = peers * own
    obs = packets[0].shape[1]
    tile = (offset[0] + lax.broadcasted_iota(jnp.int32, (1, width), 1)).astype(F32)
    for n, packet in enumerate(packets):
        anom_t[n * obs : (n + 1) * obs] = packet[:members].T
        place = scalar_rows(packet, members)[3] + (offset[1 + n] * tile_count).astype(F32)
        column = jnp.broadcast_to(place, (8, obs)).T[:, 0:1]
        near = jnp.maximum(0.0, 1.0 - jnp.abs(tile - column) / RADIUS)
        taper[n * obs : (n + 1) * obs] = near * near / (members - 1)
    for l in range(var_count):
        state = [states[s][l].astype(F32) for s in range(peers)]
        total = sum(jnp.sum(a, axis=0, keepdims=True) for a in state)
        mean = total / members
        means[l] = jnp.broadcast_to(mean, means.shape[1:])
        for s in range(peers):
            anomalies[l, s * own : (s + 1) * own] = (state[s] - mean).astype(BF16)
        for k in range(0, 3 * obs, obs):
            covariance = jnp.dot(anom_t[k : k + obs], anomalies[l], preferred_element_type=F32)
            gain[l, k : k + obs] = (covariance * taper[k : k + obs]).astype(BF16)


def gains(offset, states, packets, tile_count):
    var_count, own, width = states[0].shape
    peers = len(states)
    members = peers * own
    obs = packets[0].shape[1]
    return pl.pallas_call(
        functools.partial(gains_body, tile_count=tile_count, peers=peers),
        in_specs=[scalars()] + [whole()] * (peers + 3),
        out_specs=[whole()] * 3,
        out_shape=[
            shape_of((var_count, 3 * obs, width)),
            shape_of((var_count, members, width)),
            shape_of((var_count, 8, width), F32),
        ],
        scratch_shapes=[pltpu.VMEM((3 * obs, members), BF16), pltpu.VMEM((3 * obs, width), F32)],
        compiler_params=params(),
        name="gains",
    )(offset, *in_vmem(states), *in_vmem(packets))


def update(gain, anomalies, means, perturbed, root, blocks, l, at):
    own = blocks[0].shape[1]
    increment = jnp.dot(perturbed[...], gain[l], preferred_element_type=F32)
    result = means[l, 0:1] + root * anomalies[l].astype(F32) + increment
    for s, block in enumerate(blocks):
        block[at] = result[s * own : (s + 1) * own].astype(BF16)


def first_body(*refs, count, peers):
    gain, anomalies, means, sums = refs[:4]
    packets, blocks, (perturbed, root_out, inflation_out) = refs[4:7], refs[7 : 7 + peers], refs[7 + peers :]
    members = anomalies.shape[1]
    obs = packets[0].shape[1]
    folded = jnp.sum(sums[...], axis=0, keepdims=True)
    inflation = folded[:, 0:1] / folded[:, 1:2]
    inflation_out[0] = jnp.sum(inflation)
    root = jnp.sqrt(inflation)
    root_out[...] = jnp.broadcast_to(root, root_out.shape)
    for n, packet in enumerate(packets):
        innovation, error, spread, _ = scalar_rows(packet, members)
        bottom = jnp.where(error > 0.0, inflation * spread + error, 1.0)
        factor = jnp.where(error > 0.0, inflation / bottom, 0.0)
        scaled = packet[members : 2 * members].astype(F32)
        dev = packet[:members].astype(F32)
        perturbed[:, n * obs : (n + 1) * obs] = (
            factor * (innovation + scaled - root * dev)
        ).astype(BF16)
    for l in range(count):
        update(gain, anomalies, means, perturbed, root, blocks, l, l)


def first_updates(gain, anomalies, means, sums, packets, count, peers):
    _, members, width = anomalies.shape
    own = members // peers
    obs = packets[0].shape[1]
    out = pl.pallas_call(
        functools.partial(first_body, count=count, peers=peers),
        in_specs=[whole()] * 7,
        out_specs=[whole()] * (peers + 2) + [scalars()],
        out_shape=[shape_of((count, own, width))] * peers
        + [shape_of((members, 3 * obs)), shape_of((8, 128), F32), jax.ShapeDtypeStruct((1,), F32)],
        compiler_params=params(),
        name="first",
    )(*in_vmem((gain, anomalies, means, sums)), *in_vmem(packets))
    return out[:peers], out[peers], out[peers + 1], out[peers + 2]


def second_body(gain, anomalies, means, perturbed, root, *blocks, first):
    for l in range(blocks[0].shape[0]):
        update(gain, anomalies, means, perturbed, root[0:1, 0:1], blocks, first + l, l)


def second_updates(gain, anomalies, means, perturbed, root, first, peers):
    var_count, members, width = anomalies.shape
    own = members // peers
    return pl.pallas_call(
        functools.partial(second_body, first=first),
        in_specs=[whole()] * 5,
        out_specs=[whole()] * peers,
        out_shape=[shape_of((var_count - first, own, width))] * peers,
        compiler_params=params(),
        name="second",
    )(*in_vmem((gain, anomalies, means, perturbed, root)))


def place_body(me, *refs, first, peers):
    blocks, out, done = refs[:peers], refs[-2], refs[-1]
    count, _, width = blocks[0].shape
    copies = [
        pltpu.make_async_copy(
            blocks[s],
            out.at[first : first + count, :, pl.ds(tile_block(me[0], s, width), width)],
            done.at[s],
        )
        for s in range(peers)
    ]
    for copy in copies:
        copy.start()
    for copy in copies:
        copy.wait()


def place(me, blocks, first, var_count, before=None):
    peers = len(blocks)
    _, own, width = blocks[0].shape
    more = [] if before is None else [before]
    return pl.pallas_call(
        functools.partial(place_body, first=first, peers=peers),
        in_specs=[scalars()] + [anywhere()] * (peers + len(more)),
        out_specs=anywhere(),
        out_shape=pltpu.HBM((var_count, own, peers * width), BF16),
        scratch_shapes=[pltpu.SemaphoreType.DMA((peers,))],
        input_output_aliases={1 + peers: 0} if more else {},
        compiler_params=params(),
    )(me, *in_vmem(blocks), *more)


def swapped(value, axis, distance):
    pairs = [(i, i ^ distance) for i in range(lax.axis_size(axis))]
    return lax.ppermute(value, axis, pairs)


def exchanged(blocks, axis):
    return lax.all_to_all(blocks, axis, split_axis=0, concat_axis=0, tiled=True)


def traded(blocks, order):
    out = list(blocks)
    for s in order:
        out[s] = swapped(blocks[s], "member", s)
    return out


def shards(ensemble, obs_weights, obs_tiles, obs_values, obs_error, obs_noise):
    peers = lax.axis_size("member")
    regions = lax.axis_size("region")
    var_count, _, tile_count = ensemble.shape
    width = tile_count // peers
    me = lax.axis_index("member").astype(jnp.int32)[None]
    region = lax.axis_index("region").astype(jnp.int32)
    tiles, values, error = (a[None, :] for a in (obs_tiles, obs_values, obs_error))
    *blocks, partial = pack(me, ensemble, obs_weights, tiles, peers)
    other = swapped(partial, "depth", 1)
    states = traded(blocks, (1, 3, 2))
    joined = join(partial, other, obs_noise, error, peers)
    gathered = exchanged(joined, "member")
    packet, sums = stats(me, gathered, values, error, tiles, regions)
    near = swapped(packet, "region", 1)
    pairs = [(i, i + 1) for i in range(1, regions - 1, 2)]
    far = lax.ppermute(packet, "region", pairs + [(j, i) for i, j in pairs])
    all_sums = exchanged(sums, "region")
    side = 1 - 2 * (region % 2)
    offset = jnp.stack([me[0] * width, jnp.zeros_like(side), side, -side])
    packets = (packet, near, far)
    gain, anomalies, means = gains(offset, states, packets, tile_count)
    half = var_count // 2
    ready, perturbed, root, inflation = first_updates(
        gain, anomalies, means, all_sums, packets, half, peers
    )
    early = traded(ready, (1, 3, 2))
    ready = second_updates(gain, anomalies, means, perturbed, root, half, peers)
    late = traded(ready, (1, 3, 2))
    output = place(me, early, 0, var_count)
    output = place(me, late, half, var_count, output)
    return (output, inflation.reshape(()))


def solution(mesh):
    return jax.shard_map(
        shards,
        mesh=mesh,
        in_specs=(
            P("depth", "member", "region"),
            P("depth"),
            P("region"),
            P("region"),
            P("region"),
            P("member", "region"),
        ),
        out_specs=(P("depth", "member", "region"), P()),
        check_vma=False,
    )
```

time: 111 us -> 93.2 us (0.84)
  the two profiles are of different devices: /device:TPU:96 before, /device:TPU:0 now
where the time goes in v2:
time: 93.2 us; the launch traced here: 92.8 us
  starting transfers between devices  25.4 us (27%)
  waiting for transfers between devices  25.4 us (27%)
  blocking collectives  15.3 us (16%)
  Pallas kernels  13.5 us (14%)
  local copies, waits for them, and re-layouts  12.3 us (13%)
    ppermute x11, waiting for transfers between devices, swapped(): return lax.ppermute(value, axis, pairs)  25.4 us
    ppermute x11, starting transfers between devices, swapped(): return lax.ppermute(value, axis, pairs)  18.7 us
    all_to_all x1, blocking collectives, exchanged(): return lax.all_to_all(blocks, axis, split_axis=0, concat_axis=0, tiled=True)  15.3 us
    unnamed x28, local copies, waits for them, and re-layouts  12.3 us
    all_to_all x1, starting transfers between devices, exchanged(): return lax.all_to_all(blocks, axis, split_axis=0, concat_axis=0, tiled=True)  5.98 us
    pallas_call x1, Pallas kernels, gains(): pl.pallas_call(functools.partial(gains_body, tile_count=tile_count, peers...  4.74 us
    pallas_call x1, Pallas kernels, pack(): pl.pallas_call(pack_body, in_specs=[scalars(), scalars(), anywhere(), who...  3.15 us
  transfers between devices with their start and end apart: 13, of which 6 were waited for; matrix products, arithmetic and copies ran while one was open for 0% of the time, Pallas kernels for 8%

profile of v2, /device:TPU:0, one launch (start us, length us, event | category | flops | bytes accessed | tf_op | source)
XLA Modules:
  0.0 92.8 jit_solution(2613828955192725318)
XLA Ops:
  2.0 3.2 %pack.1 = (bf16[7,96,256]{2,1,0:T(8,128)(2,1)S(1)}, bf16[7,96,256]{2,1,0:T(8,128)(2,1)}, bf16[7,96,256]{2,1,0:T(8,128)(2,1)}, bf16[7,96,256]{2,1,0:T(8,128)(2,1)}, bf16[96,512]{1,0:T(8,128)(2,1)S(1)}) custom-call(s32[1]{0:T(128)} %bitcast.me, f32[7]{0:T(128)S(1)} %copy-done.13, bf16[7,96,1024]{2,1,0:T(8,128)(2,1)} %ensemble.1, s32[1,512]{1,0:T(1,128)S(1)} %bitcast.13), custom_call_target="tpu_custom_call" | custom-call | tf_op jit(solution)/shard_map/pack/pallas_call | solution.py:84
  5.2 3.4 %collective-permute-start.3 = (bf16[96,512]{1,0:T(8,128)(2,1)S(1)}, bf16[96,512]{1,0:T(8,128)(2,1)S(1)}, u32[]{:S(2)}, u32[]{:S(2)}) collective-permute-start(bf16[96,512]{1,0:T(8,128)(2,1)S(1)} %get-tuple-element.27.mine), channel_id=1, source_target_pairs={{0,4},{4,0},{1,5},{5,1},{2,6},{6,2},{3,7},{7,3},{8,12},{12,8},{9,1... | collective-permute-start | bytes 294920 | tf_op jit(solution)/shard_map/ppermute | solution.py:310
  8.6 2.8 %collective-permute-done.3.other = bf16[96,512]{1,0:T(8,128)(2,1)S(1)} collective-permute-done((bf16[96,512]{1,0:T(8,128)(2,1)S(1)}, bf16[96,512]{1,0:T(8,128)(2,1)S(1)}, u32[]{:S(2)}, u32[]{:S(2)}) %collective-permute-start.3) | collective-permute-done | bytes 98336 | tf_op jit(solution)/shard_map/ppermute | solution.py:310
  11.5 15.3 %all_to_all.16.gathered = bf16[4,192,512]{2,1,0:T(8,128)(2,1)S(1)} all-to-all(bf16[4,192,512]{2,1,0:T(8,128)(2,1)S(1)} %join.1), channel_id=1, replica_groups=mesh['region'=16,'depth'=2,'member'=4] {'member'}, dimensions={0} | all-to-all | bytes 1572864 | tf_op jit(solution)/shard_map/all_to_all | solution.py:314
  28.5 3.3 %collective-permute-start.4 = (bf16[784,512]{1,0:T(8,128)(2,1)S(1)}, bf16[784,512]{1,0:T(8,128)(2,1)S(1)}, u32[]{:S(2)}, u32[]{:S(2)}) collective-permute-start(bf16[784,512]{1,0:T(8,128)(2,1)S(1)} %get-tuple-element.28.refs_4_), channel_id=1, source_target_pairs={{0,8},{8,0},{16,24},{24,16},{32,40},{40,32},{48,56},{56,48},{64,72... | collective-permute-start | bytes 2408456 | tf_op jit(solution)/shard_map/ppermute | solution.py:310
  32.4 2.1 %collective-permute-start.1 = (bf16[7,96,256]{2,1,0:T(8,128)(2,1)}, bf16[7,96,256]{2,1,0:T(8,128)(2,1)}, u32[]{:S(2)}, u32[]{:S(2)}) collective-permute-start(bf16[7,96,256]{2,1,0:T(8,128)(2,1)} %get-tuple-element.25), channel_id=1, source_target_pairs={{0,2},{1,3},{2,0},{3,1},{4,6},{5,7},{6,4},{7,5},{8,10},{9,11},{10,... | collective-permute-start | bytes 1032200 | tf_op jit(solution)/shard_map/ppermute | solution.py:310
  34.5 2.1 %collective-permute-start.2 = (bf16[7,96,256]{2,1,0:T(8,128)(2,1)}, bf16[7,96,256]{2,1,0:T(8,128)(2,1)}, u32[]{:S(2)}, u32[]{:S(2)}) collective-permute-start(bf16[7,96,256]{2,1,0:T(8,128)(2,1)} %get-tuple-element.26), channel_id=1, source_target_pairs={{0,3},{1,2},{2,1},{3,0},{4,7},{5,6},{6,5},{7,4},{8,11},{9,10},{10,... | collective-permute-start | bytes 1032200 | tf_op jit(solution)/shard_map/ppermute | solution.py:310
  36.5 6.0 %all-to-all-start.1 = ((f32[16,1,128]{2,1,0:T(1,128)}), f32[16,1,128]{2,1,0:T(1,128)S(1)}, u32[]{:S(2)}, u32[]{:S(2)}) async-start(f32[16,1,128]{2,1,0:T(1,128)} %bitcast.8), calls=%async_computation.1 | async-start | bytes 16384 | tf_op jit(solution)/shard_map/all_to_all | solution.py:314
  43.7 6.6 %collective-permute-done.1.refs_2_ = bf16[7,96,256]{2,1,0:T(8,128)(2,1)} collective-permute-done((bf16[7,96,256]{2,1,0:T(8,128)(2,1)}, bf16[7,96,256]{2,1,0:T(8,128)(2,1)}, u32[]{:S(2)}, u32[]{:S(2)}) %collective-permute-start.1) | collective-permute-done | bytes 344096 | tf_op jit(solution)/shard_map/ppermute | solution.py:310
  50.3 2.6 %collective-permute-done.2.refs_3_ = bf16[7,96,256]{2,1,0:T(8,128)(2,1)} collective-permute-done((bf16[7,96,256]{2,1,0:T(8,128)(2,1)}, bf16[7,96,256]{2,1,0:T(8,128)(2,1)}, u32[]{:S(2)}, u32[]{:S(2)}) %collective-permute-start.2) | collective-permute-done | bytes 344096 | tf_op jit(solution)/shard_map/ppermute | solution.py:310
  53.7 1.1 %copy-done.4 = bf16[784,512]{1,0:T(8,128)(2,1)S(1)} copy-done((bf16[784,512]{1,0:T(8,128)(2,1)S(1)}, bf16[784,512]{1,0:T(8,128)(2,1)}, u32[]{:S(2)}) %copy-start.4) | copy-done | bytes 802840
  55.9 4.7 %gains.1 = (bf16[7,1536,256]{2,1,0:T(8,128)(2,1)S(1)}, bf16[7,384,256]{2,1,0:T(8,128)(2,1)S(1)}, f32[7,8,256]{2,1,0:T(8,128)S(1)}) custom-call(s32[4]{0:T(128)S(1)} %pad_add_fusion.offset, bf16[7,96,256]{2,1,0:T(8,128)(2,1)S(1)} %get-tuple-element.23.refs_0_, bf16[7,96,256]{2,1,0:T(8,128)(2,1)S(1)} %copy-done.7, ...), custom_call_target="tpu_custom_call" | custom-call | tf_op jit(solution)/shard_map/gains/pallas_call | solution.py:196
  60.6 2.4 %copy-done = bf16[7,1536,256]{2,1,0:T(8,128)(2,1)} copy-done((bf16[7,1536,256]{2,1,0:T(8,128)(2,1)}, bf16[7,1536,256]{2,1,0:T(8,128)(2,1)S(1)}, u32[]{:S(2)}) %copy-start) | copy-done | bytes 5505048
  63.0 2.6 %copy-done.1 = bf16[7,1536,256]{2,1,0:T(8,128)(2,1)S(1)} copy-done((bf16[7,1536,256]{2,1,0:T(8,128)(2,1)S(1)}, bf16[7,1536,256]{2,1,0:T(8,128)(2,1)}, u32[]{:S(2)}) %copy-start.1) | copy-done | bytes 5505048
  65.6 1.1 %copy-done.5 = bf16[784,512]{1,0:T(8,128)(2,1)S(1)} copy-done((bf16[784,512]{1,0:T(8,128)(2,1)S(1)}, bf16[784,512]{1,0:T(8,128)(2,1)}, u32[]{:S(2)}) %copy-start.5) | copy-done | bytes 802840
  66.7 1.4 %first.1 = (bf16[3,96,256]{2,1,0:T(8,128)(2,1)S(1)}, bf16[3,96,256]{2,1,0:T(8,128)(2,1)S(1)}, bf16[3,96,256]{2,1,0:T(8,128)(2,1)S(1)}, bf16[3,96,256]{2,1,0:T(8,...) custom-call(bf16[7,1536,256]{2,1,0:T(8,128)(2,1)S(1)} %copy-done.1, ...), custom_call_target="tpu_custom_call" | custom-call | tf_op jit(solution)/shard_map/first/pallas_call | solution.py:246
  69.3 1.4 %second.1 = (bf16[4,96,256]{2,1,0:T(8,128)(2,1)S(1)}, bf16[4,96,256]{2,1,0:T(8,128)(2,1)S(1)}, bf16[4,96,256]{2,1,0:T(8,128)(2,1)S(1)}, bf16[4,96,256]{2,1,0:T(8,128)(2,1)S(1)}) custom-call(bf16[7,1536,256]{2,1,0:T(8,128)(2,1)S(1)} %copy-done.2, bf16[7,384,256]{2,1,0:T(8,128)(2,1)S(1)} %get-tuple-element.30.refs_1_.anomalies, ...), custom_call_target="tpu_custom_call" | custom-call | tf_op jit(solution)/shard_map/second/pallas_call | solution.py:266
  70.7 1.1 %collective-permute-start.6 = (bf16[4,96,256]{2,1,0:T(8,128)(2,1)S(1)}, bf16[4,96,256]{2,1,0:T(8,128)(2,1)S(1)}, u32[]{:S(2)}, u32[]{:S(2)}) collective-permute-start(bf16[4,96,256]{2,1,0:T(8,128)(2,1)S(1)} %get-tuple-element.36), channel_id=1, source_target_pairs={{0,1},{1,0},{2,3},{3,2},{4,5},{5,4},{6,7},{7,6},{8,9},{9,8},{10,11... | collective-permute-start | bytes 589832 | tf_op jit(solution)/shard_map/ppermute | solution.py:310
  71.7 2.5 %collective-permute-start.7 = (bf16[4,96,256]{2,1,0:T(8,128)(2,1)S(1)}, bf16[4,96,256]{2,1,0:T(8,128)(2,1)S(1)}, u32[]{:S(2)}, u32[]{:S(2)}) collective-permute-start(bf16[4,96,256]{2,1,0:T(8,128)(2,1)S(1)} %get-tuple-element.37), channel_id=1, source_target_pairs={{0,2},{1,3},{2,0},{3,1},{4,6},{5,7},{6,4},{7,5},{8,10},{9,11},{10,... | collective-permute-start | bytes 589832 | tf_op jit(solution)/shard_map/ppermute | solution.py:310
  74.3 1.2 %collective-permute-start.8 = (bf16[4,96,256]{2,1,0:T(8,128)(2,1)S(1)}, bf16[4,96,256]{2,1,0:T(8,128)(2,1)S(1)}, u32[]{:S(2)}, u32[]{:S(2)}) collective-permute-start(bf16[4,96,256]{2,1,0:T(8,128)(2,1)S(1)} %get-tuple-element.38), channel_id=1, source_target_pairs={{0,3},{1,2},{2,1},{3,0},{4,7},{5,6},{6,5},{7,4},{8,11},{9,10},{10,... | collective-permute-start | bytes 589832 | tf_op jit(solution)/shard_map/ppermute | solution.py:310
  75.5 1.3 %collective-permute-start.10 = (bf16[3,96,256]{2,1,0:T(8,128)(2,1)S(1)}, bf16[3,96,256]{2,1,0:T(8,128)(2,1)S(1)}, u32[]{:S(2)}, u32[]{:S(2)}) collective-permute-start(bf16[3,96,256]{2,1,0:T(8,128)(2,1)S(1)} %get-tuple-element.41), channel_id=1, source_target_pairs={{0,2},{1,3},{2,0},{3,1},{4,6},{5,7},{6,4},{7,5},{8,10},{9,11},{10,... | collective-permute-start | bytes 442376 | tf_op jit(solution)/shard_map/ppermute | solution.py:310
  76.7 1.2 %collective-permute-start.11 = (bf16[3,96,256]{2,1,0:T(8,128)(2,1)S(1)}, bf16[3,96,256]{2,1,0:T(8,128)(2,1)S(1)}, u32[]{:S(2)}, u32[]{:S(2)}) collective-permute-start(bf16[3,96,256]{2,1,0:T(8,128)(2,1)S(1)} %get-tuple-element.42), channel_id=1, source_target_pairs={{0,3},{1,2},{2,1},{3,0},{4,7},{5,6},{6,5},{7,4},{8,11},{9,10},{10,... | collective-permute-start | bytes 442376 | tf_op jit(solution)/shard_map/ppermute | solution.py:310
  77.9 8.7 %collective-permute-done.10.refs_2_ = bf16[3,96,256]{2,1,0:T(8,128)(2,1)S(1)} collective-permute-done((bf16[3,96,256]{2,1,0:T(8,128)(2,1)S(1)}, bf16[3,96,256]{2,1,0:T(8,128)(2,1)S(1)}, u32[]{:S(2)}, u32[]{:S(2)}) %collective-permute-start.10) | collective-permute-done | bytes 147488 | tf_op jit(solution)/shard_map/ppermute | solution.py:310
  86.6 4.4 %collective-permute-done.11.refs_3_ = bf16[3,96,256]{2,1,0:T(8,128)(2,1)S(1)} collective-permute-done((bf16[3,96,256]{2,1,0:T(8,128)(2,1)S(1)}, bf16[3,96,256]{2,1,0:T(8,128)(2,1)S(1)}, u32[]{:S(2)}, u32[]{:S(2)}) %collective-permute-start.11) | collective-permute-done | bytes 147488 | tf_op jit(solution)/shard_map/ppermute | solution.py:310
  (40 shorter events, 9.6 us)
Async XLA Ops:
  0.6 10.8 %copy-start.8 = (f32[96,512]{1,0:T(8,128)S(1)}, f32[96,512]{1,0:T(8,128)}, u32[]{:S(2)}) copy-start(f32[96,512]{1,0:T(8,128)} %noise.1) | copy-start | bytes 589828
  2.0 9.4 %copy-start.11 = (f32[512]{0:T(512)S(1)}, f32[512]{0:T(512)}, u32[]{:S(2)}) copy-start(f32[512]{0:T(512)} %param.10) | copy-start | bytes 6148
  5.2 6.2 %collective-permute-start.3 = (bf16[96,512]{1,0:T(8,128)(2,1)S(1)}, bf16[96,512]{1,0:T(8,128)(2,1)S(1)}, u32[]{:S(2)}, u32[]{:S(2)}) collective-permute-start(bf16[96,512]{1,0:T(8,128)(2,1)S(1)} %get-tuple-element.27.mine), channel_id=1, source_target_pairs={{0,4},{4,0},{1,5},{5,1},{2,6},{6,2},{3,7},{7,3},{8,12},{12,8},{9,1... | collective-permute-start | bytes 294920 | tf_op jit(solution)/shard_map/ppermute | solution.py:310
  11.4 15.4 %copy-start.10 = (s32[512]{0:T(512)S(1)}, s32[512]{0:T(512)}, u32[]{:S(2)}) copy-start(s32[512]{0:T(512)} %param.8) | copy-start | bytes 6148
  11.4 15.4 %copy-start.12 = (f32[512]{0:T(512)S(1)}, f32[512]{0:T(512)}, u32[]{:S(2)}) copy-start(f32[512]{0:T(512)} %param.9) | copy-start | bytes 6148
  27.8 25.1 %collective-permute-start.5 = (bf16[784,512]{1,0:T(8,128)(2,1)S(1)}, bf16[784,512]{1,0:T(8,128)(2,1)S(1)}, u32[]{:S(2)}, u32[]{:S(2)}) collective-permute-start(bf16[784,512]{1,0:T(8,128)(2,1)S(1)} %get-tuple-element.28.refs_4_), channel_id=1, source_target_pairs={{8,16},{24,32},{40,48},{56,64},{72,80},{88,96},{104,112},{16,8},{3... | collective-permute-start | bytes 2408456 | tf_op jit(solution)/shard_map/ppermute | solution.py:340
  28.5 24.3 %collective-permute-start.4 = (bf16[784,512]{1,0:T(8,128)(2,1)S(1)}, bf16[784,512]{1,0:T(8,128)(2,1)S(1)}, u32[]{:S(2)}, u32[]{:S(2)}) collective-permute-start(bf16[784,512]{1,0:T(8,128)(2,1)S(1)} %get-tuple-element.28.refs_4_), channel_id=1, source_target_pairs={{0,8},{8,0},{16,24},{24,16},{32,40},{40,32},{48,56},{56,48},{64,72... | collective-permute-start | bytes 2408456 | tf_op jit(solution)/shard_map/ppermute | solution.py:310
  31.8 11.1 %collective-permute-start = (bf16[7,96,256]{2,1,0:T(8,128)(2,1)}, bf16[7,96,256]{2,1,0:T(8,128)(2,1)S(1)}, u32[]{:S(2)}, u32[]{:S(2)}) collective-permute-start(bf16[7,96,256]{2,1,0:T(8,128)(2,1)} %get-tuple-element.24), channel_id=1, source_target_pairs={{0,1},{1,0},{2,3},{3,2},{4,5},{5,4},{6,7},{7,6},{8,9},{9,8},{10,11... | collective-permute-start | bytes 1032200 | tf_op jit(solution)/shard_map/ppermute | solution.py:310
  32.4 17.9 %collective-permute-start.1 = (bf16[7,96,256]{2,1,0:T(8,128)(2,1)}, bf16[7,96,256]{2,1,0:T(8,128)(2,1)}, u32[]{:S(2)}, u32[]{:S(2)}) collective-permute-start(bf16[7,96,256]{2,1,0:T(8,128)(2,1)} %get-tuple-element.25), channel_id=1, source_target_pairs={{0,2},{1,3},{2,0},{3,1},{4,6},{5,7},{6,4},{7,5},{8,10},{9,11},{10,... | collective-permute-start | bytes 1032200 | tf_op jit(solution)/shard_map/ppermute | solution.py:310
  34.5 18.4 %collective-permute-start.2 = (bf16[7,96,256]{2,1,0:T(8,128)(2,1)}, bf16[7,96,256]{2,1,0:T(8,128)(2,1)}, u32[]{:S(2)}, u32[]{:S(2)}) collective-permute-start(bf16[7,96,256]{2,1,0:T(8,128)(2,1)} %get-tuple-element.26), channel_id=1, source_target_pairs={{0,3},{1,2},{2,1},{3,0},{4,7},{5,6},{6,5},{7,4},{8,11},{9,10},{10,... | collective-permute-start | bytes 1032200 | tf_op jit(solution)/shard_map/ppermute | solution.py:310
  36.5 26.5 %all-to-all-start.1 = ((f32[16,1,128]{2,1,0:T(1,128)}), f32[16,1,128]{2,1,0:T(1,128)S(1)}, u32[]{:S(2)}, u32[]{:S(2)}) async-start(f32[16,1,128]{2,1,0:T(1,128)} %bitcast.8), calls=%async_computation.1 | async-start | bytes 16384 | tf_op jit(solution)/shard_map/all_to_all | solution.py:314
  52.9 0.9 copy-start.3
  53.7 1.1 %copy-start.4 = (bf16[784,512]{1,0:T(8,128)(2,1)S(1)}, bf16[784,512]{1,0:T(8,128)(2,1)}, u32[]{:S(2)}) copy-start(bf16[784,512]{1,0:T(8,128)(2,1)} %copy-done.3) | copy-start | bytes 2408452
  54.9 1.0 %copy-start.7 = (bf16[7,96,256]{2,1,0:T(8,128)(2,1)S(1)}, bf16[7,96,256]{2,1,0:T(8,128)(2,1)}, u32[]{:S(2)}) copy-start(bf16[7,96,256]{2,1,0:T(8,128)(2,1)} %copy-done.6) | copy-start | bytes 1032196
  60.6 2.4 %copy-start = (bf16[7,1536,256]{2,1,0:T(8,128)(2,1)}, bf16[7,1536,256]{2,1,0:T(8,128)(2,1)S(1)}, u32[]{:S(2)}) copy-start(bf16[7,1536,256]{2,1,0:T(8,128)(2,1)S(1)} %get-tuple-element.29.refs_0_.gain) | copy-start | bytes 16515076
  63.0 2.6 %copy-start.1 = (bf16[7,1536,256]{2,1,0:T(8,128)(2,1)S(1)}, bf16[7,1536,256]{2,1,0:T(8,128)(2,1)}, u32[]{:S(2)}) copy-start(bf16[7,1536,256]{2,1,0:T(8,128)(2,1)} %copy-done) | copy-start | bytes 16515076
  65.6 1.1 %copy-start.5 = (bf16[784,512]{1,0:T(8,128)(2,1)S(1)}, bf16[784,512]{1,0:T(8,128)(2,1)}, u32[]{:S(2)}) copy-start(bf16[784,512]{1,0:T(8,128)(2,1)} %copy-done.3) | copy-start | bytes 2408452
  66.7 2.6 %copy-start.2 = (bf16[7,1536,256]{2,1,0:T(8,128)(2,1)S(1)}, bf16[7,1536,256]{2,1,0:T(8,128)(2,1)}, u32[]{:S(2)}) copy-start(bf16[7,1536,256]{2,1,0:T(8,128)(2,1)} %copy-done) | copy-start | bytes 16515076
  68.2 8.6 %collective-permute-start.9 = (bf16[3,96,256]{2,1,0:T(8,128)(2,1)S(1)}, bf16[3,96,256]{2,1,0:T(8,128)(2,1)S(1)}, u32[]{:S(2)}, u32[]{:S(2)}) collective-permute-start(bf16[3,96,256]{2,1,0:T(8,128)(2,1)S(1)} %get-tuple-element.40), channel_id=1, source_target_pairs={{0,1},{1,0},{2,3},{3,2},{4,5},{5,4},{6,7},{7,6},{8,9},{9,8},{10,11... | collective-permute-start | bytes 442376 | tf_op jit(solution)/shard_map/ppermute | solution.py:310
  70.7 21.1 %collective-permute-start.6 = (bf16[4,96,256]{2,1,0:T(8,128)(2,1)S(1)}, bf16[4,96,256]{2,1,0:T(8,128)(2,1)S(1)}, u32[]{:S(2)}, u32[]{:S(2)}) collective-permute-start(bf16[4,96,256]{2,1,0:T(8,128)(2,1)S(1)} %get-tuple-element.36), channel_id=1, source_target_pairs={{0,1},{1,0},{2,3},{3,2},{4,5},{5,4},{6,7},{7,6},{8,9},{9,8},{10,11... | collective-permute-start | bytes 589832 | tf_op jit(solution)/shard_map/ppermute | solution.py:310
  71.7 20.1 %collective-permute-start.7 = (bf16[4,96,256]{2,1,0:T(8,128)(2,1)S(1)}, bf16[4,96,256]{2,1,0:T(8,128)(2,1)S(1)}, u32[]{:S(2)}, u32[]{:S(2)}) collective-permute-start(bf16[4,96,256]{2,1,0:T(8,128)(2,1)S(1)} %get-tuple-element.37), channel_id=1, source_target_pairs={{0,2},{1,3},{2,0},{3,1},{4,6},{5,7},{6,4},{7,5},{8,10},{9,11},{10,... | collective-permute-start | bytes 589832 | tf_op jit(solution)/shard_map/ppermute | solution.py:310
  74.3 17.5 %collective-permute-start.8 = (bf16[4,96,256]{2,1,0:T(8,128)(2,1)S(1)}, bf16[4,96,256]{2,1,0:T(8,128)(2,1)S(1)}, u32[]{:S(2)}, u32[]{:S(2)}) collective-permute-start(bf16[4,96,256]{2,1,0:T(8,128)(2,1)S(1)} %get-tuple-element.38), channel_id=1, source_target_pairs={{0,3},{1,2},{2,1},{3,0},{4,7},{5,6},{6,5},{7,4},{8,11},{9,10},{10,... | collective-permute-start | bytes 589832 | tf_op jit(solution)/shard_map/ppermute | solution.py:310
  75.5 11.1 %collective-permute-start.10 = (bf16[3,96,256]{2,1,0:T(8,128)(2,1)S(1)}, bf16[3,96,256]{2,1,0:T(8,128)(2,1)S(1)}, u32[]{:S(2)}, u32[]{:S(2)}) collective-permute-start(bf16[3,96,256]{2,1,0:T(8,128)(2,1)S(1)} %get-tuple-element.41), channel_id=1, source_target_pairs={{0,2},{1,3},{2,0},{3,1},{4,6},{5,7},{6,4},{7,5},{8,10},{9,11},{10,... | collective-permute-start | bytes 442376 | tf_op jit(solution)/shard_map/ppermute | solution.py:310
  76.7 14.2 %collective-permute-start.11 = (bf16[3,96,256]{2,1,0:T(8,128)(2,1)S(1)}, bf16[3,96,256]{2,1,0:T(8,128)(2,1)S(1)}, u32[]{:S(2)}, u32[]{:S(2)}) collective-permute-start(bf16[3,96,256]{2,1,0:T(8,128)(2,1)S(1)} %get-tuple-element.42), channel_id=1, source_target_pairs={{0,3},{1,2},{2,1},{3,0},{4,7},{5,6},{6,5},{7,4},{8,11},{9,10},{10,... | collective-permute-start | bytes 442376 | tf_op jit(solution)/shard_map/ppermute | solution.py:310
  (3 other events, 2.1 us)

commit v3 on v2

v3 whole, which is shorter than its diff:
```python
import functools

import jax
import jax.numpy as jnp
from jax import lax
from jax.experimental import pallas as pl
from jax.experimental.pallas import tpu as pltpu
from jax.sharding import PartitionSpec as P


RADIUS = 1024
F32 = jnp.float32
BF16 = jnp.bfloat16


def params(megabytes=12):
    return pltpu.CompilerParams(vmem_limit_bytes=megabytes * 2**20)


def whole():
    return pl.BlockSpec(memory_space=pltpu.VMEM)


def scalars():
    return pl.BlockSpec(memory_space=pltpu.SMEM)


def anywhere():
    return pl.BlockSpec(memory_space=pl.ANY)


def shape_of(shape, dtype=BF16):
    return pltpu.VMEM(shape, dtype)


def in_vmem(values):
    return [pltpu.with_memory_space_constraint(v, pltpu.VMEM) for v in values]


def split_rows(value):
    first = value.astype(BF16)
    rest = value - first.astype(F32)
    second = rest.astype(BF16)
    third = (rest - second.astype(F32)).astype(BF16)
    return [first, second, third]


def tile_block(me, s, width):
    return pl.multiple_of(jnp.bitwise_xor(me, s) * width, width)


def pack_body(me, weights, ensemble, tiles, *rest):
    *blocks, predicted, arrived = rest
    peers = len(blocks)
    var_count, _, width = blocks[0].shape
    starts = [tile_block(me[0], s, width) for s in range(peers)]
    loads = [
        pltpu.make_async_copy(
            ensemble.at[:, :, pl.ds(starts[s], width)], blocks[s], arrived.at[s]
        )
        for s in range(peers)
    ]
    for load in loads:
        load.start()
    rows = lax.broadcasted_iota(jnp.int32, (width, tiles.shape[1]), 0)
    total = jnp.zeros(predicted.shape, F32)
    for s in range(peers):
        chosen = jnp.where(tiles[...] - starts[s] == rows, 1.0, 0.0).astype(BF16)
        loads[s].wait()
        mixed = weights[0] * blocks[s][0].astype(F32)
        for l in range(1, var_count):
            mixed = mixed + weights[l] * blocks[s][l].astype(F32)
        high = mixed.astype(BF16)
        low = (mixed - high.astype(F32)).astype(BF16)
        total = total + jnp.dot(high, chosen, preferred_element_type=F32)
        total = total + jnp.dot(low, chosen, preferred_element_type=F32)
    predicted[...] = total.astype(BF16)


def pack(me, ensemble, weights, tiles, peers):
    var_count, own, tile_count = ensemble.shape
    width = tile_count // peers
    obs = tiles.shape[1]
    return pl.pallas_call(
        pack_body,
        in_specs=[scalars(), scalars(), anywhere(), whole()],
        out_specs=[whole()] * (peers + 1),
        out_shape=[shape_of((var_count, own, width))] * peers + [shape_of((own, obs))],
        scratch_shapes=[pltpu.SemaphoreType.DMA((peers,))],
        compiler_params=params(),
        name="pack",
    )(me, weights, pltpu.with_memory_space_constraint(ensemble, pltpu.HBM), tiles)


def scale_body(noise, error, out):
    out[...] = (jnp.sqrt(error[...]) * noise[...]).astype(BF16)


def scale(noise, error):
    return pl.pallas_call(
        scale_body,
        in_specs=[whole()] * 2,
        out_specs=whole(),
        out_shape=shape_of(noise.shape),
        compiler_params=params(),
        name="scale",
    )(noise, error)


def join_body(mine, other, out):
    predicted = (mine[...].astype(F32) + other[...].astype(F32)).astype(BF16)
    for j in range(out.shape[0]):
        out[j] = predicted


def join(mine, other, peers):
    return pl.pallas_call(
        join_body,
        in_specs=[whole()] * 2,
        out_specs=whole(),
        out_shape=shape_of((peers, *mine.shape)),
        compiler_params=params(),
        name="join",
    )(mine, other)


def stats_body(me, gathered, values, error, tiles, *refs):
    peers, own, obs = gathered.shape
    noises, (packet, sums) = refs[:peers], refs[peers:]
    members = peers * own
    total = jnp.zeros((1, obs), F32)
    for j in range(peers):
        total = total + jnp.sum(gathered[j].astype(F32), axis=0, keepdims=True)
    mean = total / members
    square = jnp.zeros((1, obs), F32)
    for j in range(peers):
        dev = gathered[j].astype(F32) - mean
        square = square + jnp.sum(dev * dev, axis=0, keepdims=True)
    for s in range(peers):
        dev = gathered[jnp.bitwise_xor(me[0], s)].astype(F32) - mean
        packet[s * own : (s + 1) * own] = dev.astype(BF16)
        packet[members + s * own : members + (s + 1) * own] = noises[s][...]
    spread = square / (members - 1)
    innovation = values[...] - mean
    place = tiles[...]
    rows = split_rows(innovation) + split_rows(error[...]) + split_rows(spread)
    rows += [(place // 32).astype(F32).astype(BF16), (place % 32).astype(F32).astype(BF16)]
    rows += [jnp.zeros((1, obs), BF16)] * (16 - len(rows))
    packet[2 * members :] = jnp.concatenate(rows, axis=0)
    above = jnp.sum(innovation * innovation)
    below = jnp.sum(spread + error[...])
    lane = lax.broadcasted_iota(jnp.int32, sums.shape, 1)
    sums[...] = jnp.where(lane == 0, above, jnp.where(lane == 1, below, 0.0))


def stats(me, gathered, values, error, tiles, noises, regions):
    peers, own, obs = gathered.shape
    return pl.pallas_call(
        stats_body,
        in_specs=[scalars()] + [whole()] * (4 + peers),
        out_specs=[whole(), whole()],
        out_shape=[shape_of((2 * peers * own + 16, obs)), shape_of((regions, 128), F32)],
        compiler_params=params(),
        name="stats",
    )(me, gathered, values, error, tiles, *noises)


def scalar_rows(packet, members):
    rows = packet[2 * members :].astype(F32)
    innovation = rows[0:1] + rows[1:2] + rows[2:3]
    error = rows[3:4] + rows[4:5] + rows[5:6]
    spread = rows[6:7] + rows[7:8] + rows[8:9]
    return innovation, error, spread, rows[9:10] * 32.0 + rows[10:11]


def update(state, anom_t, perturbed, taper, root, anomalies, gain, blocks, at):
    own = blocks[0].shape[1]
    members = own * len(blocks)
    parts = [part.astype(F32) for part in state]
    mean = sum(jnp.sum(part, axis=0, keepdims=True) for part in parts) / members
    for s, part in enumerate(parts):
        anomalies[s * own : (s + 1) * own] = (part - mean).astype(BF16)
    obs = taper.shape[0]
    step = obs // 3
    for k in range(0, obs, step):
        covariance = jnp.dot(anom_t[k : k + step], anomalies[...], preferred_element_type=F32)
        gain[k : k + step] = (covariance * taper[k : k + step]).astype(BF16)
    increment = jnp.dot(perturbed[...], gain[...], preferred_element_type=F32)
    result = mean + root * anomalies[...].astype(F32) + increment
    for s, block in enumerate(blocks):
        block[at] = result[s * own : (s + 1) * own].astype(BF16)


def first_body(offset, *refs, tile_count, peers):
    far_states, far_packets, sums = refs[:peers], refs[peers : peers + 3], refs[peers + 3]
    refs = refs[peers + 4 :]
    blocks, (anom_t, perturbed, taper, root_out, inflation_out) = refs[:peers], refs[peers : peers + 5]
    states, packets, anomalies, gain, arrived = refs[peers + 5 :]
    count, own, width = blocks[0].shape
    members = peers * own
    obs = far_packets[0].shape[1]
    loads = [
        pltpu.make_async_copy(far_packets[n], packets.at[n], arrived.at[n]) for n in range(3)
    ]
    loads += [
        pltpu.make_async_copy(far_states[s].at[:count], states.at[s], arrived.at[3 + s])
        for s in range(peers)
    ]
    for load in loads:
        load.start()
    folded = jnp.sum(sums[...], axis=0, keepdims=True)
    inflation = folded[:, 0:1] / folded[:, 1:2]
    inflation_out[0] = jnp.sum(inflation)
    root = jnp.sqrt(inflation)
    root_out[...] = jnp.broadcast_to(root, root_out.shape)
    tile = (offset[0] + lax.broadcasted_iota(jnp.int32, (1, width), 1)).astype(F32)
    for n in range(3):
        loads[n].wait()
        packet = packets.at[n]
        dev = packet[:members]
        anom_t[n * obs : (n + 1) * obs] = dev.T
        innovation, error, spread, place = scalar_rows(packet, members)
        place = place + (offset[1 + n] * tile_count).astype(F32)
        bottom = jnp.where(error > 0.0, inflation * spread + error, 1.0)
        factor = jnp.where(error > 0.0, inflation / bottom, 0.0) / (members - 1)
        column = jnp.concatenate([place, factor, jnp.zeros((6, obs), F32)], axis=0).T
        near = jnp.maximum(0.0, 1.0 - jnp.abs(tile - column[:, 0:1]) / RADIUS)
        taper[n * obs : (n + 1) * obs] = near * near * column[:, 1:2]
        scaled = packet[members : 2 * members].astype(F32)
        perturbed[:, n * obs : (n + 1) * obs] = (
            innovation + scaled - root * dev.astype(F32)
        ).astype(BF16)
    for load in loads[3:]:
        load.wait()
    for l in range(count):
        update(
            [states[s, l] for s in range(peers)],
            anom_t, perturbed, taper, root, anomalies.at[l], gain.at[l], blocks, l,
        )


def first_updates(offset, states, packets, sums, count, tile_count):
    _, own, width = states[0].shape
    peers = len(states)
    members = own * peers
    rows, obs = packets[0].shape
    out = pl.pallas_call(
        functools.partial(first_body, tile_count=tile_count, peers=peers),
        in_specs=[scalars()] + [anywhere()] * (peers + 3) + [whole()],
        out_specs=[whole()] * (peers + 4) + [scalars()],
        out_shape=[shape_of((count, own, width))] * peers
        + [
            shape_of((3 * obs, members)),
            shape_of((members, 3 * obs)),
            shape_of((3 * obs, width), F32),
            shape_of((8, 128), F32),
            jax.ShapeDtypeStruct((1,), F32),
        ],
        scratch_shapes=[
            pltpu.VMEM((peers, count, own, width), BF16),
            pltpu.VMEM((3, rows, obs), BF16),
            pltpu.VMEM((count, members, width), BF16),
            pltpu.VMEM((count, 3 * obs, width), BF16),
            pltpu.SemaphoreType.DMA((3 + peers,)),
        ],
        compiler_params=params(16),
        name="first",
    )(offset, *states, *packets, sums)
    return out[:peers], out[peers : peers + 4], out[peers + 4]


def second_body(*refs, first, peers):
    far_states, (anom_t, perturbed, taper, root) = refs[:peers], refs[peers : peers + 4]
    blocks = refs[peers + 4 : 2 * peers + 4]
    states, anomalies, gain, arrived = refs[2 * peers + 4 :]
    count = blocks[0].shape[0]
    loads = [
        pltpu.make_async_copy(far_states[s].at[first:], states.at[s], arrived.at[s])
        for s in range(peers)
    ]
    for load in loads:
        load.start()
    for load in loads:
        load.wait()
    for l in range(count):
        update(
            [states[s, l] for s in range(peers)],
            anom_t, perturbed, taper, root[0:1, 0:1], anomalies.at[l], gain.at[l], blocks, l,
        )


def second_updates(states, shared, first):
    var_count, own, width = states[0].shape
    peers = len(states)
    members = own * peers
    count = var_count - first
    obs = shared[0].shape[0]
    return pl.pallas_call(
        functools.partial(second_body, first=first, peers=peers),
        in_specs=[anywhere()] * peers + [whole()] * 4,
        out_specs=[whole()] * peers,
        out_shape=[shape_of((count, own, width))] * peers,
        scratch_shapes=[
            pltpu.VMEM((peers, count, own, width), BF16),
            pltpu.VMEM((count, members, width), BF16),
            pltpu.VMEM((count, obs, width), BF16),
            pltpu.SemaphoreType.DMA((peers,)),
        ],
        compiler_params=params(),
        name="second",
    )(*states, *in_vmem(shared))


def place_body(me, *refs, first, peers):
    blocks, out, done = refs[:peers], refs[-2], refs[-1]
    count, _, width = blocks[0].shape
    copies = [
        pltpu.make_async_copy(
            blocks[s],
            out.at[first : first + count, :, pl.ds(tile_block(me[0], s, width), width)],
            done.at[s],
        )
        for s in range(peers)
    ]
    for copy in copies:
        copy.start()
    for copy in copies:
        copy.wait()


def place(me, blocks, first, var_count, before=None):
    peers = len(blocks)
    _, own, width = blocks[0].shape
    more = [] if before is None else [before]
    return pl.pallas_call(
        functools.partial(place_body, first=first, peers=peers),
        in_specs=[scalars()] + [anywhere()] * (peers + len(more)),
        out_specs=anywhere(),
        out_shape=pltpu.HBM((var_count, own, peers * width), BF16),
        scratch_shapes=[pltpu.SemaphoreType.DMA((peers,))],
        input_output_aliases={1 + peers: 0} if more else {},
        compiler_params=params(),
    )(me, *in_vmem(blocks), *more)


def swapped(value, axis, distance):
    pairs = [(i, i ^ distance) for i in range(lax.axis_size(axis))]
    return lax.ppermute(value, axis, pairs)


def exchanged(blocks, axis):
    return lax.all_to_all(blocks, axis, split_axis=0, concat_axis=0, tiled=True)


def traded(blocks, order):
    out = list(blocks)
    for s in order:
        out[s] = swapped(blocks[s], "member", s)
    return out


def shards(ensemble, obs_weights, obs_tiles, obs_values, obs_error, obs_noise):
    peers = lax.axis_size("member")
    regions = lax.axis_size("region")
    var_count, _, tile_count = ensemble.shape
    width = tile_count // peers
    me = lax.axis_index("member").astype(jnp.int32)[None]
    region = lax.axis_index("region").astype(jnp.int32)
    tiles, values, error = (a[None, :] for a in (obs_tiles, obs_values, obs_error))
    *blocks, partial = pack(me, ensemble, obs_weights, tiles, peers)
    other = swapped(partial, "depth", 1)
    noises = traded([scale(obs_noise, error)] * peers, (1, 3, 2))
    states = traded(blocks, (1, 3, 2))
    joined = join(partial, other, peers)
    gathered = exchanged(joined, "member")
    packet, sums = stats(me, gathered, values, error, tiles, noises, regions)
    near = swapped(packet, "region", 1)
    pairs = [(i, i + 1) for i in range(1, regions - 1, 2)]
    far = lax.ppermute(packet, "region", pairs + [(j, i) for i, j in pairs])
    all_sums = exchanged(sums, "region")
    side = 1 - 2 * (region % 2)
    offset = jnp.stack([me[0] * width, jnp.zeros_like(side), side, -side])
    half = var_count // 2
    ready, shared, inflation = first_updates(
        offset, states, (packet, near, far), all_sums, half, tile_count
    )
    early = traded(ready, (1, 3, 2))
    ready = second_updates(states, shared, half)
    late = traded(ready, (1, 3, 2))
    output = place(me, early, 0, var_count)
    output = place(me, late, half, var_count, output)
    return (output, inflation.reshape(()))


def solution(mesh):
    return jax.shard_map(
        shards,
        mesh=mesh,
        in_specs=(
            P("depth", "member", "region"),
            P("depth"),
            P("region"),
            P("region"),
            P("region"),
            P("member", "region"),
        ),
        out_specs=(P("depth", "member", "region"), P()),
        check_vma=False,
    )
```

time: 93.2 us -> 86.1 us (0.924)
  the two profiles are of different devices: /device:TPU:0 before, /device:TPU:24 now
where the time goes in v3:
time: 86.1 us; the launch traced here: 85.8 us
  waiting for transfers between devices  33.5 us (39%)
  starting transfers between devices  33.2 us (39%)
  Pallas kernels  16.9 us (20%)
  local copies, waits for them, and re-layouts  1.34 us (2%)
    ppermute x14, waiting for transfers between devices, swapped(): return lax.ppermute(value, axis, pairs)  33.5 us
    ppermute x14, starting transfers between devices, swapped(): return lax.ppermute(value, axis, pairs)  20.2 us
    all_to_all x2, starting transfers between devices, exchanged(): return lax.all_to_all(blocks, axis, split_axis=0, concat_axis=0, tiled=True)  10.6 us
    pallas_call x1, Pallas kernels, first_updates(): pl.pallas_call(functools.partial(first_body, tile_count=tile_count, peers...  5.85 us
    pallas_call x1, Pallas kernels, second_updates(): pl.pallas_call(functools.partial(second_body, first=first, peers=peers),...  4.43 us
    pallas_call x1, Pallas kernels, pack(): pl.pallas_call(pack_body, in_specs=[scalars(), scalars(), anywhere(), who...  3.09 us
    ppermute x1, starting transfers between devices, shards(): far = lax.ppermute(packet, 'region', pairs + [(j, i) for i, j in pairs])  2.37 us
    pallas_call x2, Pallas kernels, place(): pl.pallas_call(functools.partial(place_body, first=first, peers=peers), i...  1.75 us
  transfers between devices with their start and end apart: 17, of which 6 were waited for; matrix products, arithmetic and copies ran while one was open for 0% of the time, Pallas kernels for 6%

profile of v3, /device:TPU:24, one launch (start us, length us, event | category | flops | bytes accessed | tf_op | source)
XLA Modules:
  0.0 85.8 jit_solution(14773247919762246329)
XLA Ops:
  2.0 3.1 %pack.1 = (bf16[7,96,256]{2,1,0:T(8,128)(2,1)S(1)}, bf16[7,96,256]{2,1,0:T(8,128)(2,1)}, bf16[7,96,256]{2,1,0:T(8,128)(2,1)}, bf16[7,96,256]{2,1,0:T(8,128)(2,1)S(1)}, bf16[96,512]{1,0:T(8,128)(2,1)S(1)}) custom-call(s32[1]{0:T(128)} %bitcast.me, f32[7]{0:T(128)S(1)} %copy-done.5, bf16[7,96,1024]{2,1,0:T(8,128)(2,1)} %ensemble.1, s32[1,512]{1,0:T(1,128)S(1)} %bitcast.13), custom_call_target="tpu_custom_call" | custom-call | tf_op jit(solution)/shard_map/pack/pallas_call | solution.py:84
  5.1 1.3 %collective-permute-start.3 = (bf16[96,512]{1,0:T(8,128)(2,1)S(1)}, bf16[96,512]{1,0:T(8,128)(2,1)S(1)}, u32[]{:S(2)}, u32[]{:S(2)}) collective-permute-start(bf16[96,512]{1,0:T(8,128)(2,1)S(1)} %get-tuple-element.26.mine), channel_id=1, source_target_pairs={{0,4},{4,0},{1,5},{5,1},{2,6},{6,2},{3,7},{7,3},{8,12},{12,8},{9,1... | collective-permute-start | bytes 294920 | tf_op jit(solution)/shard_map/ppermute | solution.py:348
  6.4 4.9 %collective-permute-done.3.other = bf16[96,512]{1,0:T(8,128)(2,1)S(1)} collective-permute-done((bf16[96,512]{1,0:T(8,128)(2,1)S(1)}, bf16[96,512]{1,0:T(8,128)(2,1)S(1)}, u32[]{:S(2)}, u32[]{:S(2)}) %collective-permute-start.3) | collective-permute-done | bytes 98336 | tf_op jit(solution)/shard_map/ppermute | solution.py:348
  12.1 4.3 %all-to-all-start = ((bf16[4,96,512]{2,1,0:T(8,128)(2,1)}), bf16[4,96,512]{2,1,0:T(8,128)(2,1)S(1)}, u32[]{:S(2)}, u32[]{:S(2)}) async-start(bf16[4,96,512]{2,1,0:T(8,128)(2,1)} %join.1), calls=%async_computation | async-start | bytes 786432 | tf_op jit(solution)/shard_map/all_to_all | solution.py:352
  16.4 3.3 %collective-permute-start.6 = (bf16[96,512]{1,0:T(8,128)(2,1)S(1)}, bf16[96,512]{1,0:T(8,128)(2,1)S(1)}, u32[]{:S(2)}, u32[]{:S(2)}) collective-permute-start(bf16[96,512]{1,0:T(8,128)(2,1)S(1)} %scale.1.refs_0_), channel_id=1, source_target_pairs={{0,3},{1,2},{2,1},{3,0},{4,7},{5,6},{6,5},{7,4},{8,11},{9,10},{10,... | collective-permute-start | bytes 294920 | tf_op jit(solution)/shard_map/ppermute | solution.py:348
  19.7 0.9 collective-permute-start.5
  20.7 6.5 %collective-permute-done.6.refs_3_ = bf16[96,512]{1,0:T(8,128)(2,1)S(1)} collective-permute-done((bf16[96,512]{1,0:T(8,128)(2,1)S(1)}, bf16[96,512]{1,0:T(8,128)(2,1)S(1)}, u32[]{:S(2)}, u32[]{:S(2)}) %collective-permute-start.6) | collective-permute-done | bytes 98336 | tf_op jit(solution)/shard_map/ppermute | solution.py:348
  27.2 1.0 %stats.1 = (bf16[784,512]{1,0:T(8,128)(2,1)S(1)}, f32[16,128]{1,0:T(8,128)}) custom-call(s32[1]{0:T(128)} %bitcast.me, bf16[4,96,512]{2,1,0:T(8,128)(2,1)S(1)} %all-to-all-done.gathered, f32[1,512]{1,0:T(1,128)S(1)} %bitcast.17, f32[1,512]{1,0:T(1,128)S(1)} %bitcast.16, s32[1,512]{1,0:T(1,128)S(1)} %bitcast.14, bf16[96,512]{1,0:T(8,128)(2,1)S(1)} %scale.1.refs_0_, ...), custom_call_target="tpu_custom_call" | custom-call | tf_op jit(solution)/shard_map/stats/pallas_call | solution.py:158
  28.2 2.4 %collective-permute-start.8 = (bf16[784,512]{1,0:T(8,128)(2,1)S(1)}, bf16[784,512]{1,0:T(8,128)(2,1)S(1)}, u32[]{:S(2)}, u32[]{:S(2)}) collective-permute-start(bf16[784,512]{1,0:T(8,128)(2,1)S(1)} %get-tuple-element.27.refs_4_), channel_id=1, source_target_pairs={{8,16},{24,32},{40,48},{56,64},{72,80},{88,96},{104,112},{16,8},{3... | collective-permute-start | bytes 2408456 | tf_op jit(solution)/shard_map/ppermute | solution.py:379
  30.6 1.6 %collective-permute-start.7 = (bf16[784,512]{1,0:T(8,128)(2,1)S(1)}, bf16[784,512]{1,0:T(8,128)(2,1)}, u32[]{:S(2)}, u32[]{:S(2)}) collective-permute-start(bf16[784,512]{1,0:T(8,128)(2,1)S(1)} %get-tuple-element.27.refs_4_), channel_id=1, source_target_pairs={{0,8},{8,0},{16,24},{24,16},{32,40},{40,32},{48,56},{56,48},{64,72... | collective-permute-start | bytes 2408456 | tf_op jit(solution)/shard_map/ppermute | solution.py:348
  32.5 3.6 %collective-permute-start.1 = (bf16[7,96,256]{2,1,0:T(8,128)(2,1)}, bf16[7,96,256]{2,1,0:T(8,128)(2,1)S(1)}, u32[]{:S(2)}, u32[]{:S(2)}) collective-permute-start(bf16[7,96,256]{2,1,0:T(8,128)(2,1)} %get-tuple-element.24), channel_id=1, source_target_pairs={{0,2},{1,3},{2,0},{3,1},{4,6},{5,7},{6,4},{7,5},{8,10},{9,11},{10,... | collective-permute-start | bytes 1032200 | tf_op jit(solution)/shard_map/ppermute | solution.py:348
  36.1 0.8 collective-permute-start.2
  36.9 6.3 %all-to-all-start.1 = ((f32[16,1,128]{2,1,0:T(1,128)}), f32[16,1,128]{2,1,0:T(1,128)S(1)}, u32[]{:S(2)}, u32[]{:S(2)}) async-start(f32[16,1,128]{2,1,0:T(1,128)} %bitcast.8), calls=%async_computation.1 | async-start | bytes 16384 | tf_op jit(solution)/shard_map/all_to_all | solution.py:352
  43.4 8.8 %collective-permute-done.1.refs_2_ = bf16[7,96,256]{2,1,0:T(8,128)(2,1)S(1)} collective-permute-done((bf16[7,96,256]{2,1,0:T(8,128)(2,1)}, bf16[7,96,256]{2,1,0:T(8,128)(2,1)S(1)}, u32[]{:S(2)}, u32[]{:S(2)}) %collective-permute-start.1) | collective-permute-done | bytes 344096 | tf_op jit(solution)/shard_map/ppermute | solution.py:348
  52.2 2.4 %collective-permute-done.2.refs_3_ = bf16[7,96,256]{2,1,0:T(8,128)(2,1)S(1)} collective-permute-done((bf16[7,96,256]{2,1,0:T(8,128)(2,1)S(1)}, bf16[7,96,256]{2,1,0:T(8,128)(2,1)S(1)}, u32[]{:S(2)}, u32[]{:S(2)}) %collective-permute-start.2) | collective-permute-done | bytes 344096 | tf_op jit(solution)/shard_map/ppermute | solution.py:348
  54.6 5.8 %first.1 = (bf16[3,96,256]{2,1,0:T(8,128)(2,1)S(1)}, bf16[3,96,256]{2,1,0:T(8,128)(2,1)S(1)}, bf16[3,96,256]{2,1,0:T(8,128)(2,1)S(1)}, bf16[3,96,256]{2,1,0:T(8,...) custom-call(s32[4]{0:T(128)S(1)} %pad_add_fusion.offset, ...), custom_call_target="tpu_custom_call" | custom-call | tf_op jit(solution)/shard_map/first/pallas_call | solution.py:247
  60.5 4.4 %second.1 = (bf16[4,96,256]{2,1,0:T(8,128)(2,1)S(1)}, bf16[4,96,256]{2,1,0:T(8,128)(2,1)S(1)}, bf16[4,96,256]{2,1,0:T(8,128)(2,1)S(1)}, bf16[4,96,256]{2,1,0:T(8,128)(2,1)S(1)}) custom-call(bf16[7,96,256]{2,1,0:T(8,128)(2,1)S(1)} %get-tuple-element.22.refs_0_, bf16[7,96,256]{2,1,0:T(8,128)(2,1)S(1)} %collective-permute-done.refs_1_, ...), custom_call_target="tpu_custom_call" | custom-call | tf_op jit(solution)/shard_map/second/pallas_call | solution.py:298
  64.9 2.1 %collective-permute-start.9 = (bf16[4,96,256]{2,1,0:T(8,128)(2,1)S(1)}, bf16[4,96,256]{2,1,0:T(8,128)(2,1)S(1)}, u32[]{:S(2)}, u32[]{:S(2)}) collective-permute-start(bf16[4,96,256]{2,1,0:T(8,128)(2,1)S(1)} %get-tuple-element.34), channel_id=1, source_target_pairs={{0,1},{1,0},{2,3},{3,2},{4,5},{5,4},{6,7},{7,6},{8,9},{9,8},{10,11... | collective-permute-start | bytes 589832 | tf_op jit(solution)/shard_map/ppermute | solution.py:348
  67.0 2.8 %collective-permute-start.11 = (bf16[4,96,256]{2,1,0:T(8,128)(2,1)S(1)}, bf16[4,96,256]{2,1,0:T(8,128)(2,1)S(1)}, u32[]{:S(2)}, u32[]{:S(2)}) collective-permute-start(bf16[4,96,256]{2,1,0:T(8,128)(2,1)S(1)} %get-tuple-element.36), channel_id=1, source_target_pairs={{0,3},{1,2},{2,1},{3,0},{4,7},{5,6},{6,5},{7,4},{8,11},{9,10},{10,... | collective-permute-start | bytes 589832 | tf_op jit(solution)/shard_map/ppermute | solution.py:348
  70.5 2.6 %collective-permute-start.14 = (bf16[3,96,256]{2,1,0:T(8,128)(2,1)S(1)}, bf16[3,96,256]{2,1,0:T(8,128)(2,1)S(1)}, u32[]{:S(2)}, u32[]{:S(2)}) collective-permute-start(bf16[3,96,256]{2,1,0:T(8,128)(2,1)S(1)} %get-tuple-element.40), channel_id=1, source_target_pairs={{0,3},{1,2},{2,1},{3,0},{4,7},{5,6},{6,5},{7,4},{8,11},{9,10},{10,... | collective-permute-start | bytes 442376 | tf_op jit(solution)/shard_map/ppermute | solution.py:348
  73.2 4.9 %collective-permute-done.13.refs_2_ = bf16[3,96,256]{2,1,0:T(8,128)(2,1)S(1)} collective-permute-done((bf16[3,96,256]{2,1,0:T(8,128)(2,1)S(1)}, bf16[3,96,256]{2,1,0:T(8,128)(2,1)S(1)}, u32[]{:S(2)}, u32[]{:S(2)}) %collective-permute-start.13) | collective-permute-done | bytes 147488 | tf_op jit(solution)/shard_map/ppermute | solution.py:348
  78.1 5.9 %collective-permute-done.14.refs_3_ = bf16[3,96,256]{2,1,0:T(8,128)(2,1)S(1)} collective-permute-done((bf16[3,96,256]{2,1,0:T(8,128)(2,1)S(1)}, bf16[3,96,256]{2,1,0:T(8,128)(2,1)S(1)}, u32[]{:S(2)}, u32[]{:S(2)}) %collective-permute-start.14) | collective-permute-done | bytes 147488 | tf_op jit(solution)/shard_map/ppermute | solution.py:348
  84.0 0.8 shard_map.77.refs_4_
  84.9 0.9 %shard_map.78 = bf16[7,96,1024]{2,1,0:T(8,128)(2,1)} custom-call(s32[1]{0:T(128)} %bitcast.me, bf16[4,96,256]{2,1,0:T(8,128)(2,1)S(1)} %get-tuple-element.33.refs_0_, bf16[4,96,256]{2,1,0:T(8,128)(2,1)S(1)} %collective-permute-done.9.refs_1_, bf16[4,96,256]{2,1,0:T(8,128)(2,1)S(1)} %collective-permute-done.10.refs_2_, ...), custom_call_target="tpu_custom_call", output_to_operand_aliasing={{}: (5, {})} | custom-call | tf_op jit(solution)/shard_map/pallas_call | solution.py:335
  (31 shorter events, 3.5 us)
Async XLA Ops:
  0.6 0.7 copy-start.1
  1.3 0.7 copy-start.5
  2.0 14.4 %copy-start = (f32[96,512]{1,0:T(8,128)S(1)}, f32[96,512]{1,0:T(8,128)}, u32[]{:S(2)}) copy-start(f32[96,512]{1,0:T(8,128)} %noise.1) | copy-start | bytes 589828
  2.0 14.4 %copy-start.3 = (f32[512]{0:T(512)S(1)}, f32[512]{0:T(512)}, u32[]{:S(2)}) copy-start(f32[512]{0:T(512)} %param.10) | copy-start | bytes 6148
  2.0 25.2 %copy-start.2 = (s32[512]{0:T(512)S(1)}, s32[512]{0:T(512)}, u32[]{:S(2)}) copy-start(s32[512]{0:T(512)} %param.8) | copy-start | bytes 6148
  2.0 25.2 %copy-start.4 = (f32[512]{0:T(512)S(1)}, f32[512]{0:T(512)}, u32[]{:S(2)}) copy-start(f32[512]{0:T(512)} %param.9) | copy-start | bytes 6148
  5.1 6.2 %collective-permute-start.3 = (bf16[96,512]{1,0:T(8,128)(2,1)S(1)}, bf16[96,512]{1,0:T(8,128)(2,1)S(1)}, u32[]{:S(2)}, u32[]{:S(2)}) collective-permute-start(bf16[96,512]{1,0:T(8,128)(2,1)S(1)} %get-tuple-element.26.mine), channel_id=1, source_target_pairs={{0,4},{4,0},{1,5},{5,1},{2,6},{6,2},{3,7},{7,3},{8,12},{12,8},{9,1... | collective-permute-start | bytes 294920 | tf_op jit(solution)/shard_map/ppermute | solution.py:348
  12.1 15.1 %all-to-all-start = ((bf16[4,96,512]{2,1,0:T(8,128)(2,1)}), bf16[4,96,512]{2,1,0:T(8,128)(2,1)S(1)}, u32[]{:S(2)}, u32[]{:S(2)}) async-start(bf16[4,96,512]{2,1,0:T(8,128)(2,1)} %join.1), calls=%async_computation | async-start | bytes 786432 | tf_op jit(solution)/shard_map/all_to_all | solution.py:352
  16.4 10.8 %collective-permute-start.6 = (bf16[96,512]{1,0:T(8,128)(2,1)S(1)}, bf16[96,512]{1,0:T(8,128)(2,1)S(1)}, u32[]{:S(2)}, u32[]{:S(2)}) collective-permute-start(bf16[96,512]{1,0:T(8,128)(2,1)S(1)} %scale.1.refs_0_), channel_id=1, source_target_pairs={{0,3},{1,2},{2,1},{3,0},{4,7},{5,6},{6,5},{7,4},{8,11},{9,10},{10,... | collective-permute-start | bytes 294920 | tf_op jit(solution)/shard_map/ppermute | solution.py:348
  19.7 7.5 %collective-permute-start.5 = (bf16[96,512]{1,0:T(8,128)(2,1)S(1)}, bf16[96,512]{1,0:T(8,128)(2,1)S(1)}, u32[]{:S(2)}, u32[]{:S(2)}) collective-permute-start(bf16[96,512]{1,0:T(8,128)(2,1)S(1)} %scale.1.refs_0_), channel_id=1, source_target_pairs={{0,2},{1,3},{2,0},{3,1},{4,6},{5,7},{6,4},{7,5},{8,10},{9,11},{10,... | collective-permute-start | bytes 294920 | tf_op jit(solution)/shard_map/ppermute | solution.py:348
  20.6 6.6 %collective-permute-start.4 = (bf16[96,512]{1,0:T(8,128)(2,1)S(1)}, bf16[96,512]{1,0:T(8,128)(2,1)S(1)}, u32[]{:S(2)}, u32[]{:S(2)}) collective-permute-start(bf16[96,512]{1,0:T(8,128)(2,1)S(1)} %scale.1.refs_0_), channel_id=1, source_target_pairs={{0,1},{1,0},{2,3},{3,2},{4,5},{5,4},{6,7},{7,6},{8,9},{9,8},{10,11... | collective-permute-start | bytes 294920 | tf_op jit(solution)/shard_map/ppermute | solution.py:348
  28.2 26.3 %collective-permute-start.8 = (bf16[784,512]{1,0:T(8,128)(2,1)S(1)}, bf16[784,512]{1,0:T(8,128)(2,1)S(1)}, u32[]{:S(2)}, u32[]{:S(2)}) collective-permute-start(bf16[784,512]{1,0:T(8,128)(2,1)S(1)} %get-tuple-element.27.refs_4_), channel_id=1, source_target_pairs={{8,16},{24,32},{40,48},{56,64},{72,80},{88,96},{104,112},{16,8},{3... | collective-permute-start | bytes 2408456 | tf_op jit(solution)/shard_map/ppermute | solution.py:379
  30.6 23.9 %collective-permute-start.7 = (bf16[784,512]{1,0:T(8,128)(2,1)S(1)}, bf16[784,512]{1,0:T(8,128)(2,1)}, u32[]{:S(2)}, u32[]{:S(2)}) collective-permute-start(bf16[784,512]{1,0:T(8,128)(2,1)S(1)} %get-tuple-element.27.refs_4_), channel_id=1, source_target_pairs={{0,8},{8,0},{16,24},{24,16},{32,40},{40,32},{48,56},{56,48},{64,72... | collective-permute-start | bytes 2408456 | tf_op jit(solution)/shard_map/ppermute | solution.py:348
  32.2 11.1 %collective-permute-start = (bf16[7,96,256]{2,1,0:T(8,128)(2,1)}, bf16[7,96,256]{2,1,0:T(8,128)(2,1)S(1)}, u32[]{:S(2)}, u32[]{:S(2)}) collective-permute-start(bf16[7,96,256]{2,1,0:T(8,128)(2,1)} %get-tuple-element.23), channel_id=1, source_target_pairs={{0,1},{1,0},{2,3},{3,2},{4,5},{5,4},{6,7},{7,6},{8,9},{9,8},{10,11... | collective-permute-start | bytes 1032200 | tf_op jit(solution)/shard_map/ppermute | solution.py:348
  32.5 19.7 %collective-permute-start.1 = (bf16[7,96,256]{2,1,0:T(8,128)(2,1)}, bf16[7,96,256]{2,1,0:T(8,128)(2,1)S(1)}, u32[]{:S(2)}, u32[]{:S(2)}) collective-permute-start(bf16[7,96,256]{2,1,0:T(8,128)(2,1)} %get-tuple-element.24), channel_id=1, source_target_pairs={{0,2},{1,3},{2,0},{3,1},{4,6},{5,7},{6,4},{7,5},{8,10},{9,11},{10,... | collective-permute-start | bytes 1032200 | tf_op jit(solution)/shard_map/ppermute | solution.py:348
  36.1 18.4 %collective-permute-start.2 = (bf16[7,96,256]{2,1,0:T(8,128)(2,1)S(1)}, bf16[7,96,256]{2,1,0:T(8,128)(2,1)S(1)}, u32[]{:S(2)}, u32[]{:S(2)}) collective-permute-start(bf16[7,96,256]{2,1,0:T(8,128)(2,1)S(1)} %get-tuple-element.25), channel_id=1, source_target_pairs={{0,3},{1,2},{2,1},{3,0},{4,7},{5,6},{6,5},{7,4},{8,11},{9,10},{10,... | collective-permute-start | bytes 1032200 | tf_op jit(solution)/shard_map/ppermute | solution.py:348
  36.9 17.6 %all-to-all-start.1 = ((f32[16,1,128]{2,1,0:T(1,128)}), f32[16,1,128]{2,1,0:T(1,128)S(1)}, u32[]{:S(2)}, u32[]{:S(2)}) async-start(f32[16,1,128]{2,1,0:T(1,128)} %bitcast.8), calls=%async_computation.1 | async-start | bytes 16384 | tf_op jit(solution)/shard_map/all_to_all | solution.py:352
  60.4 10.1 %collective-permute-start.12 = (bf16[3,96,256]{2,1,0:T(8,128)(2,1)S(1)}, bf16[3,96,256]{2,1,0:T(8,128)(2,1)S(1)}, u32[]{:S(2)}, u32[]{:S(2)}) collective-permute-start(bf16[3,96,256]{2,1,0:T(8,128)(2,1)S(1)} %get-tuple-element.38), channel_id=1, source_target_pairs={{0,1},{1,0},{2,3},{3,2},{4,5},{5,4},{6,7},{7,6},{8,9},{9,8},{10,11... | collective-permute-start | bytes 442376 | tf_op jit(solution)/shard_map/ppermute | solution.py:348
  64.9 19.9 %collective-permute-start.9 = (bf16[4,96,256]{2,1,0:T(8,128)(2,1)S(1)}, bf16[4,96,256]{2,1,0:T(8,128)(2,1)S(1)}, u32[]{:S(2)}, u32[]{:S(2)}) collective-permute-start(bf16[4,96,256]{2,1,0:T(8,128)(2,1)S(1)} %get-tuple-element.34), channel_id=1, source_target_pairs={{0,1},{1,0},{2,3},{3,2},{4,5},{5,4},{6,7},{7,6},{8,9},{9,8},{10,11... | collective-permute-start | bytes 589832 | tf_op jit(solution)/shard_map/ppermute | solution.py:348
  67.0 17.9 %collective-permute-start.10 = (bf16[4,96,256]{2,1,0:T(8,128)(2,1)S(1)}, bf16[4,96,256]{2,1,0:T(8,128)(2,1)S(1)}, u32[]{:S(2)}, u32[]{:S(2)}) collective-permute-start(bf16[4,96,256]{2,1,0:T(8,128)(2,1)S(1)} %get-tuple-element.35), channel_id=1, source_target_pairs={{0,2},{1,3},{2,0},{3,1},{4,6},{5,7},{6,4},{7,5},{8,10},{9,11},{10,... | collective-permute-start | bytes 589832 | tf_op jit(solution)/shard_map/ppermute | solution.py:348
  67.0 17.8 %collective-permute-start.11 = (bf16[4,96,256]{2,1,0:T(8,128)(2,1)S(1)}, bf16[4,96,256]{2,1,0:T(8,128)(2,1)S(1)}, u32[]{:S(2)}, u32[]{:S(2)}) collective-permute-start(bf16[4,96,256]{2,1,0:T(8,128)(2,1)S(1)} %get-tuple-element.36), channel_id=1, source_target_pairs={{0,3},{1,2},{2,1},{3,0},{4,7},{5,6},{6,5},{7,4},{8,11},{9,10},{10,... | collective-permute-start | bytes 589832 | tf_op jit(solution)/shard_map/ppermute | solution.py:348
  69.8 8.3 %collective-permute-start.13 = (bf16[3,96,256]{2,1,0:T(8,128)(2,1)S(1)}, bf16[3,96,256]{2,1,0:T(8,128)(2,1)S(1)}, u32[]{:S(2)}, u32[]{:S(2)}) collective-permute-start(bf16[3,96,256]{2,1,0:T(8,128)(2,1)S(1)} %get-tuple-element.39), channel_id=1, source_target_pairs={{0,2},{1,3},{2,0},{3,1},{4,6},{5,7},{6,4},{7,5},{8,10},{9,11},{10,... | collective-permute-start | bytes 442376 | tf_op jit(solution)/shard_map/ppermute | solution.py:348
  70.5 13.5 %collective-permute-start.14 = (bf16[3,96,256]{2,1,0:T(8,128)(2,1)S(1)}, bf16[3,96,256]{2,1,0:T(8,128)(2,1)S(1)}, u32[]{:S(2)}, u32[]{:S(2)}) collective-permute-start(bf16[3,96,256]{2,1,0:T(8,128)(2,1)S(1)} %get-tuple-element.40), channel_id=1, source_target_pairs={{0,3},{1,2},{2,1},{3,0},{4,7},{5,6},{6,5},{7,4},{8,11},{9,10},{10,... | collective-permute-start | bytes 442376 | tf_op jit(solution)/shard_map/ppermute | solution.py:348

commit v4 on v3

v4 whole, which is shorter than its diff:
```python
import functools

import jax
import jax.numpy as jnp
from jax import lax
from jax.experimental import pallas as pl
from jax.experimental.pallas import tpu as pltpu
from jax.sharding import PartitionSpec as P


RADIUS = 1024
F32 = jnp.float32
BF16 = jnp.bfloat16


def params(megabytes=12):
    return pltpu.CompilerParams(vmem_limit_bytes=megabytes * 2**20)


def whole():
    return pl.BlockSpec(memory_space=pltpu.VMEM)


def scalars():
    return pl.BlockSpec(memory_space=pltpu.SMEM)


def anywhere():
    return pl.BlockSpec(memory_space=pl.ANY)


def shape_of(shape, dtype=BF16):
    return pltpu.VMEM(shape, dtype)


def in_vmem(values):
    return [pltpu.with_memory_space_constraint(v, pltpu.VMEM) for v in values]


def in_hbm(value):
    return pltpu.with_memory_space_constraint(value, pltpu.HBM)


def split_rows(value):
    first = value.astype(BF16)
    rest = value - first.astype(F32)
    second = rest.astype(BF16)
    third = (rest - second.astype(F32)).astype(BF16)
    return [first, second, third]


def tile_block(me, s, width):
    return pl.multiple_of(jnp.bitwise_xor(me, s) * width, width)


def pack_body(me, far_weights, ensemble, tiles, *rest):
    *blocks, predicted, weights, buffer, arrived, left = rest
    peers, var_count, _, width = buffer.shape
    starts = [tile_block(me[0], s, width) for s in range(peers)]
    loads = [
        pltpu.make_async_copy(
            ensemble.at[:, :, pl.ds(starts[s], width)], buffer.at[s], arrived.at[s]
        )
        for s in range(peers)
    ]
    stores = [pltpu.make_async_copy(buffer.at[s], blocks[s], left.at[s]) for s in range(peers)]
    light = pltpu.make_async_copy(far_weights, weights, arrived.at[peers])
    light.start()
    for load in loads:
        load.start()
    light.wait()
    rows = lax.broadcasted_iota(jnp.int32, (width, tiles.shape[1]), 0)
    total = jnp.zeros(predicted.shape, F32)
    for s in range(peers):
        chosen = jnp.where(tiles[...] - starts[s] == rows, 1.0, 0.0).astype(BF16)
        loads[s].wait()
        stores[s].start()
        mixed = weights[0] * buffer[s, 0].astype(F32)
        for l in range(1, var_count):
            mixed = mixed + weights[l] * buffer[s, l].astype(F32)
        high = mixed.astype(BF16)
        low = (mixed - high.astype(F32)).astype(BF16)
        total = total + jnp.dot(high, chosen, preferred_element_type=F32)
        total = total + jnp.dot(low, chosen, preferred_element_type=F32)
    predicted[...] = total.astype(BF16)
    for store in stores:
        store.wait()


def pack(me, ensemble, weights, tiles, peers):
    var_count, own, tile_count = ensemble.shape
    width = tile_count // peers
    obs = tiles.shape[1]
    return pl.pallas_call(
        pack_body,
        in_specs=[scalars(), anywhere(), anywhere(), whole()],
        out_specs=[anywhere()] * peers + [whole()],
        out_shape=[pltpu.HBM((var_count, own, width), BF16)] * peers + [shape_of((own, obs))],
        scratch_shapes=[
            pltpu.SMEM((var_count,), F32),
            pltpu.VMEM((peers, var_count, own, width), BF16),
            pltpu.SemaphoreType.DMA((peers + 1,)),
            pltpu.SemaphoreType.DMA((peers,)),
        ],
        compiler_params=params(),
        name="pack",
    )(me, in_hbm(weights), in_hbm(ensemble), tiles)


def scale_body(noise, error, out):
    scaled = (jnp.sqrt(error[...]) * noise[...]).astype(BF16)
    for j in range(out.shape[0]):
        out[j] = scaled


def scale(noise, error, peers):
    return pl.pallas_call(
        scale_body,
        in_specs=[whole()] * 2,
        out_specs=whole(),
        out_shape=shape_of((peers, *noise.shape)),
        compiler_params=params(),
        name="scale",
    )(noise, error)


def join_body(mine, other, out):
    out[...] = (mine[...].astype(F32) + other[...].astype(F32)).astype(BF16)


def join(mine, other):
    return pl.pallas_call(
        join_body,
        in_specs=[whole()] * 2,
        out_specs=whole(),
        out_shape=shape_of(mine.shape),
        compiler_params=params(),
        name="join",
    )(mine, other)


def stats_body(me, values, error, tiles, *refs):
    *gathered, packet, sums, ordered = refs
    peers = len(gathered)
    own, obs = gathered[0].shape
    members = peers * own
    for s in range(peers):
        part = jnp.sum(gathered[s][...].astype(F32), axis=0, keepdims=True)
        ordered[jnp.bitwise_xor(me[0], s)] = jnp.broadcast_to(part, ordered.shape[1:])
    mean = (ordered[0] + ordered[1] + ordered[2] + ordered[3])[0:1] / members
    for s in range(peers):
        dev = gathered[s][...].astype(F32) - mean
        packet[s * own : (s + 1) * own] = dev.astype(BF16)
        part = jnp.sum(dev * dev, axis=0, keepdims=True)
        ordered[jnp.bitwise_xor(me[0], s)] = jnp.broadcast_to(part, ordered.shape[1:])
    spread = (ordered[0] + ordered[1] + ordered[2] + ordered[3])[0:1] / (members - 1)
    innovation = values[...] - mean
    place = tiles[...]
    rows = split_rows(innovation) + split_rows(error[...]) + split_rows(spread)
    rows += [(place // 32).astype(F32).astype(BF16), (place % 32).astype(F32).astype(BF16)]
    rows += [jnp.zeros((1, obs), BF16)] * (16 - len(rows))
    packet[members:] = jnp.concatenate(rows, axis=0)
    above = jnp.sum(innovation * innovation)
    below = jnp.sum(spread + error[...])
    lane = lax.broadcasted_iota(jnp.int32, sums.shape, 1)
    sums[...] = jnp.where(lane == 0, above, jnp.where(lane == 1, below, 0.0))


def stats(me, gathered, values, error, tiles, regions):
    peers = len(gathered)
    own, obs = gathered[0].shape
    return pl.pallas_call(
        stats_body,
        in_specs=[scalars()] + [whole()] * (3 + peers),
        out_specs=[whole(), whole()],
        out_shape=[shape_of((peers * own + 16, obs)), shape_of((regions, 128), F32)],
        scratch_shapes=[pltpu.VMEM((peers, 8, obs), F32)],
        compiler_params=params(),
        name="stats",
    )(me, values, error, tiles, *gathered)


def scalar_rows(packet, members):
    rows = packet[members:].astype(F32)
    innovation = rows[0:1] + rows[1:2] + rows[2:3]
    error = rows[3:4] + rows[4:5] + rows[5:6]
    spread = rows[6:7] + rows[7:8] + rows[8:9]
    return innovation, error, spread, rows[9:10] * 32.0 + rows[10:11]


def gains(state, anom_t, taper, means, anomalies, gain):
    own = state[0].shape[0]
    parts = [part.astype(F32) for part in state]
    mean = sum(jnp.sum(part, axis=0, keepdims=True) for part in parts) / (own * len(parts))
    means[...] = jnp.broadcast_to(mean, means.shape)
    for s, part in enumerate(parts):
        anomalies[s * own : (s + 1) * own] = (part - mean).astype(BF16)
    obs = taper.shape[0]
    step = obs // 3
    for k in range(0, obs, step):
        covariance = jnp.dot(anom_t[k : k + step], anomalies[...], preferred_element_type=F32)
        gain[k : k + step] = (covariance * taper[k : k + step]).astype(BF16)


def posterior(gain, means, anomalies, perturbed, root, blocks, at):
    own = blocks[0].shape[1]
    increment = jnp.dot(perturbed[...], gain[...], preferred_element_type=F32)
    result = means[0:1] + root * anomalies[...].astype(F32) + increment
    for s, block in enumerate(blocks):
        block[at] = result[s * own : (s + 1) * own].astype(BF16)


def prepare_body(offset, *refs, tile_count):
    *far_packets, anom_t, taper, packets, arrived = refs
    members = anom_t.shape[1]
    obs = packets.shape[2]
    loads = [pltpu.make_async_copy(far_packets[n], packets.at[n], arrived.at[n]) for n in range(3)]
    for load in loads:
        load.start()
    tile = (offset[0] + lax.broadcasted_iota(jnp.int32, (1, taper.shape[1]), 1)).astype(F32)
    for n in range(3):
        loads[n].wait()
        packet = packets.at[n]
        anom_t[n * obs : (n + 1) * obs] = packet[:members].T
        place = scalar_rows(packet, members)[3] + (offset[1 + n] * tile_count).astype(F32)
        column = jnp.broadcast_to(place, (8, obs)).T[:, 0:1]
        near = jnp.maximum(0.0, 1.0 - jnp.abs(tile - column) / RADIUS)
        taper[n * obs : (n + 1) * obs] = near * near / (members - 1)


def prepare(offset, packets, width, tile_count):
    rows, obs = packets[0].shape
    members = rows - 16
    return pl.pallas_call(
        functools.partial(prepare_body, tile_count=tile_count),
        in_specs=[scalars()] + [anywhere()] * 3,
        out_specs=[whole()] * 2,
        out_shape=[shape_of((3 * obs, members)), shape_of((3 * obs, width), F32)],
        scratch_shapes=[pltpu.VMEM((3, rows, obs), BF16), pltpu.SemaphoreType.DMA((3,))],
        compiler_params=params(),
        name="prepare",
    )(offset, *map(in_hbm, packets))


def first_body(me, *refs, peers):
    far_states, far_packets = refs[:peers], refs[peers : peers + 3]
    far_noises, (sums, anom_t, taper) = refs[peers + 3 : peers + 6], refs[peers + 6 : peers + 9]
    refs = refs[peers + 9 :]
    blocks, (perturbed, root_out, inflation_out) = refs[:peers], refs[peers : peers + 3]
    states, packets, noises, means, anomalies, gain, arrived = refs[peers + 3 :]
    count, own, _ = blocks[0].shape
    members = peers * own
    obs = packets.shape[2]
    loads = [
        pltpu.make_async_copy(far_states[s].at[:count], states.at[s], arrived.at[s])
        for s in range(peers)
    ]
    late = [
        pltpu.make_async_copy(source[n], target.at[n], arrived.at[peers + 3 * i + n])
        for i, (source, target) in enumerate(((far_packets, packets), (far_noises, noises)))
        for n in range(3)
    ]
    for load in loads + late:
        load.start()
    for load in loads:
        load.wait()
    for l in range(count):
        state = [states[s, l] for s in range(peers)]
        gains(state, anom_t, taper, means.at[l], anomalies.at[l], gain.at[l])
    for load in late:
        load.wait()
    folded = jnp.sum(sums[...], axis=0, keepdims=True)
    inflation = folded[:, 0:1] / folded[:, 1:2]
    inflation_out[0] = jnp.sum(inflation)
    root = jnp.sqrt(inflation)
    root_out[...] = jnp.broadcast_to(root, root_out.shape)
    for n in range(3):
        innovation, error, spread, _ = scalar_rows(packets.at[n], members)
        bottom = jnp.where(error > 0.0, inflation * spread + error, 1.0)
        factor = jnp.where(error > 0.0, inflation / bottom, 0.0)
        for s in range(peers):
            rows = slice(s * own, (s + 1) * own)
            noise = noises[n, jnp.bitwise_xor(me[0], s)].astype(F32)
            dev = packets[n, rows].astype(F32)
            perturbed[rows, n * obs : (n + 1) * obs] = (
                factor * (innovation + noise - root * dev)
            ).astype(BF16)
    for l in range(count):
        posterior(gain.at[l], means.at[l], anomalies.at[l], perturbed, root, blocks, l)


def working(count, members, obs, width):
    return [
        pltpu.VMEM((count, 8, width), F32),
        pltpu.VMEM((count, members, width), BF16),
        pltpu.VMEM((count, obs, width), BF16),
    ]


def first_updates(me, states, packets, noises, sums, anom_t, taper, count):
    _, own, width = states[0].shape
    peers = len(states)
    members = own * peers
    rows, obs = packets[0].shape
    out = pl.pallas_call(
        functools.partial(first_body, peers=peers),
        in_specs=[scalars()] + [anywhere()] * (peers + 6) + [whole()] * 3,
        out_specs=[whole()] * (peers + 2) + [scalars()],
        out_shape=[shape_of((count, own, width))] * peers
        + [
            shape_of((members, 3 * obs)),
            shape_of((8, 128), F32),
            jax.ShapeDtypeStruct((1,), F32),
        ],
        scratch_shapes=[
            pltpu.VMEM((peers, count, own, width), BF16),
            pltpu.VMEM((3, rows, obs), BF16),
            pltpu.VMEM((3, peers, own, obs), BF16),
            *working(count, members, 3 * obs, width),
            pltpu.SemaphoreType.DMA((peers + 6,)),
        ],
        compiler_params=params(16),
        name="first",
    )(me, *map(in_hbm, (*states, *packets, *noises)), *in_vmem((sums, anom_t, taper)))
    return out[:peers], out[peers], out[peers + 1], out[peers + 2]


def second_body(*refs, first, peers):
    states, (anom_t, perturbed, taper, root) = refs[:peers], refs[peers : peers + 4]
    blocks = refs[peers + 4 : 2 * peers + 4]
    means, anomalies, gain = refs[2 * peers + 4 :]
    count = blocks[0].shape[0]
    for l in range(count):
        state = [states[s][first + l] for s in range(peers)]
        gains(state, anom_t, taper, means.at[l], anomalies.at[l], gain.at[l])
    for l in range(count):
        posterior(gain.at[l], means.at[l], anomalies.at[l], perturbed, root[0:1, 0:1], blocks, l)


def second_updates(states, anom_t, perturbed, taper, root, first):
    var_count, own, width = states[0].shape
    peers = len(states)
    members = own * peers
    count = var_count - first
    return pl.pallas_call(
        functools.partial(second_body, first=first, peers=peers),
        in_specs=[whole()] * (peers + 4),
        out_specs=[whole()] * peers,
        out_shape=[shape_of((count, own, width))] * peers,
        scratch_shapes=working(count, members, anom_t.shape[0], width),
        compiler_params=params(),
        name="second",
    )(*in_vmem((*states, anom_t, perturbed, taper, root)))


def place_body(me, *refs, first, peers):
    blocks, out, done = refs[:peers], refs[-2], refs[-1]
    count, _, width = blocks[0].shape
    copies = [
        pltpu.make_async_copy(
            blocks[s],
            out.at[first : first + count, :, pl.ds(tile_block(me[0], s, width), width)],
            done.at[s],
        )
        for s in range(peers)
    ]
    for copy in copies:
        copy.start()
    for copy in copies:
        copy.wait()


def place(me, blocks, first, var_count, before=None):
    peers = len(blocks)
    _, own, width = blocks[0].shape
    more = [] if before is None else [before]
    return pl.pallas_call(
        functools.partial(place_body, first=first, peers=peers),
        in_specs=[scalars()] + [anywhere()] * (peers + len(more)),
        out_specs=anywhere(),
        out_shape=pltpu.HBM((var_count, own, peers * width), BF16),
        scratch_shapes=[pltpu.SemaphoreType.DMA((peers,))],
        input_output_aliases={1 + peers: 0} if more else {},
        compiler_params=params(),
    )(me, *in_vmem(blocks), *more)


def swapped(value, axis, distance):
    pairs = [(i, i ^ distance) for i in range(lax.axis_size(axis))]
    return lax.ppermute(value, axis, pairs)


def exchanged(blocks, axis):
    return lax.all_to_all(blocks, axis, split_axis=0, concat_axis=0, tiled=True)


def traded(blocks, order):
    out = list(blocks)
    for s in order:
        out[s] = swapped(blocks[s], "member", s)
    return out


def shards(ensemble, obs_weights, obs_tiles, obs_values, obs_error, obs_noise):
    peers = lax.axis_size("member")
    regions = lax.axis_size("region")
    var_count, _, tile_count = ensemble.shape
    width = tile_count // peers
    me = lax.axis_index("member").astype(jnp.int32)[None]
    region = lax.axis_index("region").astype(jnp.int32)
    tiles, values, error = (a[None, :] for a in (obs_tiles, obs_values, obs_error))
    *blocks, partial = pack(me, ensemble, obs_weights, tiles, peers)
    other = swapped(partial, "depth", 1)
    noise = exchanged(scale(obs_noise, error, peers), "member")
    predicted = traded([join(partial, other)] * peers, (1, 3, 2))
    pairs = [(i, i + 1) for i in range(1, regions - 1, 2)]
    pairs += [(j, i) for i, j in pairs]
    near_noise = swapped(noise, "region", 1)
    far_noise = lax.ppermute(noise, "region", pairs)
    packet, sums = stats(me, predicted, values, error, tiles, regions)
    near = swapped(packet, "region", 1)
    far = lax.ppermute(packet, "region", pairs)
    states = traded(blocks, (1, 3, 2))
    all_sums = exchanged(sums, "region")
    side = 1 - 2 * (region % 2)
    offset = jnp.stack([me[0] * width, jnp.zeros_like(side), side, -side])
    packets = (packet, near, far)
    anom_t, taper = prepare(offset, packets, width, tile_count)
    half = (var_count + 1) // 2
    ready, perturbed, root, inflation = first_updates(
        me, states, packets, (noise, near_noise, far_noise), all_sums, anom_t, taper, half
    )
    early = traded(ready, (1, 3, 2))
    ready = second_updates(states, anom_t, perturbed, taper, root, half)
    late = traded(ready, (1, 3, 2))
    output = place(me, early, 0, var_count)
    output = place(me, late, half, var_count, output)
    return (output, inflation.reshape(()))


def solution(mesh):
    return jax.shard_map(
        shards,
        mesh=mesh,
        in_specs=(
            P("depth", "member", "region"),
            P("depth"),
            P("region"),
            P("region"),
            P("region"),
            P("member", "region"),
        ),
        out_specs=(P("depth", "member", "region"), P()),
        check_vma=False,
    )
```

time: 86.1 us -> 87 us (1.010)
  the two profiles are of different devices: /device:TPU:24 before, /device:TPU:0 now
where the time goes in v4:
time: 87 us; the launch traced here: 86.6 us
  starting transfers between devices  34.3 us (39%)
  waiting for transfers between devices  21.6 us (25%)
  Pallas kernels  16.6 us (19%)
  blocking collectives  11.6 us (13%)
  local copies, waits for them, and re-layouts  1.73 us (2%)
    ppermute x15, starting transfers between devices, swapped(): return lax.ppermute(value, axis, pairs)  27.8 us
    ppermute x15, waiting for transfers between devices, swapped(): return lax.ppermute(value, axis, pairs)  18.5 us
    all_to_all x1, blocking collectives, exchanged(): return lax.all_to_all(blocks, axis, split_axis=0, concat_axis=0, tiled=True)  11.6 us
    pallas_call x1, Pallas kernels, first_updates(): pl.pallas_call(functools.partial(first_body, peers=peers), in_specs=[scal...  5.03 us
    all_to_all x1, starting transfers between devices, exchanged(): return lax.all_to_all(blocks, axis, split_axis=0, concat_axis=0, tiled=True)  4.44 us
    pallas_call x1, Pallas kernels, second_updates(): pl.pallas_call(functools.partial(second_body, first=first, peers=peers),...  3.57 us
    all_to_all x1, waiting for transfers between devices, exchanged(): return lax.all_to_all(blocks, axis, split_axis=0, concat_axis=0, tiled=True)  3.06 us
    pallas_call x1, Pallas kernels, prepare(): pl.pallas_call(functools.partial(prepare_body, tile_count=tile_count), in...  2.76 us
  transfers between devices with their start and end apart: 18, of which 9 were waited for; matrix products, arithmetic and copies ran while one was open for 0% of the time, Pallas kernels for 8%

profile of v4, /device:TPU:0, one launch (start us, length us, event | category | flops | bytes accessed | tf_op | source)
XLA Modules:
  0.0 86.6 jit_solution(6208494719338506254)
XLA Ops:
  1.4 2.5 %pack.1 = (bf16[7,96,256]{2,1,0:T(8,128)(2,1)}, bf16[7,96,256]{2,1,0:T(8,128)(2,1)}, bf16[7,96,256]{2,1,0:T(8,128)(2,1)}, bf16[7,96,256]{2,1,0:T(8,128)(2,1)}, bf16[96,512]{1,0:T(8,128)(2,1)S(1)}) custom-call(s32[1]{0:T(128)} %bitcast.me, f32[7]{0:T(128)} %far_weights.1, bf16[7,96,1024]{2,1,0:T(8,128)(2,1)} %ensemble.1, s32[1,512]{1,0:T(1,128)S(1)} %bitcast.13), custom_call_target="tpu_custom_call" | custom-call | tf_op jit(solution)/shard_map/pack/pallas_call | solution.py:94
  3.9 3.4 %collective-permute-start.3 = (bf16[96,512]{1,0:T(8,128)(2,1)S(1)}, bf16[96,512]{1,0:T(8,128)(2,1)S(1)}, u32[]{:S(2)}, u32[]{:S(2)}) collective-permute-start(bf16[96,512]{1,0:T(8,128)(2,1)S(1)} %get-tuple-element.26.mine), channel_id=1, source_target_pairs={{0,4},{4,0},{1,5},{5,1},{2,6},{6,2},{3,7},{7,3},{8,12},{12,8},{9,1... | collective-permute-start | bytes 294920 | tf_op jit(solution)/shard_map/ppermute | solution.py:390
  7.2 2.8 %collective-permute-done.3.other = bf16[96,512]{1,0:T(8,128)(2,1)S(1)} collective-permute-done((bf16[96,512]{1,0:T(8,128)(2,1)S(1)}, bf16[96,512]{1,0:T(8,128)(2,1)S(1)}, u32[]{:S(2)}, u32[]{:S(2)}) %collective-permute-start.3) | collective-permute-done | bytes 98336 | tf_op jit(solution)/shard_map/ppermute | solution.py:390
  10.1 3.0 %collective-permute-start.6 = (bf16[96,512]{1,0:T(8,128)(2,1)S(1)}, bf16[96,512]{1,0:T(8,128)(2,1)S(1)}, u32[]{:S(2)}, u32[]{:S(2)}) collective-permute-start(bf16[96,512]{1,0:T(8,128)(2,1)S(1)} %join.1.refs_0_), channel_id=1, source_target_pairs={{0,3},{1,2},{2,1},{3,0},{4,7},{5,6},{6,5},{7,4},{8,11},{9,10},{10,... | collective-permute-start | bytes 294920 | tf_op jit(solution)/shard_map/ppermute | solution.py:390
  14.3 2.8 %collective-permute-done.6.refs_3_ = bf16[96,512]{1,0:T(8,128)(2,1)S(1)} collective-permute-done((bf16[96,512]{1,0:T(8,128)(2,1)S(1)}, bf16[96,512]{1,0:T(8,128)(2,1)S(1)}, u32[]{:S(2)}, u32[]{:S(2)}) %collective-permute-start.6) | collective-permute-done | bytes 98336 | tf_op jit(solution)/shard_map/ppermute | solution.py:390
  17.0 2.1 %collective-permute-done.5.refs_2_ = bf16[96,512]{1,0:T(8,128)(2,1)S(1)} collective-permute-done((bf16[96,512]{1,0:T(8,128)(2,1)S(1)}, bf16[96,512]{1,0:T(8,128)(2,1)S(1)}, u32[]{:S(2)}, u32[]{:S(2)}) %collective-permute-start.5) | collective-permute-done | bytes 98336 | tf_op jit(solution)/shard_map/ppermute | solution.py:390
  20.8 3.3 %collective-permute-start.7 = (bf16[400,512]{1,0:T(8,128)(2,1)S(1)}, bf16[400,512]{1,0:T(8,128)(2,1)S(1)}, u32[]{:S(2)}, u32[]{:S(2)}) collective-permute-start(bf16[400,512]{1,0:T(8,128)(2,1)S(1)} %get-tuple-element.27.refs_0_.refs_4_), channel_id=1, source_target_pairs={{0,8},{8,0},{16,24},{24,16},{32,40},{40,32},{48,56},{56,48},{64,72... | collective-permute-start | bytes 1228808 | tf_op jit(solution)/shard_map/ppermute | solution.py:390
  24.2 11.6 %all_to_all.16.refs_7_ = bf16[4,96,512]{2,1,0:T(8,128)(2,1)} all-to-all(bf16[4,96,512]{2,1,0:T(8,128)(2,1)S(1)} %scale.1), channel_id=1, replica_groups=mesh['region'=16,'depth'=2,'member'=4] {'member'}, dimensions={0} | all-to-all | bytes 786432 | tf_op jit(solution)/shard_map/all_to_all | solution.py:394
  35.8 1.4 %collective-permute-start.10 = (bf16[4,96,512]{2,1,0:T(8,128)(2,1)}, bf16[4,96,512]{2,1,0:T(8,128)(2,1)}, u32[]{:S(2)}, u32[]{:S(2)}) collective-permute-start(bf16[4,96,512]{2,1,0:T(8,128)(2,1)} %all_to_all.16.refs_7_), channel_id=1, source_target_pairs={{8,16},{24,32},{40,48},{56,64},{72,80},{88,96},{104,112},{16,8},{3... | collective-permute-start | bytes 1179656 | tf_op jit(solution)/shard_map/ppermute | solution.py:419
  37.2 2.6 %collective-permute-start.9 = (bf16[4,96,512]{2,1,0:T(8,128)(2,1)}, bf16[4,96,512]{2,1,0:T(8,128)(2,1)}, u32[]{:S(2)}, u32[]{:S(2)}) collective-permute-start(bf16[4,96,512]{2,1,0:T(8,128)(2,1)} %all_to_all.16.refs_7_), channel_id=1, source_target_pairs={{0,8},{8,0},{16,24},{24,16},{32,40},{40,32},{48,56},{56,48},{64,72... | collective-permute-start | bytes 1179656 | tf_op jit(solution)/shard_map/ppermute | solution.py:390
  40.4 2.1 %collective-permute-start.1 = (bf16[7,96,256]{2,1,0:T(8,128)(2,1)}, bf16[7,96,256]{2,1,0:T(8,128)(2,1)}, u32[]{:S(2)}, u32[]{:S(2)}) collective-permute-start(bf16[7,96,256]{2,1,0:T(8,128)(2,1)} %get-tuple-element.24), channel_id=1, source_target_pairs={{0,2},{1,3},{2,0},{3,1},{4,6},{5,7},{6,4},{7,5},{8,10},{9,11},{10,... | collective-permute-start | bytes 1032200 | tf_op jit(solution)/shard_map/ppermute | solution.py:390
  42.5 2.1 %collective-permute-start.2 = (bf16[7,96,256]{2,1,0:T(8,128)(2,1)}, bf16[7,96,256]{2,1,0:T(8,128)(2,1)}, u32[]{:S(2)}, u32[]{:S(2)}) collective-permute-start(bf16[7,96,256]{2,1,0:T(8,128)(2,1)} %get-tuple-element.25), channel_id=1, source_target_pairs={{0,3},{1,2},{2,1},{3,0},{4,7},{5,6},{6,5},{7,4},{8,11},{9,10},{10,... | collective-permute-start | bytes 1032200 | tf_op jit(solution)/shard_map/ppermute | solution.py:390
  44.5 4.4 %all-to-all-start.1 = ((f32[16,1,128]{2,1,0:T(1,128)}), f32[16,1,128]{2,1,0:T(1,128)S(1)}, u32[]{:S(2)}, u32[]{:S(2)}) async-start(f32[16,1,128]{2,1,0:T(1,128)} %bitcast.8), calls=%async_computation.1 | async-start | bytes 16384 | tf_op jit(solution)/shard_map/all_to_all | solution.py:394
  49.1 2.8 %prepare.1 = (bf16[1536,384]{1,0:T(8,128)(2,1)S(1)}, f32[1536,256]{1,0:T(8,128)S(1)}) custom-call(s32[4]{0:T(128)S(1)} %pad_add_fusion.offset, bf16[400,512]{1,0:T(8,128)(2,1)} %copy-done, bf16[400,512]{1,0:T(8,128)(2,1)} %copy-done.10, bf16[400,512]{1,0:T(8,128)(2,1)} %copy-done.9), custom_call_target="tpu_custom_call" | custom-call | tf_op jit(solution)/shard_map/prepare/pallas_call | solution.py:234
  51.9 3.1 %all-to-all-done.1 = f32[16,1,128]{2,1,0:T(1,128)S(1)} async-done(((f32[16,1,128]{2,1,0:T(1,128)}), f32[16,1,128]{2,1,0:T(1,128)S(1)}, u32[]{:S(2)}, u32[]{:S(2)}) %all-to-all-start.1) | async-done | bytes 8224 | tf_op jit(solution)/shard_map/all_to_all | solution.py:394
  54.9 3.4 %collective-permute-done.1.refs_2_ = bf16[7,96,256]{2,1,0:T(8,128)(2,1)} collective-permute-done((bf16[7,96,256]{2,1,0:T(8,128)(2,1)}, bf16[7,96,256]{2,1,0:T(8,128)(2,1)}, u32[]{:S(2)}, u32[]{:S(2)}) %collective-permute-start.1) | collective-permute-done | bytes 344096 | tf_op jit(solution)/shard_map/ppermute | solution.py:390
  58.3 2.6 %collective-permute-done.2.refs_3_ = bf16[7,96,256]{2,1,0:T(8,128)(2,1)} collective-permute-done((bf16[7,96,256]{2,1,0:T(8,128)(2,1)}, bf16[7,96,256]{2,1,0:T(8,128)(2,1)}, u32[]{:S(2)}, u32[]{:S(2)}) %collective-permute-start.2) | collective-permute-done | bytes 344096 | tf_op jit(solution)/shard_map/ppermute | solution.py:390
  60.9 5.0 %first.1 = (bf16[4,96,256]{2,1,0:T(8,128)(2,1)S(1)}, bf16[4,96,256]{2,1,0:T(8,128)(2,1)S(1)}, bf16[4,96,256]{2,1,0:T(8,128)(2,1)S(1)}, bf16[4,96,256]{2,1,0:T(8,...) custom-call(s32[1]{0:T(128)} %bitcast.me, ...), custom_call_target="tpu_custom_call" | custom-call | tf_op jit(solution)/shard_map/first/pallas_call | solution.py:305
  66.0 3.5 %collective-permute-start.15 = (bf16[4,96,256]{2,1,0:T(8,128)(2,1)S(1)}, bf16[4,96,256]{2,1,0:T(8,128)(2,1)S(1)}, u32[]{:S(2)}, u32[]{:S(2)}) collective-permute-start(bf16[4,96,256]{2,1,0:T(8,128)(2,1)S(1)} %get-tuple-element.39), channel_id=1, source_target_pairs={{0,2},{1,3},{2,0},{3,1},{4,6},{5,7},{6,4},{7,5},{8,10},{9,11},{10,... | collective-permute-start | bytes 589832 | tf_op jit(solution)/shard_map/ppermute | solution.py:390
  71.7 3.6 %second.1 = (bf16[3,96,256]{2,1,0:T(8,128)(2,1)S(1)}, bf16[3,96,256]{2,1,0:T(8,128)(2,1)S(1)}, bf16[3,96,256]{2,1,0:T(8,128)(2,1)S(1)}, bf16[3,96,256]{2,1,0:T(8,128)(2,1)S(1)}) custom-call(bf16[7,96,256]{2,1,0:T(8,128)(2,1)S(1)} %copy-done.1, bf16[7,96,256]{2,1,0:T(8,128)(2,1)S(1)} %copy-done.3, bf16[7,96,256]{2,1,0:T(8,128)(2,1)} %collective-permute-done.1.refs_2_, ...), custom_call_target="tpu_custom_call" | custom-call | tf_op jit(solution)/shard_map/second/pallas_call | solution.py:345
  75.4 3.5 %collective-permute-start.12 = (bf16[3,96,256]{2,1,0:T(8,128)(2,1)S(1)}, bf16[3,96,256]{2,1,0:T(8,128)(2,1)S(1)}, u32[]{:S(2)}, u32[]{:S(2)}) collective-permute-start(bf16[3,96,256]{2,1,0:T(8,128)(2,1)S(1)} %get-tuple-element.35), channel_id=1, source_target_pairs={{0,2},{1,3},{2,0},{3,1},{4,6},{5,7},{6,4},{7,5},{8,10},{9,11},{10,... | collective-permute-start | bytes 442376 | tf_op jit(solution)/shard_map/ppermute | solution.py:390
  80.1 1.5 %collective-permute-done.16.refs_3_ = bf16[4,96,256]{2,1,0:T(8,128)(2,1)S(1)} collective-permute-done((bf16[4,96,256]{2,1,0:T(8,128)(2,1)S(1)}, bf16[4,96,256]{2,1,0:T(8,128)(2,1)S(1)}, u32[]{:S(2)}, u32[]{:S(2)}) %collective-permute-start.16) | collective-permute-done | bytes 196640 | tf_op jit(solution)/shard_map/ppermute | solution.py:390
  82.5 1.2 %collective-permute-done.12.refs_2_ = bf16[3,96,256]{2,1,0:T(8,128)(2,1)S(1)} collective-permute-done((bf16[3,96,256]{2,1,0:T(8,128)(2,1)S(1)}, bf16[3,96,256]{2,1,0:T(8,128)(2,1)S(1)}, u32[]{:S(2)}, u32[]{:S(2)}) %collective-permute-start.12) | collective-permute-done | bytes 147488 | tf_op jit(solution)/shard_map/ppermute | solution.py:390
  83.7 2.1 %collective-permute-done.13.refs_3_ = bf16[3,96,256]{2,1,0:T(8,128)(2,1)S(1)} collective-permute-done((bf16[3,96,256]{2,1,0:T(8,128)(2,1)S(1)}, bf16[3,96,256]{2,1,0:T(8,128)(2,1)S(1)}, u32[]{:S(2)}, u32[]{:S(2)}) %collective-permute-start.13) | collective-permute-done | bytes 147488 | tf_op jit(solution)/shard_map/ppermute | solution.py:390
  (45 shorter events, 9.5 us)
Async XLA Ops:
  0.6 23.5 %copy-start.4 = (f32[96,512]{1,0:T(8,128)S(1)}, f32[96,512]{1,0:T(8,128)}, u32[]{:S(2)}) copy-start(f32[96,512]{1,0:T(8,128)} %noise.1) | copy-start | bytes 589828
  1.4 17.8 %copy-start.6 = (s32[512]{0:T(512)S(1)}, s32[512]{0:T(512)}, u32[]{:S(2)}) copy-start(s32[512]{0:T(512)} %param.8) | copy-start | bytes 6148
  1.4 17.8 %copy-start.7 = (f32[512]{0:T(512)S(1)}, f32[512]{0:T(512)}, u32[]{:S(2)}) copy-start(f32[512]{0:T(512)} %param.10) | copy-start | bytes 6148
  1.4 17.8 %copy-start.8 = (f32[512]{0:T(512)S(1)}, f32[512]{0:T(512)}, u32[]{:S(2)}) copy-start(f32[512]{0:T(512)} %param.9) | copy-start | bytes 6148
  3.9 6.2 %collective-permute-start.3 = (bf16[96,512]{1,0:T(8,128)(2,1)S(1)}, bf16[96,512]{1,0:T(8,128)(2,1)S(1)}, u32[]{:S(2)}, u32[]{:S(2)}) collective-permute-start(bf16[96,512]{1,0:T(8,128)(2,1)S(1)} %get-tuple-element.26.mine), channel_id=1, source_target_pairs={{0,4},{4,0},{1,5},{5,1},{2,6},{6,2},{3,7},{7,3},{8,12},{12,8},{9,1... | collective-permute-start | bytes 294920 | tf_op jit(solution)/shard_map/ppermute | solution.py:390
  10.1 7.0 %collective-permute-start.6 = (bf16[96,512]{1,0:T(8,128)(2,1)S(1)}, bf16[96,512]{1,0:T(8,128)(2,1)S(1)}, u32[]{:S(2)}, u32[]{:S(2)}) collective-permute-start(bf16[96,512]{1,0:T(8,128)(2,1)S(1)} %join.1.refs_0_), channel_id=1, source_target_pairs={{0,3},{1,2},{2,1},{3,0},{4,7},{5,6},{6,5},{7,4},{8,11},{9,10},{10,... | collective-permute-start | bytes 294920 | tf_op jit(solution)/shard_map/ppermute | solution.py:390
  13.0 6.1 %collective-permute-start.5 = (bf16[96,512]{1,0:T(8,128)(2,1)S(1)}, bf16[96,512]{1,0:T(8,128)(2,1)S(1)}, u32[]{:S(2)}, u32[]{:S(2)}) collective-permute-start(bf16[96,512]{1,0:T(8,128)(2,1)S(1)} %join.1.refs_0_), channel_id=1, source_target_pairs={{0,2},{1,3},{2,0},{3,1},{4,6},{5,7},{6,4},{7,5},{8,10},{9,11},{10,... | collective-permute-start | bytes 294920 | tf_op jit(solution)/shard_map/ppermute | solution.py:390
  13.8 5.3 %collective-permute-start.4 = (bf16[96,512]{1,0:T(8,128)(2,1)S(1)}, bf16[96,512]{1,0:T(8,128)(2,1)S(1)}, u32[]{:S(2)}, u32[]{:S(2)}) collective-permute-start(bf16[96,512]{1,0:T(8,128)(2,1)S(1)} %join.1.refs_0_), channel_id=1, source_target_pairs={{0,1},{1,0},{2,3},{3,2},{4,5},{5,4},{6,7},{7,6},{8,9},{9,8},{10,11... | collective-permute-start | bytes 294920 | tf_op jit(solution)/shard_map/ppermute | solution.py:390
  20.1 29.0 %copy-start = (bf16[400,512]{1,0:T(8,128)(2,1)}, bf16[400,512]{1,0:T(8,128)(2,1)S(1)}, u32[]{:S(2)}) copy-start(bf16[400,512]{1,0:T(8,128)(2,1)S(1)} %get-tuple-element.27.refs_0_.refs_4_) | copy-start | bytes 1228804
  20.1 20.3 %collective-permute-start.8 = (bf16[400,512]{1,0:T(8,128)(2,1)S(1)}, bf16[400,512]{1,0:T(8,128)(2,1)S(1)}, u32[]{:S(2)}, u32[]{:S(2)}) collective-permute-start(bf16[400,512]{1,0:T(8,128)(2,1)S(1)} %get-tuple-element.27.refs_0_.refs_4_), channel_id=1, source_target_pairs={{8,16},{24,32},{40,48},{56,64},{72,80},{88,96},{104,112},{16,8},{3... | collective-permute-start | bytes 1228808 | tf_op jit(solution)/shard_map/ppermute | solution.py:422
  20.8 21.7 %collective-permute-start.7 = (bf16[400,512]{1,0:T(8,128)(2,1)S(1)}, bf16[400,512]{1,0:T(8,128)(2,1)S(1)}, u32[]{:S(2)}, u32[]{:S(2)}) collective-permute-start(bf16[400,512]{1,0:T(8,128)(2,1)S(1)} %get-tuple-element.27.refs_0_.refs_4_), channel_id=1, source_target_pairs={{0,8},{8,0},{16,24},{24,16},{32,40},{40,32},{48,56},{56,48},{64,72... | collective-permute-start | bytes 1228808 | tf_op jit(solution)/shard_map/ppermute | solution.py:390
  35.8 25.1 %collective-permute-start.10 = (bf16[4,96,512]{2,1,0:T(8,128)(2,1)}, bf16[4,96,512]{2,1,0:T(8,128)(2,1)}, u32[]{:S(2)}, u32[]{:S(2)}) collective-permute-start(bf16[4,96,512]{2,1,0:T(8,128)(2,1)} %all_to_all.16.refs_7_), channel_id=1, source_target_pairs={{8,16},{24,32},{40,48},{56,64},{72,80},{88,96},{104,112},{16,8},{3... | collective-permute-start | bytes 1179656 | tf_op jit(solution)/shard_map/ppermute | solution.py:419
  37.2 23.7 %collective-permute-start.9 = (bf16[4,96,512]{2,1,0:T(8,128)(2,1)}, bf16[4,96,512]{2,1,0:T(8,128)(2,1)}, u32[]{:S(2)}, u32[]{:S(2)}) collective-permute-start(bf16[4,96,512]{2,1,0:T(8,128)(2,1)} %all_to_all.16.refs_7_), channel_id=1, source_target_pairs={{0,8},{8,0},{16,24},{24,16},{32,40},{40,32},{48,56},{56,48},{64,72... | collective-permute-start | bytes 1179656 | tf_op jit(solution)/shard_map/ppermute | solution.py:390
  39.8 15.1 %collective-permute-start = (bf16[7,96,256]{2,1,0:T(8,128)(2,1)}, bf16[7,96,256]{2,1,0:T(8,128)(2,1)S(1)}, u32[]{:S(2)}, u32[]{:S(2)}) collective-permute-start(bf16[7,96,256]{2,1,0:T(8,128)(2,1)} %get-tuple-element.23), channel_id=1, source_target_pairs={{0,1},{1,0},{2,3},{3,2},{4,5},{5,4},{6,7},{7,6},{8,9},{9,8},{10,11... | collective-permute-start | bytes 1032200 | tf_op jit(solution)/shard_map/ppermute | solution.py:390
  40.4 17.9 %collective-permute-start.1 = (bf16[7,96,256]{2,1,0:T(8,128)(2,1)}, bf16[7,96,256]{2,1,0:T(8,128)(2,1)}, u32[]{:S(2)}, u32[]{:S(2)}) collective-permute-start(bf16[7,96,256]{2,1,0:T(8,128)(2,1)} %get-tuple-element.24), channel_id=1, source_target_pairs={{0,2},{1,3},{2,0},{3,1},{4,6},{5,7},{6,4},{7,5},{8,10},{9,11},{10,... | collective-permute-start | bytes 1032200 | tf_op jit(solution)/shard_map/ppermute | solution.py:390
  42.5 18.4 %collective-permute-start.2 = (bf16[7,96,256]{2,1,0:T(8,128)(2,1)}, bf16[7,96,256]{2,1,0:T(8,128)(2,1)}, u32[]{:S(2)}, u32[]{:S(2)}) collective-permute-start(bf16[7,96,256]{2,1,0:T(8,128)(2,1)} %get-tuple-element.25), channel_id=1, source_target_pairs={{0,3},{1,2},{2,1},{3,0},{4,7},{5,6},{6,5},{7,4},{8,11},{9,10},{10,... | collective-permute-start | bytes 1032200 | tf_op jit(solution)/shard_map/ppermute | solution.py:390
  44.5 10.4 %all-to-all-start.1 = ((f32[16,1,128]{2,1,0:T(1,128)}), f32[16,1,128]{2,1,0:T(1,128)S(1)}, u32[]{:S(2)}, u32[]{:S(2)}) async-start(f32[16,1,128]{2,1,0:T(1,128)} %bitcast.8), calls=%async_computation.1 | async-start | bytes 16384 | tf_op jit(solution)/shard_map/all_to_all | solution.py:394
  60.9 9.8 %copy-start.1 = (bf16[7,96,256]{2,1,0:T(8,128)(2,1)S(1)}, bf16[7,96,256]{2,1,0:T(8,128)(2,1)}, u32[]{:S(2)}) copy-start(bf16[7,96,256]{2,1,0:T(8,128)(2,1)} %get-tuple-element.22.refs_0_) | copy-start | bytes 1032196
  65.9 13.0 %collective-permute-start.14 = (bf16[4,96,256]{2,1,0:T(8,128)(2,1)S(1)}, bf16[4,96,256]{2,1,0:T(8,128)(2,1)S(1)}, u32[]{:S(2)}, u32[]{:S(2)}) collective-permute-start(bf16[4,96,256]{2,1,0:T(8,128)(2,1)S(1)} %get-tuple-element.38), channel_id=1, source_target_pairs={{0,1},{1,0},{2,3},{3,2},{4,5},{5,4},{6,7},{7,6},{8,9},{9,8},{10,11... | collective-permute-start | bytes 589832 | tf_op jit(solution)/shard_map/ppermute | solution.py:390
  66.0 14.0 %collective-permute-start.15 = (bf16[4,96,256]{2,1,0:T(8,128)(2,1)S(1)}, bf16[4,96,256]{2,1,0:T(8,128)(2,1)S(1)}, u32[]{:S(2)}, u32[]{:S(2)}) collective-permute-start(bf16[4,96,256]{2,1,0:T(8,128)(2,1)S(1)} %get-tuple-element.39), channel_id=1, source_target_pairs={{0,2},{1,3},{2,0},{3,1},{4,6},{5,7},{6,4},{7,5},{8,10},{9,11},{10,... | collective-permute-start | bytes 589832 | tf_op jit(solution)/shard_map/ppermute | solution.py:390
  69.5 12.0 %collective-permute-start.16 = (bf16[4,96,256]{2,1,0:T(8,128)(2,1)S(1)}, bf16[4,96,256]{2,1,0:T(8,128)(2,1)S(1)}, u32[]{:S(2)}, u32[]{:S(2)}) collective-permute-start(bf16[4,96,256]{2,1,0:T(8,128)(2,1)S(1)} %get-tuple-element.40), channel_id=1, source_target_pairs={{0,3},{1,2},{2,1},{3,0},{4,7},{5,6},{6,5},{7,4},{8,11},{9,10},{10,... | collective-permute-start | bytes 589832 | tf_op jit(solution)/shard_map/ppermute | solution.py:390
  75.3 7.2 %collective-permute-start.11 = (bf16[3,96,256]{2,1,0:T(8,128)(2,1)S(1)}, bf16[3,96,256]{2,1,0:T(8,128)(2,1)S(1)}, u32[]{:S(2)}, u32[]{:S(2)}) collective-permute-start(bf16[3,96,256]{2,1,0:T(8,128)(2,1)S(1)} %get-tuple-element.34), channel_id=1, source_target_pairs={{0,1},{1,0},{2,3},{3,2},{4,5},{5,4},{6,7},{7,6},{8,9},{9,8},{10,11... | collective-permute-start | bytes 442376 | tf_op jit(solution)/shard_map/ppermute | solution.py:390
  75.4 8.4 %collective-permute-start.12 = (bf16[3,96,256]{2,1,0:T(8,128)(2,1)S(1)}, bf16[3,96,256]{2,1,0:T(8,128)(2,1)S(1)}, u32[]{:S(2)}, u32[]{:S(2)}) collective-permute-start(bf16[3,96,256]{2,1,0:T(8,128)(2,1)S(1)} %get-tuple-element.35), channel_id=1, source_target_pairs={{0,2},{1,3},{2,0},{3,1},{4,6},{5,7},{6,4},{7,5},{8,10},{9,11},{10,... | collective-permute-start | bytes 442376 | tf_op jit(solution)/shard_map/ppermute | solution.py:390
  78.9 6.9 %collective-permute-start.13 = (bf16[3,96,256]{2,1,0:T(8,128)(2,1)S(1)}, bf16[3,96,256]{2,1,0:T(8,128)(2,1)S(1)}, u32[]{:S(2)}, u32[]{:S(2)}) collective-permute-start(bf16[3,96,256]{2,1,0:T(8,128)(2,1)S(1)} %get-tuple-element.36), channel_id=1, source_target_pairs={{0,3},{1,2},{2,1},{3,0},{4,7},{5,6},{6,5},{7,4},{8,11},{9,10},{10,... | collective-permute-start | bytes 442376 | tf_op jit(solution)/shard_map/ppermute | solution.py:390
  (5 other events, 22.8 us)

commit v5 on v4

--- a/solution.py
+++ b/solution.py
@@ -53,8 +53,8 @@
     return pl.multiple_of(jnp.bitwise_xor(me, s) * width, width)
 
 
-def pack_body(me, far_weights, ensemble, tiles, *rest):
-    *blocks, predicted, weights, buffer, arrived, left = rest
+def pack_body(me, far_weights, ensemble, far_tiles, *rest):
+    *blocks, predicted, weights, tiles, buffer, arrived, left = rest
     peers, var_count, _, width = buffer.shape
     starts = [tile_block(me[0], s, width) for s in range(peers)]
     loads = [
@@ -64,11 +64,14 @@
         for s in range(peers)
     ]
     stores = [pltpu.make_async_copy(buffer.at[s], blocks[s], left.at[s]) for s in range(peers)]
-    light = pltpu.make_async_copy(far_weights, weights, arrived.at[peers])
-    light.start()
-    for load in loads:
+    light = [
+        pltpu.make_async_copy(far_weights, weights, arrived.at[peers]),
+        pltpu.make_async_copy(far_tiles, tiles, arrived.at[peers + 1]),
+    ]
+    for load in light + loads:
         load.start()
-    light.wait()
+    for load in light:
+        load.wait()
     rows = lax.broadcasted_iota(jnp.int32, (width, tiles.shape[1]), 0)
     total = jnp.zeros(predicted.shape, F32)
     for s in range(peers):
@@ -93,35 +96,53 @@
     obs = tiles.shape[1]
     return pl.pallas_call(
         pack_body,
-        in_specs=[scalars(), anywhere(), anywhere(), whole()],
+        in_specs=[scalars()] + [anywhere()] * 3,
         out_specs=[anywhere()] * peers + [whole()],
         out_shape=[pltpu.HBM((var_count, own, width), BF16)] * peers + [shape_of((own, obs))],
         scratch_shapes=[
             pltpu.SMEM((var_count,), F32),
+            pltpu.VMEM((1, obs), jnp.int32),
             pltpu.VMEM((peers, var_count, own, width), BF16),
-            pltpu.SemaphoreType.DMA((peers + 1,)),
+            pltpu.SemaphoreType.DMA((peers + 2,)),
             pltpu.SemaphoreType.DMA((peers,)),
         ],
         compiler_params=params(),
         name="pack",
-    )(me, in_hbm(weights), in_hbm(ensemble), tiles)
+    )(me, in_hbm(weights), in_hbm(ensemble), in_hbm(tiles))
 
 
 def scale_body(noise, error, out):
-    scaled = (jnp.sqrt(error[...]) * noise[...]).astype(BF16)
-    for j in range(out.shape[0]):
-        out[j] = scaled
-
-
-def scale(noise, error, peers):
+    out[...] = (jnp.sqrt(error[...]) * noise[...]).astype(BF16)
+
+
+def scale(noise, error):
     return pl.pallas_call(
         scale_body,
         in_specs=[whole()] * 2,
         out_specs=whole(),
-        out_shape=shape_of((peers, *noise.shape)),
+        out_shape=shape_of(noise.shape),
         compiler_params=params(),
         name="scale",
     )(noise, error)
+
+
+def join_noise_body(*refs):
+    *parts, out = refs
+    own = parts[0].shape[0]
+    for s, part in enumerate(parts):
+        out[s * own : (s + 1) * own] = part[...]
+
+
+def join_noise(parts):
+    own, obs = parts[0].shape
+    return pl.pallas_call(
+        join_noise_body,
+        in_specs=[whole()] * len(parts),
+        out_specs=whole(),
+        out_shape=shape_of((len(parts) * own, obs)),
+        compiler_params=params(),
+        name="joinnoise",
+    )(*parts)
 
 
 def join_body(mine, other, out):
@@ -180,8 +201,8 @@
     )(me, values, error, tiles, *gathered)
 
 
-def scalar_rows(packet, members):
-    rows = packet[members:].astype(F32)
+def scalar_rows(rows):
+    rows = rows.astype(F32)
     innovation = rows[0:1] + rows[1:2] + rows[2:3]
     error = rows[3:4] + rows[4:5] + rows[5:6]
     spread = rows[6:7] + rows[7:8] + rows[8:9]
@@ -195,11 +216,11 @@
     means[...] = jnp.broadcast_to(mean, means.shape)
     for s, part in enumerate(parts):
         anomalies[s * own : (s + 1) * own] = (part - mean).astype(BF16)
-    obs = taper.shape[0]
-    step = obs // 3
-    for k in range(0, obs, step):
-        covariance = jnp.dot(anom_t[k : k + step], anomalies[...], preferred_element_type=F32)
-        gain[k : k + step] = (covariance * taper[k : k + step]).astype(BF16)
+    at = 0
+    for some_t, tapers in zip(anom_t, taper):
+        covariance = jnp.dot(some_t[...], anomalies[...], preferred_element_type=F32)
+        gain[at : at + tapers.shape[0]] = (covariance * tapers[...]).astype(BF16)
+        at += tapers.shape[0]
 
 
 def posterior(gain, means, anomalies, perturbed, root, blocks, at):
@@ -210,82 +231,135 @@
         block[at] = result[s * own : (s + 1) * own].astype(BF16)
 
 
+def tapers(scales, offset, side, width, members, tile_count):
+    tile = (offset[0] + lax.broadcasted_iota(jnp.int32, (1, width), 1)).astype(F32)
+    place = scalar_rows(scales)[3] + (offset[side] * tile_count).astype(F32)
+    column = jnp.broadcast_to(place, (8, place.shape[1])).T[:, 0:1]
+    near = jnp.maximum(0.0, 1.0 - jnp.abs(tile - column) / RADIUS)
+    return near * near / (members - 1)
+
+
 def prepare_body(offset, *refs, tile_count):
     *far_packets, anom_t, taper, packets, arrived = refs
     members = anom_t.shape[1]
     obs = packets.shape[2]
-    loads = [pltpu.make_async_copy(far_packets[n], packets.at[n], arrived.at[n]) for n in range(3)]
+    loads = [
+        pltpu.make_async_copy(packet, packets.at[n], arrived.at[n])
+        for n, packet in enumerate(far_packets)
+    ]
     for load in loads:
         load.start()
-    tile = (offset[0] + lax.broadcasted_iota(jnp.int32, (1, taper.shape[1]), 1)).astype(F32)
-    for n in range(3):
-        loads[n].wait()
-        packet = packets.at[n]
-        anom_t[n * obs : (n + 1) * obs] = packet[:members].T
-        place = scalar_rows(packet, members)[3] + (offset[1 + n] * tile_count).astype(F32)
-        column = jnp.broadcast_to(place, (8, obs)).T[:, 0:1]
-        near = jnp.maximum(0.0, 1.0 - jnp.abs(tile - column) / RADIUS)
-        taper[n * obs : (n + 1) * obs] = near * near / (members - 1)
+    for n, load in enumerate(loads):
+        load.wait()
+        rows = slice(n * obs, (n + 1) * obs)
+        anom_t[rows] = packets[n, :members].T
+        taper[rows] = tapers(packets[n, members:], offset, 1 + n, taper.shape[1], members, tile_count)
 
 
 def prepare(offset, packets, width, tile_count):
     rows, obs = packets[0].shape
     members = rows - 16
+    count = len(packets)
     return pl.pallas_call(
         functools.partial(prepare_body, tile_count=tile_count),
-        in_specs=[scalars()] + [anywhere()] * 3,
+        in_specs=[scalars()] + [anywhere()] * count,
         out_specs=[whole()] * 2,
-        out_shape=[shape_of((3 * obs, members)), shape_of((3 * obs, width), F32)],
-        scratch_shapes=[pltpu.VMEM((3, rows, obs), BF16), pltpu.SemaphoreType.DMA((3,))],
+        out_shape=[shape_of((count * obs, members)), shape_of((count * obs, width), F32)],
+        scratch_shapes=[
+            pltpu.VMEM((count, rows, obs), BF16),
+            pltpu.SemaphoreType.DMA((count,)),
+        ],
         compiler_params=params(),
         name="prepare",
     )(offset, *map(in_hbm, packets))
 
 
-def first_body(me, *refs, peers):
+def start_body(offset, *refs, peers, tile_count):
     far_states, far_packets = refs[:peers], refs[peers : peers + 3]
-    far_noises, (sums, anom_t, taper) = refs[peers + 3 : peers + 6], refs[peers + 6 : peers + 9]
-    refs = refs[peers + 9 :]
-    blocks, (perturbed, root_out, inflation_out) = refs[:peers], refs[peers : peers + 3]
-    states, packets, noises, means, anomalies, gain, arrived = refs[peers + 3 :]
-    count, own, _ = blocks[0].shape
-    members = peers * own
-    obs = packets.shape[2]
+    anom_0, taper_0, anom_2, taper_2, means, anomalies, gain, packets, rest = refs[peers + 3 : peers + 12]
+    states, arrived, near, passed = refs[peers + 12 :]
+    members, width = anomalies.shape[1:]
+    count = gain.shape[0]
     loads = [
         pltpu.make_async_copy(far_states[s].at[:count], states.at[s], arrived.at[s])
         for s in range(peers)
     ]
     late = [
-        pltpu.make_async_copy(source[n], target.at[n], arrived.at[peers + 3 * i + n])
-        for i, (source, target) in enumerate(((far_packets, packets), (far_noises, noises)))
-        for n in range(3)
-    ]
-    for load in loads + late:
+        pltpu.make_async_copy(far_packets[n], packets.at[n], near.at[n]) for n in range(3)
+    ]
+    onward = [
+        pltpu.make_async_copy(far_states[s].at[count:], rest.at[s], passed.at[s])
+        for s in range(peers)
+    ]
+    for load in [late[2], *loads, late[0], late[1], *onward]:
         load.start()
+    late[2].wait()
+    anom_2[...] = packets[2, :members].T
+    taper_2[...] = tapers(packets[2, members:], offset, 3, width, members, tile_count)
     for load in loads:
         load.wait()
     for l in range(count):
         state = [states[s, l] for s in range(peers)]
-        gains(state, anom_t, taper, means.at[l], anomalies.at[l], gain.at[l])
-    for load in late:
+        gains(
+            state, (anom_0, anom_2), (taper_0, taper_2), means.at[l], anomalies.at[l], gain.at[l]
+        )
+    for load in [late[0], late[1], *onward]:
         load.wait()
+
+
+def start_gains(offset, states, packets, anom_0, taper_0, count, tile_count):
+    var_count, own, width = states[0].shape
+    peers = len(states)
+    members = own * peers
+    rows, obs = packets[0].shape
+    return pl.pallas_call(
+        functools.partial(start_body, peers=peers, tile_count=tile_count),
+        in_specs=[scalars()] + [anywhere()] * (peers + 3) + [whole()] * 2,
+        out_specs=[whole()] * 7,
+        out_shape=[
+            shape_of((obs, members)),
+            shape_of((obs, width), F32),
+            shape_of((count, 8, width), F32),
+            shape_of((count, members, width)),
+            shape_of((count, 3 * obs, width)),
+            shape_of((3, rows, obs)),
+            shape_of((peers, var_count - count, own, width)),
+        ],
+        scratch_shapes=[
+            pltpu.VMEM((peers, count, own, width), BF16),
+            pltpu.SemaphoreType.DMA((peers,)),
+            pltpu.SemaphoreType.DMA((3,)),
+            pltpu.SemaphoreType.DMA((peers,)),
+        ],
+        compiler_params=params(8),
+        name="start",
+    )(
+        offset,
+        in_hbm(states[0]),
+        *states[1:],
+        *map(in_hbm, packets),
+        *in_vmem((anom_0, taper_0)),
+    )
+
+
+def first_body(means, anomalies, gain, packets, sums, *refs):
+    noises, (*blocks, perturbed, root_out, inflation_out) = refs[:3], refs[3:]
+    members = anomalies.shape[1]
+    obs = packets.shape[2]
     folded = jnp.sum(sums[...], axis=0, keepdims=True)
     inflation = folded[:, 0:1] / folded[:, 1:2]
     inflation_out[0] = jnp.sum(inflation)
     root = jnp.sqrt(inflation)
     root_out[...] = jnp.broadcast_to(root, root_out.shape)
     for n in range(3):
-        innovation, error, spread, _ = scalar_rows(packets.at[n], members)
+        innovation, error, spread, _ = scalar_rows(packets[n, members:])
         bottom = jnp.where(error > 0.0, inflation * spread + error, 1.0)
         factor = jnp.where(error > 0.0, inflation / bottom, 0.0)
-        for s in range(peers):
-            rows = slice(s * own, (s + 1) * own)
-            noise = noises[n, jnp.bitwise_xor(me[0], s)].astype(F32)
-            dev = packets[n, rows].astype(F32)
-            perturbed[rows, n * obs : (n + 1) * obs] = (
-                factor * (innovation + noise - root * dev)
-            ).astype(BF16)
-    for l in range(count):
+        dev = packets[n, :members].astype(F32)
+        perturbed[:, n * obs : (n + 1) * obs] = (
+            factor * (innovation + noises[n][...].astype(F32) - root * dev)
+        ).astype(BF16)
+    for l in range(gain.shape[0]):
         posterior(gain.at[l], means.at[l], anomalies.at[l], perturbed, root, blocks, l)
 
 
@@ -297,60 +371,47 @@
     ]
 
 
-def first_updates(me, states, packets, noises, sums, anom_t, taper, count):
-    _, own, width = states[0].shape
-    peers = len(states)
-    members = own * peers
-    rows, obs = packets[0].shape
+def first_updates(means, anomalies, gain, packets, sums, noises, peers):
+    count, members, width = anomalies.shape
+    obs = packets.shape[2]
     out = pl.pallas_call(
-        functools.partial(first_body, peers=peers),
-        in_specs=[scalars()] + [anywhere()] * (peers + 6) + [whole()] * 3,
+        first_body,
+        in_specs=[whole()] * 8,
         out_specs=[whole()] * (peers + 2) + [scalars()],
-        out_shape=[shape_of((count, own, width))] * peers
+        out_shape=[shape_of((count, members // peers, width))] * peers
         + [
             shape_of((members, 3 * obs)),
             shape_of((8, 128), F32),
             jax.ShapeDtypeStruct((1,), F32),
         ],
-        scratch_shapes=[
-            pltpu.VMEM((peers, count, own, width), BF16),
-            pltpu.VMEM((3, rows, obs), BF16),
-            pltpu.VMEM((3, peers, own, obs), BF16),
-            *working(count, members, 3 * obs, width),
-            pltpu.SemaphoreType.DMA((peers + 6,)),
-        ],
-        compiler_params=params(16),
+        compiler_params=params(4),
         name="first",
-    )(me, *map(in_hbm, (*states, *packets, *noises)), *in_vmem((sums, anom_t, taper)))
-    return out[:peers], out[peers], out[peers + 1], out[peers + 2]
-
-
-def second_body(*refs, first, peers):
-    states, (anom_t, perturbed, taper, root) = refs[:peers], refs[peers : peers + 4]
-    blocks = refs[peers + 4 : 2 * peers + 4]
-    means, anomalies, gain = refs[2 * peers + 4 :]
+    )(*in_vmem((means, anomalies, gain, packets, sums, *noises)))
+    return out[:peers], *out[peers:]
+
+
+def second_body(states, perturbed, root, *refs):
+    shared, (*blocks, means, anomalies, gain) = refs[:4], refs[4:]
+    peers = len(blocks)
     count = blocks[0].shape[0]
     for l in range(count):
-        state = [states[s][first + l] for s in range(peers)]
-        gains(state, anom_t, taper, means.at[l], anomalies.at[l], gain.at[l])
+        state = [states[s, l] for s in range(peers)]
+        gains(state, shared[:2], shared[2:], means.at[l], anomalies.at[l], gain.at[l])
     for l in range(count):
         posterior(gain.at[l], means.at[l], anomalies.at[l], perturbed, root[0:1, 0:1], blocks, l)
 
 
-def second_updates(states, anom_t, perturbed, taper, root, first):
-    var_count, own, width = states[0].shape
-    peers = len(states)
-    members = own * peers
-    count = var_count - first
-    return pl.pallas_call(
-        functools.partial(second_body, first=first, peers=peers),
-        in_specs=[whole()] * (peers + 4),
+def second_updates(states, perturbed, root, shared):
+    peers, count, own, width = states.shape
+    return pl.pallas_call(
+        second_body,
+        in_specs=[whole()] * 7,
         out_specs=[whole()] * peers,
         out_shape=[shape_of((count, own, width))] * peers,
-        scratch_shapes=working(count, members, anom_t.shape[0], width),
+        scratch_shapes=working(count, peers * own, perturbed.shape[1], width),
         compiler_params=params(),
         name="second",
-    )(*in_vmem((*states, anom_t, perturbed, taper, root)))
+    )(*in_vmem((states, perturbed, root, *shared)))
 
 
 def place_body(me, *refs, first, peers):
@@ -411,27 +472,31 @@
     tiles, values, error = (a[None, :] for a in (obs_tiles, obs_values, obs_error))
     *blocks, partial = pack(me, ensemble, obs_weights, tiles, peers)
     other = swapped(partial, "depth", 1)
-    noise = exchanged(scale(obs_noise, error, peers), "member")
+    noises = traded([scale(obs_noise, error)] * peers, (1, 3, 2))
     predicted = traded([join(partial, other)] * peers, (1, 3, 2))
     pairs = [(i, i + 1) for i in range(1, regions - 1, 2)]
     pairs += [(j, i) for i, j in pairs]
-    near_noise = swapped(noise, "region", 1)
-    far_noise = lax.ppermute(noise, "region", pairs)
     packet, sums = stats(me, predicted, values, error, tiles, regions)
     near = swapped(packet, "region", 1)
     far = lax.ppermute(packet, "region", pairs)
     states = traded(blocks, (1, 3, 2))
     all_sums = exchanged(sums, "region")
+    noise = join_noise(noises)
+    near_noise = swapped(noise, "region", 1)
+    far_noise = lax.ppermute(noise, "region", pairs)
     side = 1 - 2 * (region % 2)
     offset = jnp.stack([me[0] * width, jnp.zeros_like(side), side, -side])
-    packets = (packet, near, far)
-    anom_t, taper = prepare(offset, packets, width, tile_count)
+    anom_0, taper_0 = prepare(offset, (packet, near), width, tile_count)
     half = (var_count + 1) // 2
+    anom_2, taper_2, means, anomalies, gain, packets, rest = start_gains(
+        offset, states, (packet, near, far), anom_0, taper_0, half, tile_count
+    )
     ready, perturbed, root, inflation = first_updates(
-        me, states, packets, (noise, near_noise, far_noise), all_sums, anom_t, taper, half
+        means, anomalies, gain, packets, all_sums, (noise, near_noise, far_noise), peers
     )
+    shared = (anom_0, anom_2, taper_0, taper_2)
     early = traded(ready, (1, 3, 2))
-    ready = second_updates(states, anom_t, perturbed, taper, root, half)
+    ready = second_updates(rest, perturbed, root, shared)
     late = traded(ready, (1, 3, 2))
     output = place(me, early, 0, var_count)
     output = place(me, late, half, var_count, output)

time: 87 us -> 103 us (1.18)
  the two profiles are of different devices: /device:TPU:0 before, /device:TPU:96 now
where the time goes in v5:
time: 103 us; the launch traced here: 102 us
  starting transfers between devices  36.2 us (35%)
  waiting for transfers between devices  34.4 us (33%)
  Pallas kernels  17.2 us (17%)
  local copies, waits for them, and re-layouts  12.6 us (12%)
  between operations  1.04 us (1%)
    ppermute x18, waiting for transfers between devices, swapped(): return lax.ppermute(value, axis, pairs)  34.4 us
    ppermute x18, starting transfers between devices, swapped(): return lax.ppermute(value, axis, pairs)  25.4 us
    unnamed x40, local copies, waits for them, and re-layouts  12.6 us
    all_to_all x1, starting transfers between devices, exchanged(): return lax.all_to_all(blocks, axis, split_axis=0, concat_axis=0, tiled=True)  5.54 us
    pallas_call x1, Pallas kernels, start_gains(): pl.pallas_call(functools.partial(start_body, peers=peers, tile_count=tile...  4.4 us
    ppermute x1, starting transfers between devices, shards(): far_noise = lax.ppermute(noise, 'region', pairs)  3.35 us
    pallas_call x1, Pallas kernels, first_updates(): pl.pallas_call(first_body, in_specs=[whole()] * 8, out_specs=[whole()] *...  2.82 us
    pallas_call x1, Pallas kernels, pack(): pl.pallas_call(pack_body, in_specs=[scalars()] + [anywhere()] * 3, out_sp...  2.52 us
  transfers between devices with their start and end apart: 21, of which 10 were waited for; matrix products, arithmetic and copies ran while one was open for 0% of the time, Pallas kernels for 10%

profile of v5, /device:TPU:96, one launch (start us, length us, event | category | flops | bytes accessed | tf_op | source)
XLA Modules:
  0.0 101.5 jit_solution(3924357910720014231)
XLA Ops:
  0.7 2.5 %pack.1 = (bf16[7,96,256]{2,1,0:T(8,128)(2,1)}, bf16[7,96,256]{2,1,0:T(8,128)(2,1)}, bf16[7,96,256]{2,1,0:T(8,128)(2,1)}, bf16[7,96,256]{2,1,0:T(8,128)(2,1)}, bf16[96,512]{1,0:T(8,128)(2,1)S(1)}) custom-call(s32[1]{0:T(128)} %bitcast.me, f32[7]{0:T(128)} %far_weights.1, bf16[7,96,1024]{2,1,0:T(8,128)(2,1)} %ensemble.1, s32[1,512]{1,0:T(1,128)} %bitcast.13), custom_call_target="tpu_custom_call" | custom-call | tf_op jit(solution)/shard_map/pack/pallas_call | solution.py:97
  3.2 3.3 %collective-permute-start.3 = (bf16[96,512]{1,0:T(8,128)(2,1)S(1)}, bf16[96,512]{1,0:T(8,128)(2,1)S(1)}, u32[]{:S(2)}, u32[]{:S(2)}) collective-permute-start(bf16[96,512]{1,0:T(8,128)(2,1)S(1)} %get-tuple-element.33.mine), channel_id=1, source_target_pairs={{0,4},{4,0},{1,5},{5,1},{2,6},{6,2},{3,7},{7,3},{8,12},{12,8},{9,1... | collective-permute-start | bytes 294920 | tf_op jit(solution)/shard_map/ppermute | solution.py:451
  6.5 2.9 %collective-permute-done.3.other = bf16[96,512]{1,0:T(8,128)(2,1)S(1)} collective-permute-done((bf16[96,512]{1,0:T(8,128)(2,1)S(1)}, bf16[96,512]{1,0:T(8,128)(2,1)S(1)}, u32[]{:S(2)}, u32[]{:S(2)}) %collective-permute-start.3) | collective-permute-done | bytes 98336 | tf_op jit(solution)/shard_map/ppermute | solution.py:451
  11.0 2.7 %collective-permute-start.5 = (bf16[96,512]{1,0:T(8,128)(2,1)S(1)}, bf16[96,512]{1,0:T(8,128)(2,1)S(1)}, u32[]{:S(2)}, u32[]{:S(2)}) collective-permute-start(bf16[96,512]{1,0:T(8,128)(2,1)S(1)} %join.1.refs_0_), channel_id=1, source_target_pairs={{0,2},{1,3},{2,0},{3,1},{4,6},{5,7},{6,4},{7,5},{8,10},{9,11},{10,... | collective-permute-start | bytes 294920 | tf_op jit(solution)/shard_map/ppermute | solution.py:451
  15.0 2.4 %collective-permute-done.5.refs_2_ = bf16[96,512]{1,0:T(8,128)(2,1)S(1)} collective-permute-done((bf16[96,512]{1,0:T(8,128)(2,1)S(1)}, bf16[96,512]{1,0:T(8,128)(2,1)S(1)}, u32[]{:S(2)}, u32[]{:S(2)}) %collective-permute-start.5) | collective-permute-done | bytes 98336 | tf_op jit(solution)/shard_map/ppermute | solution.py:451
  17.5 2.1 %collective-permute-done.6.refs_3_ = bf16[96,512]{1,0:T(8,128)(2,1)S(1)} collective-permute-done((bf16[96,512]{1,0:T(8,128)(2,1)S(1)}, bf16[96,512]{1,0:T(8,128)(2,1)S(1)}, u32[]{:S(2)}, u32[]{:S(2)}) %collective-permute-start.6) | collective-permute-done | bytes 98336 | tf_op jit(solution)/shard_map/ppermute | solution.py:451
  20.6 2.2 %collective-permute-start.10 = (bf16[96,512]{1,0:T(8,128)(2,1)S(1)}, bf16[96,512]{1,0:T(8,128)(2,1)S(1)}, u32[]{:S(2)}, u32[]{:S(2)}) collective-permute-start(bf16[96,512]{1,0:T(8,128)(2,1)S(1)} %scale.1.refs_0_), channel_id=1, source_target_pairs={{0,2},{1,3},{2,0},{3,1},{4,6},{5,7},{6,4},{7,5},{8,10},{9,11},{10,... | collective-permute-start | bytes 294920 | tf_op jit(solution)/shard_map/ppermute | solution.py:451
  22.8 2.5 %collective-permute-start.11 = (bf16[96,512]{1,0:T(8,128)(2,1)S(1)}, bf16[96,512]{1,0:T(8,128)(2,1)S(1)}, u32[]{:S(2)}, u32[]{:S(2)}) collective-permute-start(bf16[96,512]{1,0:T(8,128)(2,1)S(1)} %scale.1.refs_0_), channel_id=1, source_target_pairs={{0,3},{1,2},{2,1},{3,0},{4,7},{5,6},{6,5},{7,4},{8,11},{9,10},{10,... | collective-permute-start | bytes 294920 | tf_op jit(solution)/shard_map/ppermute | solution.py:451
  25.3 8.6 %collective-permute-done.10.refs_2_ = bf16[96,512]{1,0:T(8,128)(2,1)S(1)} collective-permute-done((bf16[96,512]{1,0:T(8,128)(2,1)S(1)}, bf16[96,512]{1,0:T(8,128)(2,1)S(1)}, u32[]{:S(2)}, u32[]{:S(2)}) %collective-permute-start.10) | collective-permute-done | bytes 98336 | tf_op jit(solution)/shard_map/ppermute | solution.py:451
  33.9 1.9 %collective-permute-start.8 = (bf16[400,512]{1,0:T(8,128)(2,1)S(1)}, bf16[400,512]{1,0:T(8,128)(2,1)}, u32[]{:S(2)}, u32[]{:S(2)}) collective-permute-start(bf16[400,512]{1,0:T(8,128)(2,1)S(1)} %get-tuple-element.34.refs_0_.refs_4_), channel_id=1, source_target_pairs={{8,16},{24,32},{40,48},{56,64},{72,80},{88,96},{104,112},{16,8},{3... | collective-permute-start | bytes 1228808 | tf_op jit(solution)/shard_map/ppermute | solution.py:481
  36.3 3.3 %collective-permute-start.13 = (bf16[384,512]{1,0:T(8,128)(2,1)S(1)}, bf16[384,512]{1,0:T(8,128)(2,1)}, u32[]{:S(2)}, u32[]{:S(2)}) collective-permute-start(bf16[384,512]{1,0:T(8,128)(2,1)S(1)} %joinnoise.1.refs_0_), channel_id=1, source_target_pairs={{8,16},{24,32},{40,48},{56,64},{72,80},{88,96},{104,112},{16,8},{3... | collective-permute-start | bytes 1179656 | tf_op jit(solution)/shard_map/ppermute | solution.py:486
  43.0 5.5 %all-to-all-start = ((f32[16,1,128]{2,1,0:T(1,128)}), f32[16,1,128]{2,1,0:T(1,128)S(1)}, u32[]{:S(2)}, u32[]{:S(2)}) async-start(f32[16,1,128]{2,1,0:T(1,128)} %bitcast.8), calls=%async_computation | async-start | bytes 16384 | tf_op jit(solution)/shard_map/all_to_all | solution.py:455
  48.7 2.4 %prepare.1 = (bf16[1024,384]{1,0:T(8,128)(2,1)S(1)}, f32[1024,256]{1,0:T(8,128)S(1)}) custom-call(s32[4]{0:T(128)S(1)} %pad_add_fusion.offset, bf16[400,512]{1,0:T(8,128)(2,1)} %copy-done.2, bf16[400,512]{1,0:T(8,128)(2,1)} %copy-done.19), custom_call_target="tpu_custom_call" | custom-call | tf_op jit(solution)/shard_map/prepare/pallas_call | solution.py:263
  51.0 1.8 %collective-permute-done.1.refs_2_ = bf16[7,96,256]{2,1,0:T(8,128)(2,1)S(1)} collective-permute-done((bf16[7,96,256]{2,1,0:T(8,128)(2,1)}, bf16[7,96,256]{2,1,0:T(8,128)(2,1)S(1)}, u32[]{:S(2)}, u32[]{:S(2)}) %collective-permute-start.1) | collective-permute-done | bytes 344096 | tf_op jit(solution)/shard_map/ppermute | solution.py:451
  53.6 6.8 %collective-permute-done.2.refs_3_ = bf16[7,96,256]{2,1,0:T(8,128)(2,1)S(1)} collective-permute-done((bf16[7,96,256]{2,1,0:T(8,128)(2,1)}, bf16[7,96,256]{2,1,0:T(8,128)(2,1)S(1)}, u32[]{:S(2)}, u32[]{:S(2)}) %collective-permute-start.2) | collective-permute-done | bytes 344096 | tf_op jit(solution)/shard_map/ppermute | solution.py:451
  64.0 4.4 %start.1 = (bf16[512,384]{1,0:T(8,128)(2,1)S(1)}, f32[512,256]{1,0:T(8,128)S(1)}, f32[4,8,256]{2,1,0:T(8,128)S(1)}, bf16[4,384,256]{2,1,0:T(8,128)(2,1)S(1)}, bf...) custom-call(s32[4]{0:T(128)S(1)} %pad_add_fusion.offset, ...), custom_call_target="tpu_custom_call" | custom-call | tf_op jit(solution)/shard_map/start/pallas_call | solution.py:315
  68.5 1.6 %copy-done = bf16[4,1536,256]{2,1,0:T(8,128)(2,1)} copy-done((bf16[4,1536,256]{2,1,0:T(8,128)(2,1)}, bf16[4,1536,256]{2,1,0:T(8,128)(2,1)S(1)}, u32[]{:S(2)}) %copy-start) | copy-done | bytes 3145752
  72.7 1.9 %copy-done.1 = bf16[4,1536,256]{2,1,0:T(8,128)(2,1)S(1)} copy-done((bf16[4,1536,256]{2,1,0:T(8,128)(2,1)S(1)}, bf16[4,1536,256]{2,1,0:T(8,128)(2,1)}, u32[]{:S(2)}) %copy-start.1) | copy-done | bytes 3145752
  75.9 2.8 %first.1 = (bf16[4,96,256]{2,1,0:T(8,128)(2,1)S(1)}, bf16[4,96,256]{2,1,0:T(8,128)(2,1)S(1)}, bf16[4,96,256]{2,1,0:T(8,128)(2,1)S(1)}, bf16[4,96,256]{2,1,0:T(8,...) custom-call(f32[4,8,256]{2,1,0:T(8,128)S(1)} %get-tuple-element.38.means, ...), custom_call_target="tpu_custom_call" | custom-call | tf_op jit(solution)/shard_map/first/pallas_call | solution.py:377
  78.8 3.6 %collective-permute-start.18 = (bf16[4,96,256]{2,1,0:T(8,128)(2,1)S(1)}, bf16[4,96,256]{2,1,0:T(8,128)(2,1)S(1)}, u32[]{:S(2)}, u32[]{:S(2)}) collective-permute-start(bf16[4,96,256]{2,1,0:T(8,128)(2,1)S(1)} %get-tuple-element.53), channel_id=1, source_target_pairs={{0,2},{1,3},{2,0},{3,1},{4,6},{5,7},{6,4},{7,5},{8,10},{9,11},{10,... | collective-permute-start | bytes 589832 | tf_op jit(solution)/shard_map/ppermute | solution.py:451
  83.5 2.4 %second.1 = (bf16[3,96,256]{2,1,0:T(8,128)(2,1)S(1)}, bf16[3,96,256]{2,1,0:T(8,128)(2,1)S(1)}, bf16[3,96,256]{2,1,0:T(8,128)(2,1)S(1)}, bf16[3,96,256]{2,1,0:T(8,128)(2,1)S(1)}) custom-call(bf16[4,3,96,256]{3,2,1,0:T(8,128)(2,1)S(1)} %copy-done.6, bf16[384,1536]{1,0:T(8,128)(2,1)S(1)} %get-tuple-element.43.perturbed, f32[8,128]{1,0:T(8,128)S(1)} %get-tuple-element.44.root, ...), custom_call_target="tpu_custom_call" | custom-call | tf_op jit(solution)/shard_map/second/pallas_call | solution.py:406
  86.0 3.6 %collective-permute-start.15 = (bf16[3,96,256]{2,1,0:T(8,128)(2,1)S(1)}, bf16[3,96,256]{2,1,0:T(8,128)(2,1)S(1)}, u32[]{:S(2)}, u32[]{:S(2)}) collective-permute-start(bf16[3,96,256]{2,1,0:T(8,128)(2,1)S(1)} %get-tuple-element.49), channel_id=1, source_target_pairs={{0,2},{1,3},{2,0},{3,1},{4,6},{5,7},{6,4},{7,5},{8,10},{9,11},{10,... | collective-permute-start | bytes 442376 | tf_op jit(solution)/shard_map/ppermute | solution.py:451
  90.7 1.7 %collective-permute-done.18.refs_2_ = bf16[4,96,256]{2,1,0:T(8,128)(2,1)S(1)} collective-permute-done((bf16[4,96,256]{2,1,0:T(8,128)(2,1)S(1)}, bf16[4,96,256]{2,1,0:T(8,128)(2,1)S(1)}, u32[]{:S(2)}, u32[]{:S(2)}) %collective-permute-start.18) | collective-permute-done | bytes 196640 | tf_op jit(solution)/shard_map/ppermute | solution.py:451
  92.4 6.0 %collective-permute-done.19.refs_3_ = bf16[4,96,256]{2,1,0:T(8,128)(2,1)S(1)} collective-permute-done((bf16[4,96,256]{2,1,0:T(8,128)(2,1)S(1)}, bf16[4,96,256]{2,1,0:T(8,128)(2,1)S(1)}, u32[]{:S(2)}, u32[]{:S(2)}) %collective-permute-start.19) | collective-permute-done | bytes 196640 | tf_op jit(solution)/shard_map/ppermute | solution.py:451
  (70 shorter events, 21.4 us)
Async XLA Ops:
  0.6 18.9 %copy-start.16 = (s32[512]{0:T(512)S(1)}, s32[512]{0:T(512)}, u32[]{:S(2)}) copy-start(s32[512]{0:T(512)} %param.8) | copy-start | bytes 6148
  0.7 19.9 %copy-start.15 = (f32[96,512]{1,0:T(8,128)S(1)}, f32[96,512]{1,0:T(8,128)}, u32[]{:S(2)}) copy-start(f32[96,512]{1,0:T(8,128)} %noise.1) | copy-start | bytes 589828
  3.2 6.2 %collective-permute-start.3 = (bf16[96,512]{1,0:T(8,128)(2,1)S(1)}, bf16[96,512]{1,0:T(8,128)(2,1)S(1)}, u32[]{:S(2)}, u32[]{:S(2)}) collective-permute-start(bf16[96,512]{1,0:T(8,128)(2,1)S(1)} %get-tuple-element.33.mine), channel_id=1, source_target_pairs={{0,4},{4,0},{1,5},{5,1},{2,6},{6,2},{3,7},{7,3},{8,12},{12,8},{9,1... | collective-permute-start | bytes 294920 | tf_op jit(solution)/shard_map/ppermute | solution.py:451
  9.4 5.6 %collective-permute-start.4 = (bf16[96,512]{1,0:T(8,128)(2,1)S(1)}, bf16[96,512]{1,0:T(8,128)(2,1)S(1)}, u32[]{:S(2)}, u32[]{:S(2)}) collective-permute-start(bf16[96,512]{1,0:T(8,128)(2,1)S(1)} %join.1.refs_0_), channel_id=1, source_target_pairs={{0,1},{1,0},{2,3},{3,2},{4,5},{5,4},{6,7},{7,6},{8,9},{9,8},{10,11... | collective-permute-start | bytes 294920 | tf_op jit(solution)/shard_map/ppermute | solution.py:451
  11.0 6.5 %collective-permute-start.5 = (bf16[96,512]{1,0:T(8,128)(2,1)S(1)}, bf16[96,512]{1,0:T(8,128)(2,1)S(1)}, u32[]{:S(2)}, u32[]{:S(2)}) collective-permute-start(bf16[96,512]{1,0:T(8,128)(2,1)S(1)} %join.1.refs_0_), channel_id=1, source_target_pairs={{0,2},{1,3},{2,0},{3,1},{4,6},{5,7},{6,4},{7,5},{8,10},{9,11},{10,... | collective-permute-start | bytes 294920 | tf_op jit(solution)/shard_map/ppermute | solution.py:451
  13.7 5.8 %collective-permute-start.6 = (bf16[96,512]{1,0:T(8,128)(2,1)S(1)}, bf16[96,512]{1,0:T(8,128)(2,1)S(1)}, u32[]{:S(2)}, u32[]{:S(2)}) collective-permute-start(bf16[96,512]{1,0:T(8,128)(2,1)S(1)} %join.1.refs_0_), channel_id=1, source_target_pairs={{0,3},{1,2},{2,1},{3,0},{4,7},{5,6},{6,5},{7,4},{8,11},{9,10},{10,... | collective-permute-start | bytes 294920 | tf_op jit(solution)/shard_map/ppermute | solution.py:451
  20.5 28.2 %copy-start.2 = (bf16[400,512]{1,0:T(8,128)(2,1)}, bf16[400,512]{1,0:T(8,128)(2,1)S(1)}, u32[]{:S(2)}) copy-start(bf16[400,512]{1,0:T(8,128)(2,1)S(1)} %get-tuple-element.34.refs_0_.refs_4_) | copy-start | bytes 1228804
  20.5 21.2 %collective-permute-start.7 = (bf16[400,512]{1,0:T(8,128)(2,1)S(1)}, bf16[400,512]{1,0:T(8,128)(2,1)S(1)}, u32[]{:S(2)}, u32[]{:S(2)}) collective-permute-start(bf16[400,512]{1,0:T(8,128)(2,1)S(1)} %get-tuple-element.34.refs_0_.refs_4_), channel_id=1, source_target_pairs={{0,8},{8,0},{16,24},{24,16},{32,40},{40,32},{48,56},{56,48},{64,72... | collective-permute-start | bytes 1228808 | tf_op jit(solution)/shard_map/ppermute | solution.py:451
  20.5 19.1 %collective-permute-start = (bf16[7,96,256]{2,1,0:T(8,128)(2,1)}, bf16[7,96,256]{2,1,0:T(8,128)(2,1)S(1)}, u32[]{:S(2)}, u32[]{:S(2)}) collective-permute-start(bf16[7,96,256]{2,1,0:T(8,128)(2,1)} %get-tuple-element.30), channel_id=1, source_target_pairs={{0,1},{1,0},{2,3},{3,2},{4,5},{5,4},{6,7},{7,6},{8,9},{9,8},{10,11... | collective-permute-start | bytes 1032200 | tf_op jit(solution)/shard_map/ppermute | solution.py:451
  20.6 13.4 %collective-permute-start.10 = (bf16[96,512]{1,0:T(8,128)(2,1)S(1)}, bf16[96,512]{1,0:T(8,128)(2,1)S(1)}, u32[]{:S(2)}, u32[]{:S(2)}) collective-permute-start(bf16[96,512]{1,0:T(8,128)(2,1)S(1)} %scale.1.refs_0_), channel_id=1, source_target_pairs={{0,2},{1,3},{2,0},{3,1},{4,6},{5,7},{6,4},{7,5},{8,10},{9,11},{10,... | collective-permute-start | bytes 294920 | tf_op jit(solution)/shard_map/ppermute | solution.py:451
  22.8 13.0 %collective-permute-start.11 = (bf16[96,512]{1,0:T(8,128)(2,1)S(1)}, bf16[96,512]{1,0:T(8,128)(2,1)S(1)}, u32[]{:S(2)}, u32[]{:S(2)}) collective-permute-start(bf16[96,512]{1,0:T(8,128)(2,1)S(1)} %scale.1.refs_0_), channel_id=1, source_target_pairs={{0,3},{1,2},{2,1},{3,0},{4,7},{5,6},{6,5},{7,4},{8,11},{9,10},{10,... | collective-permute-start | bytes 294920 | tf_op jit(solution)/shard_map/ppermute | solution.py:451
  25.3 10.5 %collective-permute-start.9 = (bf16[96,512]{1,0:T(8,128)(2,1)S(1)}, bf16[96,512]{1,0:T(8,128)(2,1)S(1)}, u32[]{:S(2)}, u32[]{:S(2)}) collective-permute-start(bf16[96,512]{1,0:T(8,128)(2,1)S(1)} %scale.1.refs_0_), channel_id=1, source_target_pairs={{0,1},{1,0},{2,3},{3,2},{4,5},{5,4},{6,7},{7,6},{8,9},{9,8},{10,11... | collective-permute-start | bytes 294920 | tf_op jit(solution)/shard_map/ppermute | solution.py:451
  33.9 27.2 %collective-permute-start.8 = (bf16[400,512]{1,0:T(8,128)(2,1)S(1)}, bf16[400,512]{1,0:T(8,128)(2,1)}, u32[]{:S(2)}, u32[]{:S(2)}) collective-permute-start(bf16[400,512]{1,0:T(8,128)(2,1)S(1)} %get-tuple-element.34.refs_0_.refs_4_), channel_id=1, source_target_pairs={{8,16},{24,32},{40,48},{56,64},{72,80},{88,96},{104,112},{16,8},{3... | collective-permute-start | bytes 1228808 | tf_op jit(solution)/shard_map/ppermute | solution.py:481
  35.9 36.8 %collective-permute-start.12 = (bf16[384,512]{1,0:T(8,128)(2,1)S(1)}, bf16[384,512]{1,0:T(8,128)(2,1)}, u32[]{:S(2)}, u32[]{:S(2)}) collective-permute-start(bf16[384,512]{1,0:T(8,128)(2,1)S(1)} %joinnoise.1.refs_0_), channel_id=1, source_target_pairs={{0,8},{8,0},{16,24},{24,16},{32,40},{40,32},{48,56},{56,48},{64,72... | collective-permute-start | bytes 1179656 | tf_op jit(solution)/shard_map/ppermute | solution.py:451
  36.3 36.4 %collective-permute-start.13 = (bf16[384,512]{1,0:T(8,128)(2,1)S(1)}, bf16[384,512]{1,0:T(8,128)(2,1)}, u32[]{:S(2)}, u32[]{:S(2)}) collective-permute-start(bf16[384,512]{1,0:T(8,128)(2,1)S(1)} %joinnoise.1.refs_0_), channel_id=1, source_target_pairs={{8,16},{24,32},{40,48},{56,64},{72,80},{88,96},{104,112},{16,8},{3... | collective-permute-start | bytes 1179656 | tf_op jit(solution)/shard_map/ppermute | solution.py:486
  40.4 12.4 %collective-permute-start.1 = (bf16[7,96,256]{2,1,0:T(8,128)(2,1)}, bf16[7,96,256]{2,1,0:T(8,128)(2,1)S(1)}, u32[]{:S(2)}, u32[]{:S(2)}) collective-permute-start(bf16[7,96,256]{2,1,0:T(8,128)(2,1)} %get-tuple-element.31), channel_id=1, source_target_pairs={{0,2},{1,3},{2,0},{3,1},{4,6},{5,7},{6,4},{7,5},{8,10},{9,11},{10,... | collective-permute-start | bytes 1032200 | tf_op jit(solution)/shard_map/ppermute | solution.py:451
  41.7 18.6 %collective-permute-start.2 = (bf16[7,96,256]{2,1,0:T(8,128)(2,1)}, bf16[7,96,256]{2,1,0:T(8,128)(2,1)S(1)}, u32[]{:S(2)}, u32[]{:S(2)}) collective-permute-start(bf16[7,96,256]{2,1,0:T(8,128)(2,1)} %get-tuple-element.32), channel_id=1, source_target_pairs={{0,3},{1,2},{2,1},{3,0},{4,7},{5,6},{6,5},{7,4},{8,11},{9,10},{10,... | collective-permute-start | bytes 1032200 | tf_op jit(solution)/shard_map/ppermute | solution.py:451
  43.0 29.7 %all-to-all-start = ((f32[16,1,128]{2,1,0:T(1,128)}), f32[16,1,128]{2,1,0:T(1,128)S(1)}, u32[]{:S(2)}, u32[]{:S(2)}) async-start(f32[16,1,128]{2,1,0:T(1,128)} %bitcast.8), calls=%async_computation | async-start | bytes 16384 | tf_op jit(solution)/shard_map/all_to_all | solution.py:455
  78.7 10.9 %collective-permute-start.17 = (bf16[4,96,256]{2,1,0:T(8,128)(2,1)S(1)}, bf16[4,96,256]{2,1,0:T(8,128)(2,1)S(1)}, u32[]{:S(2)}, u32[]{:S(2)}) collective-permute-start(bf16[4,96,256]{2,1,0:T(8,128)(2,1)S(1)} %get-tuple-element.52), channel_id=1, source_target_pairs={{0,1},{1,0},{2,3},{3,2},{4,5},{5,4},{6,7},{7,6},{8,9},{9,8},{10,11... | collective-permute-start | bytes 589832 | tf_op jit(solution)/shard_map/ppermute | solution.py:451
  78.8 13.6 %collective-permute-start.18 = (bf16[4,96,256]{2,1,0:T(8,128)(2,1)S(1)}, bf16[4,96,256]{2,1,0:T(8,128)(2,1)S(1)}, u32[]{:S(2)}, u32[]{:S(2)}) collective-permute-start(bf16[4,96,256]{2,1,0:T(8,128)(2,1)S(1)} %get-tuple-element.53), channel_id=1, source_target_pairs={{0,2},{1,3},{2,0},{3,1},{4,6},{5,7},{6,4},{7,5},{8,10},{9,11},{10,... | collective-permute-start | bytes 589832 | tf_op jit(solution)/shard_map/ppermute | solution.py:451
  82.4 16.0 %collective-permute-start.19 = (bf16[4,96,256]{2,1,0:T(8,128)(2,1)S(1)}, bf16[4,96,256]{2,1,0:T(8,128)(2,1)S(1)}, u32[]{:S(2)}, u32[]{:S(2)}) collective-permute-start(bf16[4,96,256]{2,1,0:T(8,128)(2,1)S(1)} %get-tuple-element.54), channel_id=1, source_target_pairs={{0,3},{1,2},{2,1},{3,0},{4,7},{5,6},{6,5},{7,4},{8,11},{9,10},{10,... | collective-permute-start | bytes 589832 | tf_op jit(solution)/shard_map/ppermute | solution.py:451
  85.9 13.4 %collective-permute-start.14 = (bf16[3,96,256]{2,1,0:T(8,128)(2,1)S(1)}, bf16[3,96,256]{2,1,0:T(8,128)(2,1)S(1)}, u32[]{:S(2)}, u32[]{:S(2)}) collective-permute-start(bf16[3,96,256]{2,1,0:T(8,128)(2,1)S(1)} %get-tuple-element.48), channel_id=1, source_target_pairs={{0,1},{1,0},{2,3},{3,2},{4,5},{5,4},{6,7},{7,6},{8,9},{9,8},{10,11... | collective-permute-start | bytes 442376 | tf_op jit(solution)/shard_map/ppermute | solution.py:451
  86.0 13.3 %collective-permute-start.15 = (bf16[3,96,256]{2,1,0:T(8,128)(2,1)S(1)}, bf16[3,96,256]{2,1,0:T(8,128)(2,1)S(1)}, u32[]{:S(2)}, u32[]{:S(2)}) collective-permute-start(bf16[3,96,256]{2,1,0:T(8,128)(2,1)S(1)} %get-tuple-element.49), channel_id=1, source_target_pairs={{0,2},{1,3},{2,0},{3,1},{4,6},{5,7},{6,4},{7,5},{8,10},{9,11},{10,... | collective-permute-start | bytes 442376 | tf_op jit(solution)/shard_map/ppermute | solution.py:451
  89.6 10.9 %collective-permute-start.16 = (bf16[3,96,256]{2,1,0:T(8,128)(2,1)S(1)}, bf16[3,96,256]{2,1,0:T(8,128)(2,1)S(1)}, u32[]{:S(2)}, u32[]{:S(2)}) collective-permute-start(bf16[3,96,256]{2,1,0:T(8,128)(2,1)S(1)} %get-tuple-element.50), channel_id=1, source_target_pairs={{0,3},{1,2},{2,1},{3,0},{4,7},{5,6},{6,5},{7,4},{8,11},{9,10},{10,... | collective-permute-start | bytes 442376 | tf_op jit(solution)/shard_map/ppermute | solution.py:451
  (17 other events, 72.5 us)

commit v6 on v5

--- a/solution.py
+++ b/solution.py
@@ -54,7 +54,7 @@
 
 
 def pack_body(me, far_weights, ensemble, far_tiles, *rest):
-    *blocks, predicted, weights, tiles, buffer, arrived, left = rest
+    *blocks, predicted, weights, tiles, chosen, halves, buffer, arrived, left = rest
     peers, var_count, _, width = buffer.shape
     starts = [tile_block(me[0], s, width) for s in range(peers)]
     loads = [
@@ -73,19 +73,23 @@
     for load in light:
         load.wait()
     rows = lax.broadcasted_iota(jnp.int32, (width, tiles.shape[1]), 0)
-    total = jnp.zeros(predicted.shape, F32)
     for s in range(peers):
-        chosen = jnp.where(tiles[...] - starts[s] == rows, 1.0, 0.0).astype(BF16)
+        chosen[s * width : (s + 1) * width] = jnp.where(
+            tiles[...] - starts[s] == rows, 1.0, 0.0
+        ).astype(BF16)
+    for s in range(peers):
         loads[s].wait()
         stores[s].start()
         mixed = weights[0] * buffer[s, 0].astype(F32)
         for l in range(1, var_count):
             mixed = mixed + weights[l] * buffer[s, l].astype(F32)
         high = mixed.astype(BF16)
-        low = (mixed - high.astype(F32)).astype(BF16)
-        total = total + jnp.dot(high, chosen, preferred_element_type=F32)
-        total = total + jnp.dot(low, chosen, preferred_element_type=F32)
-    predicted[...] = total.astype(BF16)
+        columns = slice(s * width, (s + 1) * width)
+        halves[: mixed.shape[0], columns] = high
+        halves[mixed.shape[0] :, columns] = (mixed - high.astype(F32)).astype(BF16)
+    picked = jnp.dot(halves[...], chosen[...], preferred_element_type=F32)
+    own = predicted.shape[0]
+    predicted[...] = (picked[:own] + picked[own:]).astype(BF16)
     for store in stores:
         store.wait()
 
@@ -102,6 +106,8 @@
         scratch_shapes=[
             pltpu.SMEM((var_count,), F32),
             pltpu.VMEM((1, obs), jnp.int32),
+            pltpu.VMEM((tile_count, obs), BF16),
+            pltpu.VMEM((2 * own, tile_count), BF16),
             pltpu.VMEM((peers, var_count, own, width), BF16),
             pltpu.SemaphoreType.DMA((peers + 2,)),
             pltpu.SemaphoreType.DMA((peers,)),
@@ -240,20 +246,13 @@
 
 
 def prepare_body(offset, *refs, tile_count):
-    *far_packets, anom_t, taper, packets, arrived = refs
+    *packets, anom_t, taper = refs
     members = anom_t.shape[1]
-    obs = packets.shape[2]
-    loads = [
-        pltpu.make_async_copy(packet, packets.at[n], arrived.at[n])
-        for n, packet in enumerate(far_packets)
-    ]
-    for load in loads:
-        load.start()
-    for n, load in enumerate(loads):
-        load.wait()
+    obs = packets[0].shape[1]
+    for n, packet in enumerate(packets):
         rows = slice(n * obs, (n + 1) * obs)
-        anom_t[rows] = packets[n, :members].T
-        taper[rows] = tapers(packets[n, members:], offset, 1 + n, taper.shape[1], members, tile_count)
+        anom_t[rows] = packet[:members].T
+        taper[rows] = tapers(packet[members:], offset, 1 + n, taper.shape[1], members, tile_count)
 
 
 def prepare(offset, packets, width, tile_count):
@@ -262,16 +261,12 @@
     count = len(packets)
     return pl.pallas_call(
         functools.partial(prepare_body, tile_count=tile_count),
-        in_specs=[scalars()] + [anywhere()] * count,
+        in_specs=[scalars()] + [whole()] * count,
         out_specs=[whole()] * 2,
         out_shape=[shape_of((count * obs, members)), shape_of((count * obs, width), F32)],
-        scratch_shapes=[
-            pltpu.VMEM((count, rows, obs), BF16),
-            pltpu.SemaphoreType.DMA((count,)),
-        ],
-        compiler_params=params(),
+        compiler_params=params(4),
         name="prepare",
-    )(offset, *map(in_hbm, packets))
+    )(offset, *in_vmem(packets))
 
 
 def start_body(offset, *refs, peers, tile_count):
@@ -342,22 +337,26 @@
     )
 
 
-def first_body(means, anomalies, gain, packets, sums, *refs):
-    noises, (*blocks, perturbed, root_out, inflation_out) = refs[:3], refs[3:]
+def first_body(means, anomalies, gain, packets, sums, noise_0, noise_1, far_noise, *refs):
+    *blocks, perturbed, root_out, inflation_out, noise_2, arrived = refs
     members = anomalies.shape[1]
     obs = packets.shape[2]
+    load = pltpu.make_async_copy(far_noise, noise_2, arrived)
+    load.start()
     folded = jnp.sum(sums[...], axis=0, keepdims=True)
     inflation = folded[:, 0:1] / folded[:, 1:2]
     inflation_out[0] = jnp.sum(inflation)
     root = jnp.sqrt(inflation)
     root_out[...] = jnp.broadcast_to(root, root_out.shape)
-    for n in range(3):
+    for n, noise in enumerate((noise_0, noise_1, noise_2)):
+        if n == 2:
+            load.wait()
         innovation, error, spread, _ = scalar_rows(packets[n, members:])
         bottom = jnp.where(error > 0.0, inflation * spread + error, 1.0)
         factor = jnp.where(error > 0.0, inflation / bottom, 0.0)
         dev = packets[n, :members].astype(F32)
         perturbed[:, n * obs : (n + 1) * obs] = (
-            factor * (innovation + noises[n][...].astype(F32) - root * dev)
+            factor * (innovation + noise[...].astype(F32) - root * dev)
         ).astype(BF16)
     for l in range(gain.shape[0]):
         posterior(gain.at[l], means.at[l], anomalies.at[l], perturbed, root, blocks, l)
@@ -376,7 +375,7 @@
     obs = packets.shape[2]
     out = pl.pallas_call(
         first_body,
-        in_specs=[whole()] * 8,
+        in_specs=[whole()] * 7 + [anywhere()],
         out_specs=[whole()] * (peers + 2) + [scalars()],
         out_shape=[shape_of((count, members // peers, width))] * peers
         + [
@@ -384,9 +383,10 @@
             shape_of((8, 128), F32),
             jax.ShapeDtypeStruct((1,), F32),
         ],
+        scratch_shapes=[pltpu.VMEM(noises[2].shape, BF16), pltpu.SemaphoreType.DMA],
         compiler_params=params(4),
         name="first",
-    )(*in_vmem((means, anomalies, gain, packets, sums, *noises)))
+    )(*in_vmem((means, anomalies, gain, packets, sums, *noises[:2])), noises[2])
     return out[:peers], *out[peers:]
 
 

time: 103 us -> 103 us (level)
  Pallas kernels: 17.2 us -> 15.3 us
  waiting for transfers between devices: 34.4 us -> 36.3 us
    ppermute x18, waiting for transfers between devices: 34.4 us -> 36.3 us  [swapped(): return lax.ppermute(value, axis, pairs)]
    pallas_call x1, Pallas kernels: 2.35 us -> 1.24 us  [prepare(): pl.pallas_call(functools.partial(prepare_body, tile_count=tile_count), in...]
  transfers between devices with their start and end apart: 21 -> 21, of which waited for: 10 -> 10; matrix products, arithmetic and copies ran while one was open for 0% -> 0% of each run, Pallas kernels for 10% -> 9%
where the time goes in v6:
time: 103 us; the launch traced here: 101 us
  waiting for transfers between devices  36.3 us (35%)
  starting transfers between devices  36.2 us (35%)
  Pallas kernels  15.3 us (15%)
  local copies, waits for them, and re-layouts  12 us (12%)
  between operations  1.04 us (1%)
    ppermute x18, waiting for transfers between devices, swapped(): return lax.ppermute(value, axis, pairs)  36.3 us
    ppermute x18, starting transfers between devices, swapped(): return lax.ppermute(value, axis, pairs)  25.4 us
    unnamed x40, local copies, waits for them, and re-layouts  12 us
    all_to_all x1, starting transfers between devices, exchanged(): return lax.all_to_all(blocks, axis, split_axis=0, concat_axis=0, tiled=True)  5.54 us
    pallas_call x1, Pallas kernels, start_gains(): pl.pallas_call(functools.partial(start_body, peers=peers, tile_count=tile...  4.11 us
    ppermute x1, starting transfers between devices, shards(): far_noise = lax.ppermute(noise, 'region', pairs)  3.34 us
    pallas_call x1, Pallas kernels, first_updates(): pl.pallas_call(first_body, in_specs=[whole()] * 7 + [anywhere()], out_spe...  2.51 us
    pallas_call x1, Pallas kernels, second_updates(): pl.pallas_call(second_body, in_specs=[whole()] * 7, out_specs=[whole()] *...  2.4 us
  transfers between devices with their start and end apart: 21, of which 10 were waited for; matrix products, arithmetic and copies ran while one was open for 0% of the time, Pallas kernels for 9%

profile of v6, /device:TPU:96, one launch (start us, length us, event | category | flops | bytes accessed | tf_op | source)
XLA Modules:
  0.0 101.0 jit_solution(18225612597510558851)
XLA Ops:
  0.7 2.3 %pack.1 = (bf16[7,96,256]{2,1,0:T(8,128)(2,1)}, bf16[7,96,256]{2,1,0:T(8,128)(2,1)}, bf16[7,96,256]{2,1,0:T(8,128)(2,1)}, bf16[7,96,256]{2,1,0:T(8,128)(2,1)}, bf16[96,512]{1,0:T(8,128)(2,1)S(1)}) custom-call(s32[1]{0:T(128)} %bitcast.me, f32[7]{0:T(128)} %far_weights.1, bf16[7,96,1024]{2,1,0:T(8,128)(2,1)} %ensemble.1, s32[1,512]{1,0:T(1,128)} %bitcast.13), custom_call_target="tpu_custom_call" | custom-call | tf_op jit(solution)/shard_map/pack/pallas_call | solution.py:101
  3.0 3.3 %collective-permute-start.3 = (bf16[96,512]{1,0:T(8,128)(2,1)S(1)}, bf16[96,512]{1,0:T(8,128)(2,1)S(1)}, u32[]{:S(2)}, u32[]{:S(2)}) collective-permute-start(bf16[96,512]{1,0:T(8,128)(2,1)S(1)} %get-tuple-element.33.mine), channel_id=1, source_target_pairs={{0,4},{4,0},{1,5},{5,1},{2,6},{6,2},{3,7},{7,3},{8,12},{12,8},{9,1... | collective-permute-start | bytes 294920 | tf_op jit(solution)/shard_map/ppermute | solution.py:451
  6.3 2.9 %collective-permute-done.3.other = bf16[96,512]{1,0:T(8,128)(2,1)S(1)} collective-permute-done((bf16[96,512]{1,0:T(8,128)(2,1)S(1)}, bf16[96,512]{1,0:T(8,128)(2,1)S(1)}, u32[]{:S(2)}, u32[]{:S(2)}) %collective-permute-start.3) | collective-permute-done | bytes 98336 | tf_op jit(solution)/shard_map/ppermute | solution.py:451
  9.2 1.6 %collective-permute-start.4 = (bf16[96,512]{1,0:T(8,128)(2,1)S(1)}, bf16[96,512]{1,0:T(8,128)(2,1)S(1)}, u32[]{:S(2)}, u32[]{:S(2)}) collective-permute-start(bf16[96,512]{1,0:T(8,128)(2,1)S(1)} %join.1.refs_0_), channel_id=1, source_target_pairs={{0,1},{1,0},{2,3},{3,2},{4,5},{5,4},{6,7},{7,6},{8,9},{9,8},{10,11... | collective-permute-start | bytes 294920 | tf_op jit(solution)/shard_map/ppermute | solution.py:451
  10.8 2.7 %collective-permute-start.5 = (bf16[96,512]{1,0:T(8,128)(2,1)S(1)}, bf16[96,512]{1,0:T(8,128)(2,1)S(1)}, u32[]{:S(2)}, u32[]{:S(2)}) collective-permute-start(bf16[96,512]{1,0:T(8,128)(2,1)S(1)} %join.1.refs_0_), channel_id=1, source_target_pairs={{0,2},{1,3},{2,0},{3,1},{4,6},{5,7},{6,4},{7,5},{8,10},{9,11},{10,... | collective-permute-start | bytes 294920 | tf_op jit(solution)/shard_map/ppermute | solution.py:451
  14.8 2.4 %collective-permute-done.5.refs_2_ = bf16[96,512]{1,0:T(8,128)(2,1)S(1)} collective-permute-done((bf16[96,512]{1,0:T(8,128)(2,1)S(1)}, bf16[96,512]{1,0:T(8,128)(2,1)S(1)}, u32[]{:S(2)}, u32[]{:S(2)}) %collective-permute-start.5) | collective-permute-done | bytes 98336 | tf_op jit(solution)/shard_map/ppermute | solution.py:451
  17.3 2.1 %collective-permute-done.6.refs_3_ = bf16[96,512]{1,0:T(8,128)(2,1)S(1)} collective-permute-done((bf16[96,512]{1,0:T(8,128)(2,1)S(1)}, bf16[96,512]{1,0:T(8,128)(2,1)S(1)}, u32[]{:S(2)}, u32[]{:S(2)}) %collective-permute-start.6) | collective-permute-done | bytes 98336 | tf_op jit(solution)/shard_map/ppermute | solution.py:451
  20.4 2.2 %collective-permute-start.10 = (bf16[96,512]{1,0:T(8,128)(2,1)S(1)}, bf16[96,512]{1,0:T(8,128)(2,1)S(1)}, u32[]{:S(2)}, u32[]{:S(2)}) collective-permute-start(bf16[96,512]{1,0:T(8,128)(2,1)S(1)} %scale.1.refs_0_), channel_id=1, source_target_pairs={{0,2},{1,3},{2,0},{3,1},{4,6},{5,7},{6,4},{7,5},{8,10},{9,11},{10,... | collective-permute-start | bytes 294920 | tf_op jit(solution)/shard_map/ppermute | solution.py:451
  22.6 2.5 %collective-permute-start.11 = (bf16[96,512]{1,0:T(8,128)(2,1)S(1)}, bf16[96,512]{1,0:T(8,128)(2,1)S(1)}, u32[]{:S(2)}, u32[]{:S(2)}) collective-permute-start(bf16[96,512]{1,0:T(8,128)(2,1)S(1)} %scale.1.refs_0_), channel_id=1, source_target_pairs={{0,3},{1,2},{2,1},{3,0},{4,7},{5,6},{6,5},{7,4},{8,11},{9,10},{10,... | collective-permute-start | bytes 294920 | tf_op jit(solution)/shard_map/ppermute | solution.py:451
  25.1 8.6 %collective-permute-done.10.refs_2_ = bf16[96,512]{1,0:T(8,128)(2,1)S(1)} collective-permute-done((bf16[96,512]{1,0:T(8,128)(2,1)S(1)}, bf16[96,512]{1,0:T(8,128)(2,1)S(1)}, u32[]{:S(2)}, u32[]{:S(2)}) %collective-permute-start.10) | collective-permute-done | bytes 98336 | tf_op jit(solution)/shard_map/ppermute | solution.py:451
  33.7 1.9 %collective-permute-start.8 = (bf16[400,512]{1,0:T(8,128)(2,1)S(1)}, bf16[400,512]{1,0:T(8,128)(2,1)}, u32[]{:S(2)}, u32[]{:S(2)}) collective-permute-start(bf16[400,512]{1,0:T(8,128)(2,1)S(1)} %get-tuple-element.34.refs_0_.refs_4_), channel_id=1, source_target_pairs={{8,16},{24,32},{40,48},{56,64},{72,80},{88,96},{104,112},{16,8},{3... | collective-permute-start | bytes 1228808 | tf_op jit(solution)/shard_map/ppermute | solution.py:481
  36.1 3.3 %collective-permute-start.13 = (bf16[384,512]{1,0:T(8,128)(2,1)S(1)}, bf16[384,512]{1,0:T(8,128)(2,1)}, u32[]{:S(2)}, u32[]{:S(2)}) collective-permute-start(bf16[384,512]{1,0:T(8,128)(2,1)S(1)} %joinnoise.1.noise_0), channel_id=1, source_target_pairs={{8,16},{24,32},{40,48},{56,64},{72,80},{88,96},{104,112},{16,8},{3... | collective-permute-start | bytes 1179656 | tf_op jit(solution)/shard_map/ppermute | solution.py:486
  42.8 5.5 %all-to-all-start = ((f32[16,1,128]{2,1,0:T(1,128)}), f32[16,1,128]{2,1,0:T(1,128)S(1)}, u32[]{:S(2)}, u32[]{:S(2)}) async-start(f32[16,1,128]{2,1,0:T(1,128)} %bitcast.8), calls=%async_computation | async-start | bytes 16384 | tf_op jit(solution)/shard_map/all_to_all | solution.py:455
  49.7 3.0 %collective-permute-done.1.refs_2_ = bf16[7,96,256]{2,1,0:T(8,128)(2,1)} collective-permute-done((bf16[7,96,256]{2,1,0:T(8,128)(2,1)}, bf16[7,96,256]{2,1,0:T(8,128)(2,1)}, u32[]{:S(2)}, u32[]{:S(2)}) %collective-permute-start.1) | collective-permute-done | bytes 344096 | tf_op jit(solution)/shard_map/ppermute | solution.py:451
  52.7 7.5 %collective-permute-done.2.refs_3_ = bf16[7,96,256]{2,1,0:T(8,128)(2,1)} collective-permute-done((bf16[7,96,256]{2,1,0:T(8,128)(2,1)}, bf16[7,96,256]{2,1,0:T(8,128)(2,1)}, u32[]{:S(2)}, u32[]{:S(2)}) %collective-permute-start.2) | collective-permute-done | bytes 344096 | tf_op jit(solution)/shard_map/ppermute | solution.py:451
  61.2 4.1 %start.1 = (bf16[512,384]{1,0:T(8,128)(2,1)S(1)}, f32[512,256]{1,0:T(8,128)S(1)}, f32[4,8,256]{2,1,0:T(8,128)S(1)}, bf16[4,384,256]{2,1,0:T(8,128)(2,1)S(1)}, bf...) custom-call(s32[4]{0:T(128)S(1)} %pad_add_fusion.offset, ...), custom_call_target="tpu_custom_call" | custom-call | tf_op jit(solution)/shard_map/start/pallas_call | solution.py:310
  65.4 1.6 %copy-done = bf16[4,1536,256]{2,1,0:T(8,128)(2,1)} copy-done((bf16[4,1536,256]{2,1,0:T(8,128)(2,1)}, bf16[4,1536,256]{2,1,0:T(8,128)(2,1)S(1)}, u32[]{:S(2)}) %copy-start) | copy-done | bytes 3145752
  71.4 1.9 %copy-done.1 = bf16[4,1536,256]{2,1,0:T(8,128)(2,1)S(1)} copy-done((bf16[4,1536,256]{2,1,0:T(8,128)(2,1)S(1)}, bf16[4,1536,256]{2,1,0:T(8,128)(2,1)}, u32[]{:S(2)}) %copy-start.1) | copy-done | bytes 3145752
  75.7 2.5 %first.1 = (bf16[4,96,256]{2,1,0:T(8,128)(2,1)S(1)}, bf16[4,96,256]{2,1,0:T(8,128)(2,1)S(1)}, bf16[4,96,256]{2,1,0:T(8,128)(2,1)S(1)}, bf16[4,96,256]{2,1,0:T(8,...) custom-call(f32[4,8,256]{2,1,0:T(8,128)S(1)} %get-tuple-element.38.means, ...), custom_call_target="tpu_custom_call" | custom-call | tf_op jit(solution)/shard_map/first/pallas_call | solution.py:376
  78.3 3.6 %collective-permute-start.18 = (bf16[4,96,256]{2,1,0:T(8,128)(2,1)S(1)}, bf16[4,96,256]{2,1,0:T(8,128)(2,1)S(1)}, u32[]{:S(2)}, u32[]{:S(2)}) collective-permute-start(bf16[4,96,256]{2,1,0:T(8,128)(2,1)S(1)} %get-tuple-element.53), channel_id=1, source_target_pairs={{0,2},{1,3},{2,0},{3,1},{4,6},{5,7},{6,4},{7,5},{8,10},{9,11},{10,... | collective-permute-start | bytes 589832 | tf_op jit(solution)/shard_map/ppermute | solution.py:451
  83.0 2.4 %second.1 = (bf16[3,96,256]{2,1,0:T(8,128)(2,1)S(1)}, bf16[3,96,256]{2,1,0:T(8,128)(2,1)S(1)}, bf16[3,96,256]{2,1,0:T(8,128)(2,1)S(1)}, bf16[3,96,256]{2,1,0:T(8,128)(2,1)S(1)}) custom-call(bf16[4,3,96,256]{3,2,1,0:T(8,128)(2,1)S(1)} %copy-done.9, bf16[384,1536]{1,0:T(8,128)(2,1)S(1)} %get-tuple-element.43.perturbed, f32[8,128]{1,0:T(8,128)S(1)} %get-tuple-element.44.root, ...), custom_call_target="tpu_custom_call" | custom-call | tf_op jit(solution)/shard_map/second/pallas_call | solution.py:406
  85.5 3.6 %collective-permute-start.15 = (bf16[3,96,256]{2,1,0:T(8,128)(2,1)S(1)}, bf16[3,96,256]{2,1,0:T(8,128)(2,1)S(1)}, u32[]{:S(2)}, u32[]{:S(2)}) collective-permute-start(bf16[3,96,256]{2,1,0:T(8,128)(2,1)S(1)} %get-tuple-element.49), channel_id=1, source_target_pairs={{0,2},{1,3},{2,0},{3,1},{4,6},{5,7},{6,4},{7,5},{8,10},{9,11},{10,... | collective-permute-start | bytes 442376 | tf_op jit(solution)/shard_map/ppermute | solution.py:451
  90.2 1.7 %collective-permute-done.18.refs_2_ = bf16[4,96,256]{2,1,0:T(8,128)(2,1)S(1)} collective-permute-done((bf16[4,96,256]{2,1,0:T(8,128)(2,1)S(1)}, bf16[4,96,256]{2,1,0:T(8,128)(2,1)S(1)}, u32[]{:S(2)}, u32[]{:S(2)}) %collective-permute-start.18) | collective-permute-done | bytes 196640 | tf_op jit(solution)/shard_map/ppermute | solution.py:451
  91.9 6.0 %collective-permute-done.19.refs_3_ = bf16[4,96,256]{2,1,0:T(8,128)(2,1)S(1)} collective-permute-done((bf16[4,96,256]{2,1,0:T(8,128)(2,1)S(1)}, bf16[4,96,256]{2,1,0:T(8,128)(2,1)S(1)}, u32[]{:S(2)}, u32[]{:S(2)}) %collective-permute-start.19) | collective-permute-done | bytes 196640 | tf_op jit(solution)/shard_map/ppermute | solution.py:451
  (70 shorter events, 20.5 us)
Async XLA Ops:
  0.6 18.7 %copy-start.17 = (s32[512]{0:T(512)S(1)}, s32[512]{0:T(512)}, u32[]{:S(2)}) copy-start(s32[512]{0:T(512)} %param.8) | copy-start | bytes 6148
  0.7 19.7 %copy-start.16 = (f32[96,512]{1,0:T(8,128)S(1)}, f32[96,512]{1,0:T(8,128)}, u32[]{:S(2)}) copy-start(f32[96,512]{1,0:T(8,128)} %noise.1) | copy-start | bytes 589828
  3.0 6.2 %collective-permute-start.3 = (bf16[96,512]{1,0:T(8,128)(2,1)S(1)}, bf16[96,512]{1,0:T(8,128)(2,1)S(1)}, u32[]{:S(2)}, u32[]{:S(2)}) collective-permute-start(bf16[96,512]{1,0:T(8,128)(2,1)S(1)} %get-tuple-element.33.mine), channel_id=1, source_target_pairs={{0,4},{4,0},{1,5},{5,1},{2,6},{6,2},{3,7},{7,3},{8,12},{12,8},{9,1... | collective-permute-start | bytes 294920 | tf_op jit(solution)/shard_map/ppermute | solution.py:451
  9.2 5.6 %collective-permute-start.4 = (bf16[96,512]{1,0:T(8,128)(2,1)S(1)}, bf16[96,512]{1,0:T(8,128)(2,1)S(1)}, u32[]{:S(2)}, u32[]{:S(2)}) collective-permute-start(bf16[96,512]{1,0:T(8,128)(2,1)S(1)} %join.1.refs_0_), channel_id=1, source_target_pairs={{0,1},{1,0},{2,3},{3,2},{4,5},{5,4},{6,7},{7,6},{8,9},{9,8},{10,11... | collective-permute-start | bytes 294920 | tf_op jit(solution)/shard_map/ppermute | solution.py:451
  10.8 6.5 %collective-permute-start.5 = (bf16[96,512]{1,0:T(8,128)(2,1)S(1)}, bf16[96,512]{1,0:T(8,128)(2,1)S(1)}, u32[]{:S(2)}, u32[]{:S(2)}) collective-permute-start(bf16[96,512]{1,0:T(8,128)(2,1)S(1)} %join.1.refs_0_), channel_id=1, source_target_pairs={{0,2},{1,3},{2,0},{3,1},{4,6},{5,7},{6,4},{7,5},{8,10},{9,11},{10,... | collective-permute-start | bytes 294920 | tf_op jit(solution)/shard_map/ppermute | solution.py:451
  13.5 5.8 %collective-permute-start.6 = (bf16[96,512]{1,0:T(8,128)(2,1)S(1)}, bf16[96,512]{1,0:T(8,128)(2,1)S(1)}, u32[]{:S(2)}, u32[]{:S(2)}) collective-permute-start(bf16[96,512]{1,0:T(8,128)(2,1)S(1)} %join.1.refs_0_), channel_id=1, source_target_pairs={{0,3},{1,2},{2,1},{3,0},{4,7},{5,6},{6,5},{7,4},{8,11},{9,10},{10,... | collective-permute-start | bytes 294920 | tf_op jit(solution)/shard_map/ppermute | solution.py:451
  20.3 40.0 %copy-start.2 = (bf16[400,512]{1,0:T(8,128)(2,1)}, bf16[400,512]{1,0:T(8,128)(2,1)S(1)}, u32[]{:S(2)}) copy-start(bf16[400,512]{1,0:T(8,128)(2,1)S(1)} %get-tuple-element.34.refs_0_.refs_4_) | copy-start | bytes 1228804
  20.3 21.2 %collective-permute-start.7 = (bf16[400,512]{1,0:T(8,128)(2,1)S(1)}, bf16[400,512]{1,0:T(8,128)(2,1)S(1)}, u32[]{:S(2)}, u32[]{:S(2)}) collective-permute-start(bf16[400,512]{1,0:T(8,128)(2,1)S(1)} %get-tuple-element.34.refs_0_.refs_4_), channel_id=1, source_target_pairs={{0,8},{8,0},{16,24},{24,16},{32,40},{40,32},{48,56},{56,48},{64,72... | collective-permute-start | bytes 1228808 | tf_op jit(solution)/shard_map/ppermute | solution.py:451
  20.3 19.1 %collective-permute-start = (bf16[7,96,256]{2,1,0:T(8,128)(2,1)}, bf16[7,96,256]{2,1,0:T(8,128)(2,1)S(1)}, u32[]{:S(2)}, u32[]{:S(2)}) collective-permute-start(bf16[7,96,256]{2,1,0:T(8,128)(2,1)} %get-tuple-element.30), channel_id=1, source_target_pairs={{0,1},{1,0},{2,3},{3,2},{4,5},{5,4},{6,7},{7,6},{8,9},{9,8},{10,11... | collective-permute-start | bytes 1032200 | tf_op jit(solution)/shard_map/ppermute | solution.py:451
  20.4 13.4 %collective-permute-start.10 = (bf16[96,512]{1,0:T(8,128)(2,1)S(1)}, bf16[96,512]{1,0:T(8,128)(2,1)S(1)}, u32[]{:S(2)}, u32[]{:S(2)}) collective-permute-start(bf16[96,512]{1,0:T(8,128)(2,1)S(1)} %scale.1.refs_0_), channel_id=1, source_target_pairs={{0,2},{1,3},{2,0},{3,1},{4,6},{5,7},{6,4},{7,5},{8,10},{9,11},{10,... | collective-permute-start | bytes 294920 | tf_op jit(solution)/shard_map/ppermute | solution.py:451
  22.6 13.0 %collective-permute-start.11 = (bf16[96,512]{1,0:T(8,128)(2,1)S(1)}, bf16[96,512]{1,0:T(8,128)(2,1)S(1)}, u32[]{:S(2)}, u32[]{:S(2)}) collective-permute-start(bf16[96,512]{1,0:T(8,128)(2,1)S(1)} %scale.1.refs_0_), channel_id=1, source_target_pairs={{0,3},{1,2},{2,1},{3,0},{4,7},{5,6},{6,5},{7,4},{8,11},{9,10},{10,... | collective-permute-start | bytes 294920 | tf_op jit(solution)/shard_map/ppermute | solution.py:451
  25.1 10.5 %collective-permute-start.9 = (bf16[96,512]{1,0:T(8,128)(2,1)S(1)}, bf16[96,512]{1,0:T(8,128)(2,1)S(1)}, u32[]{:S(2)}, u32[]{:S(2)}) collective-permute-start(bf16[96,512]{1,0:T(8,128)(2,1)S(1)} %scale.1.refs_0_), channel_id=1, source_target_pairs={{0,1},{1,0},{2,3},{3,2},{4,5},{5,4},{6,7},{7,6},{8,9},{9,8},{10,11... | collective-permute-start | bytes 294920 | tf_op jit(solution)/shard_map/ppermute | solution.py:451
  33.7 26.5 %collective-permute-start.8 = (bf16[400,512]{1,0:T(8,128)(2,1)S(1)}, bf16[400,512]{1,0:T(8,128)(2,1)}, u32[]{:S(2)}, u32[]{:S(2)}) collective-permute-start(bf16[400,512]{1,0:T(8,128)(2,1)S(1)} %get-tuple-element.34.refs_0_.refs_4_), channel_id=1, source_target_pairs={{8,16},{24,32},{40,48},{56,64},{72,80},{88,96},{104,112},{16,8},{3... | collective-permute-start | bytes 1228808 | tf_op jit(solution)/shard_map/ppermute | solution.py:481
  35.7 35.6 %collective-permute-start.12 = (bf16[384,512]{1,0:T(8,128)(2,1)S(1)}, bf16[384,512]{1,0:T(8,128)(2,1)S(1)}, u32[]{:S(2)}, u32[]{:S(2)}) collective-permute-start(bf16[384,512]{1,0:T(8,128)(2,1)S(1)} %joinnoise.1.noise_0), channel_id=1, source_target_pairs={{0,8},{8,0},{16,24},{24,16},{32,40},{40,32},{48,56},{56,48},{64,72... | collective-permute-start | bytes 1179656 | tf_op jit(solution)/shard_map/ppermute | solution.py:451
  36.1 35.3 %collective-permute-start.13 = (bf16[384,512]{1,0:T(8,128)(2,1)S(1)}, bf16[384,512]{1,0:T(8,128)(2,1)}, u32[]{:S(2)}, u32[]{:S(2)}) collective-permute-start(bf16[384,512]{1,0:T(8,128)(2,1)S(1)} %joinnoise.1.noise_0), channel_id=1, source_target_pairs={{8,16},{24,32},{40,48},{56,64},{72,80},{88,96},{104,112},{16,8},{3... | collective-permute-start | bytes 1179656 | tf_op jit(solution)/shard_map/ppermute | solution.py:486
  40.2 12.5 %collective-permute-start.1 = (bf16[7,96,256]{2,1,0:T(8,128)(2,1)}, bf16[7,96,256]{2,1,0:T(8,128)(2,1)}, u32[]{:S(2)}, u32[]{:S(2)}) collective-permute-start(bf16[7,96,256]{2,1,0:T(8,128)(2,1)} %get-tuple-element.31), channel_id=1, source_target_pairs={{0,2},{1,3},{2,0},{3,1},{4,6},{5,7},{6,4},{7,5},{8,10},{9,11},{10,... | collective-permute-start | bytes 1032200 | tf_op jit(solution)/shard_map/ppermute | solution.py:451
  41.5 18.7 %collective-permute-start.2 = (bf16[7,96,256]{2,1,0:T(8,128)(2,1)}, bf16[7,96,256]{2,1,0:T(8,128)(2,1)}, u32[]{:S(2)}, u32[]{:S(2)}) collective-permute-start(bf16[7,96,256]{2,1,0:T(8,128)(2,1)} %get-tuple-element.32), channel_id=1, source_target_pairs={{0,3},{1,2},{2,1},{3,0},{4,7},{5,6},{6,5},{7,4},{8,11},{9,10},{10,... | collective-permute-start | bytes 1032200 | tf_op jit(solution)/shard_map/ppermute | solution.py:451
  42.8 28.5 %all-to-all-start = ((f32[16,1,128]{2,1,0:T(1,128)}), f32[16,1,128]{2,1,0:T(1,128)S(1)}, u32[]{:S(2)}, u32[]{:S(2)}) async-start(f32[16,1,128]{2,1,0:T(1,128)} %bitcast.8), calls=%async_computation | async-start | bytes 16384 | tf_op jit(solution)/shard_map/all_to_all | solution.py:455
  78.2 10.9 %collective-permute-start.17 = (bf16[4,96,256]{2,1,0:T(8,128)(2,1)S(1)}, bf16[4,96,256]{2,1,0:T(8,128)(2,1)S(1)}, u32[]{:S(2)}, u32[]{:S(2)}) collective-permute-start(bf16[4,96,256]{2,1,0:T(8,128)(2,1)S(1)} %get-tuple-element.52), channel_id=1, source_target_pairs={{0,1},{1,0},{2,3},{3,2},{4,5},{5,4},{6,7},{7,6},{8,9},{9,8},{10,11... | collective-permute-start | bytes 589832 | tf_op jit(solution)/shard_map/ppermute | solution.py:451
  78.3 13.6 %collective-permute-start.18 = (bf16[4,96,256]{2,1,0:T(8,128)(2,1)S(1)}, bf16[4,96,256]{2,1,0:T(8,128)(2,1)S(1)}, u32[]{:S(2)}, u32[]{:S(2)}) collective-permute-start(bf16[4,96,256]{2,1,0:T(8,128)(2,1)S(1)} %get-tuple-element.53), channel_id=1, source_target_pairs={{0,2},{1,3},{2,0},{3,1},{4,6},{5,7},{6,4},{7,5},{8,10},{9,11},{10,... | collective-permute-start | bytes 589832 | tf_op jit(solution)/shard_map/ppermute | solution.py:451
  81.9 16.0 %collective-permute-start.19 = (bf16[4,96,256]{2,1,0:T(8,128)(2,1)S(1)}, bf16[4,96,256]{2,1,0:T(8,128)(2,1)S(1)}, u32[]{:S(2)}, u32[]{:S(2)}) collective-permute-start(bf16[4,96,256]{2,1,0:T(8,128)(2,1)S(1)} %get-tuple-element.54), channel_id=1, source_target_pairs={{0,3},{1,2},{2,1},{3,0},{4,7},{5,6},{6,5},{7,4},{8,11},{9,10},{10,... | collective-permute-start | bytes 589832 | tf_op jit(solution)/shard_map/ppermute | solution.py:451
  85.4 13.4 %collective-permute-start.14 = (bf16[3,96,256]{2,1,0:T(8,128)(2,1)S(1)}, bf16[3,96,256]{2,1,0:T(8,128)(2,1)S(1)}, u32[]{:S(2)}, u32[]{:S(2)}) collective-permute-start(bf16[3,96,256]{2,1,0:T(8,128)(2,1)S(1)} %get-tuple-element.48), channel_id=1, source_target_pairs={{0,1},{1,0},{2,3},{3,2},{4,5},{5,4},{6,7},{7,6},{8,9},{9,8},{10,11... | collective-permute-start | bytes 442376 | tf_op jit(solution)/shard_map/ppermute | solution.py:451
  85.5 13.3 %collective-permute-start.15 = (bf16[3,96,256]{2,1,0:T(8,128)(2,1)S(1)}, bf16[3,96,256]{2,1,0:T(8,128)(2,1)S(1)}, u32[]{:S(2)}, u32[]{:S(2)}) collective-permute-start(bf16[3,96,256]{2,1,0:T(8,128)(2,1)S(1)} %get-tuple-element.49), channel_id=1, source_target_pairs={{0,2},{1,3},{2,0},{3,1},{4,6},{5,7},{6,4},{7,5},{8,10},{9,11},{10,... | collective-permute-start | bytes 442376 | tf_op jit(solution)/shard_map/ppermute | solution.py:451
  89.1 10.9 %collective-permute-start.16 = (bf16[3,96,256]{2,1,0:T(8,128)(2,1)S(1)}, bf16[3,96,256]{2,1,0:T(8,128)(2,1)S(1)}, u32[]{:S(2)}, u32[]{:S(2)}) collective-permute-start(bf16[3,96,256]{2,1,0:T(8,128)(2,1)S(1)} %get-tuple-element.50), channel_id=1, source_target_pairs={{0,3},{1,2},{2,1},{3,0},{4,7},{5,6},{6,5},{7,4},{8,11},{9,10},{10,... | collective-permute-start | bytes 442376 | tf_op jit(solution)/shard_map/ppermute | solution.py:451
  (17 other events, 90.1 us)

commit v7 on v6

--- a/solution.py
+++ b/solution.py
@@ -223,10 +223,11 @@
     for s, part in enumerate(parts):
         anomalies[s * own : (s + 1) * own] = (part - mean).astype(BF16)
     at = 0
-    for some_t, tapers in zip(anom_t, taper):
+    for some_t in anom_t:
+        rows = slice(at, at + some_t.shape[0])
         covariance = jnp.dot(some_t[...], anomalies[...], preferred_element_type=F32)
-        gain[at : at + tapers.shape[0]] = (covariance * tapers[...]).astype(BF16)
-        at += tapers.shape[0]
+        gain[rows] = (covariance * taper[rows]).astype(BF16)
+        at = rows.stop
 
 
 def posterior(gain, means, anomalies, perturbed, root, blocks, at):
@@ -237,93 +238,98 @@
         block[at] = result[s * own : (s + 1) * own].astype(BF16)
 
 
-def tapers(scales, offset, side, width, members, tile_count):
+def tapers(scales, offset, taper, members, tile_count):
+    width = taper.shape[1]
     tile = (offset[0] + lax.broadcasted_iota(jnp.int32, (1, width), 1)).astype(F32)
-    place = scalar_rows(scales)[3] + (offset[side] * tile_count).astype(F32)
-    column = jnp.broadcast_to(place, (8, place.shape[1])).T[:, 0:1]
-    near = jnp.maximum(0.0, 1.0 - jnp.abs(tile - column) / RADIUS)
-    return near * near / (members - 1)
-
-
-def prepare_body(offset, *refs, tile_count):
-    *packets, anom_t, taper = refs
+    places = [
+        scalar_rows(rows)[3] + (offset[1 + n] * tile_count).astype(F32)
+        for n, rows in enumerate(scales)
+    ]
+    obs = places[0].shape[1]
+    columns = jnp.concatenate([*places, jnp.zeros((8 - len(places), obs), F32)], axis=0).T
+    for n in range(len(places)):
+        near = jnp.maximum(0.0, 1.0 - jnp.abs(tile - columns[:, n : n + 1]) * (1.0 / RADIUS))
+        taper[n * obs : (n + 1) * obs] = near * near * (1.0 / (members - 1))
+
+
+def prepare_body(*refs):
+    *packets, anom_t = refs
     members = anom_t.shape[1]
     obs = packets[0].shape[1]
     for n, packet in enumerate(packets):
-        rows = slice(n * obs, (n + 1) * obs)
-        anom_t[rows] = packet[:members].T
-        taper[rows] = tapers(packet[members:], offset, 1 + n, taper.shape[1], members, tile_count)
-
-
-def prepare(offset, packets, width, tile_count):
+        anom_t[n * obs : (n + 1) * obs] = packet[:members].T
+
+
+def prepare(packets):
     rows, obs = packets[0].shape
     members = rows - 16
     count = len(packets)
     return pl.pallas_call(
-        functools.partial(prepare_body, tile_count=tile_count),
-        in_specs=[scalars()] + [whole()] * count,
-        out_specs=[whole()] * 2,
-        out_shape=[shape_of((count * obs, members)), shape_of((count * obs, width), F32)],
+        prepare_body,
+        in_specs=[whole()] * count,
+        out_specs=whole(),
+        out_shape=shape_of((count * obs, members)),
         compiler_params=params(4),
         name="prepare",
-    )(offset, *in_vmem(packets))
+    )(*in_vmem(packets))
 
 
 def start_body(offset, *refs, peers, tile_count):
-    far_states, far_packets = refs[:peers], refs[peers : peers + 3]
-    anom_0, taper_0, anom_2, taper_2, means, anomalies, gain, packets, rest = refs[peers + 3 : peers + 12]
-    states, arrived, near, passed = refs[peers + 12 :]
-    members, width = anomalies.shape[1:]
+    far_states, far_packets, far = refs[:peers], refs[peers : peers + 2], refs[peers + 2]
+    anom_0, anom_2, taper, means, anomalies, gain, packets, rest = refs[peers + 3 : peers + 11]
+    states, arrived, near, passed = refs[peers + 11 :]
+    members = anomalies.shape[1]
     count = gain.shape[0]
     loads = [
         pltpu.make_async_copy(far_states[s].at[:count], states.at[s], arrived.at[s])
         for s in range(peers)
     ]
     late = [
-        pltpu.make_async_copy(far_packets[n], packets.at[n], near.at[n]) for n in range(3)
+        pltpu.make_async_copy(packet, packets.at[n], near.at[n])
+        for n, packet in enumerate(far_packets)
     ]
     onward = [
         pltpu.make_async_copy(far_states[s].at[count:], rest.at[s], passed.at[s])
         for s in range(peers)
     ]
-    for load in [late[2], *loads, late[0], late[1], *onward]:
+    for load in [*late, *loads, *onward]:
         load.start()
-    late[2].wait()
-    anom_2[...] = packets[2, :members].T
-    taper_2[...] = tapers(packets[2, members:], offset, 3, width, members, tile_count)
+    anom_2[...] = far[:members].T
+    for load in late:
+        load.wait()
+    rows = packets[0, members:], packets[1, members:], far[members:]
+    tapers(rows, offset, taper, members, tile_count)
     for load in loads:
         load.wait()
     for l in range(count):
         state = [states[s, l] for s in range(peers)]
-        gains(
-            state, (anom_0, anom_2), (taper_0, taper_2), means.at[l], anomalies.at[l], gain.at[l]
-        )
-    for load in [late[0], late[1], *onward]:
+        gains(state, (anom_0, anom_2), taper, means.at[l], anomalies.at[l], gain.at[l])
+    for load in onward:
         load.wait()
 
 
-def start_gains(offset, states, packets, anom_0, taper_0, count, tile_count):
+def start_gains(offset, states, packets, anom_0, count, tile_count):
     var_count, own, width = states[0].shape
     peers = len(states)
     members = own * peers
     rows, obs = packets[0].shape
     return pl.pallas_call(
         functools.partial(start_body, peers=peers, tile_count=tile_count),
-        in_specs=[scalars()] + [anywhere()] * (peers + 3) + [whole()] * 2,
+        in_specs=[scalars()] + [anywhere()] * (peers + 2) + [whole()] * 2,
         out_specs=[whole()] * 7,
         out_shape=[
             shape_of((obs, members)),
-            shape_of((obs, width), F32),
+            shape_of((3 * obs, width), F32),
             shape_of((count, 8, width), F32),
             shape_of((count, members, width)),
             shape_of((count, 3 * obs, width)),
-            shape_of((3, rows, obs)),
+            shape_of((2, rows, obs)),
             shape_of((peers, var_count - count, own, width)),
         ],
         scratch_shapes=[
             pltpu.VMEM((peers, count, own, width), BF16),
             pltpu.SemaphoreType.DMA((peers,)),
-            pltpu.SemaphoreType.DMA((3,)),
+            pltpu.SemaphoreType.DMA((2,)),
             pltpu.SemaphoreType.DMA((peers,)),
         ],
         compiler_params=params(8),
@@ -332,29 +338,26 @@
         offset,
         in_hbm(states[0]),
         *states[1:],
-        *map(in_hbm, packets),
-        *in_vmem((anom_0, taper_0)),
+        *map(in_hbm, packets[:2]),
+        *in_vmem((packets[2], anom_0)),
     )
 
 
-def first_body(means, anomalies, gain, packets, sums, noise_0, noise_1, far_noise, *refs):
-    *blocks, perturbed, root_out, inflation_out, noise_2, arrived = refs
+def first_body(means, anomalies, gain, packets, far, sums, noise_0, noise_1, noise_2, *refs):
+    *blocks, perturbed, root_out, inflation_out = refs
     members = anomalies.shape[1]
     obs = packets.shape[2]
-    load = pltpu.make_async_copy(far_noise, noise_2, arrived)
-    load.start()
     folded = jnp.sum(sums[...], axis=0, keepdims=True)
     inflation = folded[:, 0:1] / folded[:, 1:2]
     inflation_out[0] = jnp.sum(inflation)
     root = jnp.sqrt(inflation)
     root_out[...] = jnp.broadcast_to(root, root_out.shape)
     for n, noise in enumerate((noise_0, noise_1, noise_2)):
-        if n == 2:
-            load.wait()
-        innovation, error, spread, _ = scalar_rows(packets[n, members:])
+        packet = far if n == 2 else packets.at[n]
+        innovation, error, spread, _ = scalar_rows(packet[members:])
         bottom = jnp.where(error > 0.0, inflation * spread + error, 1.0)
         factor = jnp.where(error > 0.0, inflation / bottom, 0.0)
-        dev = packets[n, :members].astype(F32)
+        dev = packet[:members].astype(F32)
         perturbed[:, n * obs : (n + 1) * obs] = (
             factor * (innovation + noise[...].astype(F32) - root * dev)
         ).astype(BF16)
@@ -370,12 +373,12 @@
     ]
 
 
-def first_updates(means, anomalies, gain, packets, sums, noises, peers):
+def first_updates(means, anomalies, gain, packets, far, sums, noises, peers):
     count, members, width = anomalies.shape
     obs = packets.shape[2]
     out = pl.pallas_call(
         first_body,
-        in_specs=[whole()] * 7 + [anywhere()],
+        in_specs=[whole()] * 9,
         out_specs=[whole()] * (peers + 2) + [scalars()],
         out_shape=[shape_of((count, members // peers, width))] * peers
         + [
@@ -383,20 +386,19 @@
             shape_of((8, 128), F32),
             jax.ShapeDtypeStruct((1,), F32),
         ],
-        scratch_shapes=[pltpu.VMEM(noises[2].shape, BF16), pltpu.SemaphoreType.DMA],
         compiler_params=params(4),
         name="first",
-    )(*in_vmem((means, anomalies, gain, packets, sums, *noises[:2])), noises[2])
+    )(*in_vmem((means, anomalies, gain, packets, far, sums, *noises)))
     return out[:peers], *out[peers:]
 
 
-def second_body(states, perturbed, root, *refs):
-    shared, (*blocks, means, anomalies, gain) = refs[:4], refs[4:]
+def second_body(states, perturbed, root, anom_0, anom_2, taper, *refs):
+    *blocks, means, anomalies, gain = refs
     peers = len(blocks)
     count = blocks[0].shape[0]
     for l in range(count):
         state = [states[s, l] for s in range(peers)]
-        gains(state, shared[:2], shared[2:], means.at[l], anomalies.at[l], gain.at[l])
+        gains(state, (anom_0, anom_2), taper, means.at[l], anomalies.at[l], gain.at[l])
     for l in range(count):
         posterior(gain.at[l], means.at[l], anomalies.at[l], perturbed, root[0:1, 0:1], blocks, l)
 
@@ -405,7 +407,7 @@
     peers, count, own, width = states.shape
     return pl.pallas_call(
         second_body,
-        in_specs=[whole()] * 7,
+        in_specs=[whole()] * 6,
         out_specs=[whole()] * peers,
         out_shape=[shape_of((count, own, width))] * peers,
         scratch_shapes=working(count, peers * own, perturbed.shape[1], width),
@@ -486,15 +488,15 @@
     far_noise = lax.ppermute(noise, "region", pairs)
     side = 1 - 2 * (region % 2)
     offset = jnp.stack([me[0] * width, jnp.zeros_like(side), side, -side])
-    anom_0, taper_0 = prepare(offset, (packet, near), width, tile_count)
+    anom_0 = prepare((packet, near))
     half = (var_count + 1) // 2
-    anom_2, taper_2, means, anomalies, gain, packets, rest = start_gains(
-        offset, states, (packet, near, far), anom_0, taper_0, half, tile_count
+    anom_2, taper, means, anomalies, gain, packets, rest = start_gains(
+        offset, states, (packet, near, far), anom_0, half, tile_count
     )
     ready, perturbed, root, inflation = first_updates(
-        means, anomalies, gain, packets, all_sums, (noise, near_noise, far_noise), peers
+        means, anomalies, gain, packets, far, all_sums, (noise, near_noise, far_noise), peers
     )
-    shared = (anom_0, anom_2, taper_0, taper_2)
+    shared = (anom_0, anom_2, taper)
     early = traded(ready, (1, 3, 2))
     ready = second_updates(rest, perturbed, root, shared)
     late = traded(ready, (1, 3, 2))

time: 103 us -> 102 us (level)
  transfers between devices with their start and end apart: 21 -> 21, of which waited for: 10 -> 10; matrix products, arithmetic and copies ran while one was open for 0% -> 0% of each run, Pallas kernels for 9% -> 8%
where the time goes in v7:
time: 102 us; the launch traced here: 101 us
  waiting for transfers between devices  36.5 us (36%)
  starting transfers between devices  36.2 us (35%)
  Pallas kernels  15.3 us (15%)
  local copies, waits for them, and re-layouts  11.7 us (11%)
    ppermute x18, waiting for transfers between devices, swapped(): return lax.ppermute(value, axis, pairs)  36.5 us
    ppermute x18, starting transfers between devices, swapped(): return lax.ppermute(value, axis, pairs)  25.4 us
    unnamed x40, local copies, waits for them, and re-layouts  11.7 us
    all_to_all x1, starting transfers between devices, exchanged(): return lax.all_to_all(blocks, axis, split_axis=0, concat_axis=0, tiled=True)  5.54 us
    pallas_call x1, Pallas kernels, start_gains(): pl.pallas_call(functools.partial(start_body, peers=peers, tile_count=tile...  4.7 us
    ppermute x1, starting transfers between devices, shards(): far_noise = lax.ppermute(noise, 'region', pairs)  3.34 us
    pallas_call x1, Pallas kernels, first_updates(): pl.pallas_call(first_body, in_specs=[whole()] * 9, out_specs=[whole()] *...  2.87 us
    pallas_call x1, Pallas kernels, second_updates(): pl.pallas_call(second_body, in_specs=[whole()] * 6, out_specs=[whole()] *...  2.4 us
  transfers between devices with their start and end apart: 21, of which 10 were waited for; matrix products, arithmetic and copies ran while one was open for 0% of the time, Pallas kernels for 8%

profile of v7, /device:TPU:96, one launch (start us, length us, event | category | flops | bytes accessed | tf_op | source)
XLA Modules:
  0.0 100.6 jit_solution(4369883667731650687)
XLA Ops:
  0.7 2.3 %pack.1 = (bf16[7,96,256]{2,1,0:T(8,128)(2,1)}, bf16[7,96,256]{2,1,0:T(8,128)(2,1)}, bf16[7,96,256]{2,1,0:T(8,128)(2,1)}, bf16[7,96,256]{2,1,0:T(8,128)(2,1)}, bf16[96,512]{1,0:T(8,128)(2,1)S(1)}) custom-call(s32[1]{0:T(128)} %bitcast.me, f32[7]{0:T(128)} %far_weights.1, bf16[7,96,1024]{2,1,0:T(8,128)(2,1)} %ensemble.1, s32[1,512]{1,0:T(1,128)} %bitcast.13), custom_call_target="tpu_custom_call" | custom-call | tf_op jit(solution)/shard_map/pack/pallas_call | solution.py:101
  3.0 3.3 %collective-permute-start.3 = (bf16[96,512]{1,0:T(8,128)(2,1)S(1)}, bf16[96,512]{1,0:T(8,128)(2,1)S(1)}, u32[]{:S(2)}, u32[]{:S(2)}) collective-permute-start(bf16[96,512]{1,0:T(8,128)(2,1)S(1)} %get-tuple-element.31.mine), channel_id=1, source_target_pairs={{0,4},{4,0},{1,5},{5,1},{2,6},{6,2},{3,7},{7,3},{8,12},{12,8},{9,1... | collective-permute-start | bytes 294920 | tf_op jit(solution)/shard_map/ppermute | solution.py:453
  6.3 2.9 %collective-permute-done.3.other = bf16[96,512]{1,0:T(8,128)(2,1)S(1)} collective-permute-done((bf16[96,512]{1,0:T(8,128)(2,1)S(1)}, bf16[96,512]{1,0:T(8,128)(2,1)S(1)}, u32[]{:S(2)}, u32[]{:S(2)}) %collective-permute-start.3) | collective-permute-done | bytes 98336 | tf_op jit(solution)/shard_map/ppermute | solution.py:453
  9.2 1.6 %collective-permute-start.4 = (bf16[96,512]{1,0:T(8,128)(2,1)S(1)}, bf16[96,512]{1,0:T(8,128)(2,1)S(1)}, u32[]{:S(2)}, u32[]{:S(2)}) collective-permute-start(bf16[96,512]{1,0:T(8,128)(2,1)S(1)} %join.1.refs_0_), channel_id=1, source_target_pairs={{0,1},{1,0},{2,3},{3,2},{4,5},{5,4},{6,7},{7,6},{8,9},{9,8},{10,11... | collective-permute-start | bytes 294920 | tf_op jit(solution)/shard_map/ppermute | solution.py:453
  10.8 2.7 %collective-permute-start.5 = (bf16[96,512]{1,0:T(8,128)(2,1)S(1)}, bf16[96,512]{1,0:T(8,128)(2,1)S(1)}, u32[]{:S(2)}, u32[]{:S(2)}) collective-permute-start(bf16[96,512]{1,0:T(8,128)(2,1)S(1)} %join.1.refs_0_), channel_id=1, source_target_pairs={{0,2},{1,3},{2,0},{3,1},{4,6},{5,7},{6,4},{7,5},{8,10},{9,11},{10,... | collective-permute-start | bytes 294920 | tf_op jit(solution)/shard_map/ppermute | solution.py:453
  14.8 2.4 %collective-permute-done.5.refs_2_ = bf16[96,512]{1,0:T(8,128)(2,1)S(1)} collective-permute-done((bf16[96,512]{1,0:T(8,128)(2,1)S(1)}, bf16[96,512]{1,0:T(8,128)(2,1)S(1)}, u32[]{:S(2)}, u32[]{:S(2)}) %collective-permute-start.5) | collective-permute-done | bytes 98336 | tf_op jit(solution)/shard_map/ppermute | solution.py:453
  17.3 2.1 %collective-permute-done.6.refs_3_ = bf16[96,512]{1,0:T(8,128)(2,1)S(1)} collective-permute-done((bf16[96,512]{1,0:T(8,128)(2,1)S(1)}, bf16[96,512]{1,0:T(8,128)(2,1)S(1)}, u32[]{:S(2)}, u32[]{:S(2)}) %collective-permute-start.6) | collective-permute-done | bytes 98336 | tf_op jit(solution)/shard_map/ppermute | solution.py:453
  20.3 2.2 %collective-permute-start.10 = (bf16[96,512]{1,0:T(8,128)(2,1)S(1)}, bf16[96,512]{1,0:T(8,128)(2,1)S(1)}, u32[]{:S(2)}, u32[]{:S(2)}) collective-permute-start(bf16[96,512]{1,0:T(8,128)(2,1)S(1)} %scale.1.refs_0_), channel_id=1, source_target_pairs={{0,2},{1,3},{2,0},{3,1},{4,6},{5,7},{6,4},{7,5},{8,10},{9,11},{10,... | collective-permute-start | bytes 294920 | tf_op jit(solution)/shard_map/ppermute | solution.py:453
  22.6 2.5 %collective-permute-start.11 = (bf16[96,512]{1,0:T(8,128)(2,1)S(1)}, bf16[96,512]{1,0:T(8,128)(2,1)S(1)}, u32[]{:S(2)}, u32[]{:S(2)}) collective-permute-start(bf16[96,512]{1,0:T(8,128)(2,1)S(1)} %scale.1.refs_0_), channel_id=1, source_target_pairs={{0,3},{1,2},{2,1},{3,0},{4,7},{5,6},{6,5},{7,4},{8,11},{9,10},{10,... | collective-permute-start | bytes 294920 | tf_op jit(solution)/shard_map/ppermute | solution.py:453
  25.1 8.6 %collective-permute-done.10.refs_2_ = bf16[96,512]{1,0:T(8,128)(2,1)S(1)} collective-permute-done((bf16[96,512]{1,0:T(8,128)(2,1)S(1)}, bf16[96,512]{1,0:T(8,128)(2,1)S(1)}, u32[]{:S(2)}, u32[]{:S(2)}) %collective-permute-start.10) | collective-permute-done | bytes 98336 | tf_op jit(solution)/shard_map/ppermute | solution.py:453
  33.7 1.9 %collective-permute-start.8 = (bf16[400,512]{1,0:T(8,128)(2,1)S(1)}, bf16[400,512]{1,0:T(8,128)(2,1)S(1)}, u32[]{:S(2)}, u32[]{:S(2)}) collective-permute-start(bf16[400,512]{1,0:T(8,128)(2,1)S(1)} %get-tuple-element.32.refs_0_.refs_4_), channel_id=1, source_target_pairs={{8,16},{24,32},{40,48},{56,64},{72,80},{88,96},{104,112},{16,8},{3... | collective-permute-start | bytes 1228808 | tf_op jit(solution)/shard_map/ppermute | solution.py:483
  36.1 3.3 %collective-permute-start.13 = (bf16[384,512]{1,0:T(8,128)(2,1)S(1)}, bf16[384,512]{1,0:T(8,128)(2,1)}, u32[]{:S(2)}, u32[]{:S(2)}) collective-permute-start(bf16[384,512]{1,0:T(8,128)(2,1)S(1)} %joinnoise.1.noise_0), channel_id=1, source_target_pairs={{8,16},{24,32},{40,48},{56,64},{72,80},{88,96},{104,112},{16,8},{3... | collective-permute-start | bytes 1179656 | tf_op jit(solution)/shard_map/ppermute | solution.py:488
  42.8 5.5 %all-to-all-start = ((f32[16,1,128]{2,1,0:T(1,128)}), f32[16,1,128]{2,1,0:T(1,128)S(1)}, u32[]{:S(2)}, u32[]{:S(2)}) async-start(f32[16,1,128]{2,1,0:T(1,128)} %bitcast.8), calls=%async_computation | async-start | bytes 16384 | tf_op jit(solution)/shard_map/all_to_all | solution.py:457
  48.7 3.9 %collective-permute-done.1.refs_2_ = bf16[7,96,256]{2,1,0:T(8,128)(2,1)S(1)} collective-permute-done((bf16[7,96,256]{2,1,0:T(8,128)(2,1)}, bf16[7,96,256]{2,1,0:T(8,128)(2,1)S(1)}, u32[]{:S(2)}, u32[]{:S(2)}) %collective-permute-start.1) | collective-permute-done | bytes 344096 | tf_op jit(solution)/shard_map/ppermute | solution.py:453
  53.3 6.8 %collective-permute-done.2.refs_3_ = bf16[7,96,256]{2,1,0:T(8,128)(2,1)S(1)} collective-permute-done((bf16[7,96,256]{2,1,0:T(8,128)(2,1)}, bf16[7,96,256]{2,1,0:T(8,128)(2,1)S(1)}, u32[]{:S(2)}, u32[]{:S(2)}) %collective-permute-start.2) | collective-permute-done | bytes 344096 | tf_op jit(solution)/shard_map/ppermute | solution.py:453
  62.8 4.7 %start.1 = (bf16[512,384]{1,0:T(8,128)(2,1)S(1)}, f32[1536,256]{1,0:T(8,128)S(1)}, f32[4,8,256]{2,1,0:T(8,128)S(1)}, bf16[4,384,256]{2,1,0:T(8,128)(2,1)S(1)}, b...) custom-call(s32[4]{0:T(128)S(1)} %pad_add_fusion.offset, ...), custom_call_target="tpu_custom_call" | custom-call | tf_op jit(solution)/shard_map/start/pallas_call | solution.py:316
  67.6 1.6 %copy-done = bf16[4,1536,256]{2,1,0:T(8,128)(2,1)} copy-done((bf16[4,1536,256]{2,1,0:T(8,128)(2,1)}, bf16[4,1536,256]{2,1,0:T(8,128)(2,1)S(1)}, u32[]{:S(2)}) %copy-start) | copy-done | bytes 3145752
  72.1 1.9 %copy-done.1 = bf16[4,1536,256]{2,1,0:T(8,128)(2,1)S(1)} copy-done((bf16[4,1536,256]{2,1,0:T(8,128)(2,1)S(1)}, bf16[4,1536,256]{2,1,0:T(8,128)(2,1)}, u32[]{:S(2)}) %copy-start.1) | copy-done | bytes 3145752
  75.1 2.9 %first.1 = (bf16[4,96,256]{2,1,0:T(8,128)(2,1)S(1)}, bf16[4,96,256]{2,1,0:T(8,128)(2,1)S(1)}, bf16[4,96,256]{2,1,0:T(8,128)(2,1)S(1)}, bf16[4,96,256]{2,1,0:T(8,...) custom-call(f32[4,8,256]{2,1,0:T(8,128)S(1)} %get-tuple-element.34.means, ...), custom_call_target="tpu_custom_call" | custom-call | tf_op jit(solution)/shard_map/first/pallas_call | solution.py:379
  78.1 3.6 %collective-permute-start.18 = (bf16[4,96,256]{2,1,0:T(8,128)(2,1)S(1)}, bf16[4,96,256]{2,1,0:T(8,128)(2,1)S(1)}, u32[]{:S(2)}, u32[]{:S(2)}) collective-permute-start(bf16[4,96,256]{2,1,0:T(8,128)(2,1)S(1)} %get-tuple-element.49), channel_id=1, source_target_pairs={{0,2},{1,3},{2,0},{3,1},{4,6},{5,7},{6,4},{7,5},{8,10},{9,11},{10,... | collective-permute-start | bytes 589832 | tf_op jit(solution)/shard_map/ppermute | solution.py:453
  82.8 2.4 %second.1 = (bf16[3,96,256]{2,1,0:T(8,128)(2,1)S(1)}, bf16[3,96,256]{2,1,0:T(8,128)(2,1)S(1)}, bf16[3,96,256]{2,1,0:T(8,128)(2,1)S(1)}, bf16[3,96,256]{2,1,0:T(8,128)(2,1)S(1)}) custom-call(bf16[4,3,96,256]{3,2,1,0:T(8,128)(2,1)S(1)} %copy-done.9, bf16[384,1536]{1,0:T(8,128)(2,1)S(1)} %get-tuple-element.39.perturbed, f32[8,128]{1,0:T(8,128)S(1)} %get-tuple-element.40.root, ...), custom_call_target="tpu_custom_call" | custom-call | tf_op jit(solution)/shard_map/second/pallas_call | solution.py:408
  85.3 3.6 %collective-permute-start.15 = (bf16[3,96,256]{2,1,0:T(8,128)(2,1)S(1)}, bf16[3,96,256]{2,1,0:T(8,128)(2,1)S(1)}, u32[]{:S(2)}, u32[]{:S(2)}) collective-permute-start(bf16[3,96,256]{2,1,0:T(8,128)(2,1)S(1)} %get-tuple-element.45), channel_id=1, source_target_pairs={{0,2},{1,3},{2,0},{3,1},{4,6},{5,7},{6,4},{7,5},{8,10},{9,11},{10,... | collective-permute-start | bytes 442376 | tf_op jit(solution)/shard_map/ppermute | solution.py:453
  90.0 1.7 %collective-permute-done.18.refs_2_ = bf16[4,96,256]{2,1,0:T(8,128)(2,1)S(1)} collective-permute-done((bf16[4,96,256]{2,1,0:T(8,128)(2,1)S(1)}, bf16[4,96,256]{2,1,0:T(8,128)(2,1)S(1)}, u32[]{:S(2)}, u32[]{:S(2)}) %collective-permute-start.18) | collective-permute-done | bytes 196640 | tf_op jit(solution)/shard_map/ppermute | solution.py:453
  91.7 6.0 %collective-permute-done.19.refs_3_ = bf16[4,96,256]{2,1,0:T(8,128)(2,1)S(1)} collective-permute-done((bf16[4,96,256]{2,1,0:T(8,128)(2,1)S(1)}, bf16[4,96,256]{2,1,0:T(8,128)(2,1)S(1)}, u32[]{:S(2)}, u32[]{:S(2)}) %collective-permute-start.19) | collective-permute-done | bytes 196640 | tf_op jit(solution)/shard_map/ppermute | solution.py:453
  (70 shorter events, 19.2 us)
Async XLA Ops:
  0.7 19.6 %copy-start.16 = (f32[96,512]{1,0:T(8,128)S(1)}, f32[96,512]{1,0:T(8,128)}, u32[]{:S(2)}) copy-start(f32[96,512]{1,0:T(8,128)} %noise.1) | copy-start | bytes 589828
  3.0 6.2 %collective-permute-start.3 = (bf16[96,512]{1,0:T(8,128)(2,1)S(1)}, bf16[96,512]{1,0:T(8,128)(2,1)S(1)}, u32[]{:S(2)}, u32[]{:S(2)}) collective-permute-start(bf16[96,512]{1,0:T(8,128)(2,1)S(1)} %get-tuple-element.31.mine), channel_id=1, source_target_pairs={{0,4},{4,0},{1,5},{5,1},{2,6},{6,2},{3,7},{7,3},{8,12},{12,8},{9,1... | collective-permute-start | bytes 294920 | tf_op jit(solution)/shard_map/ppermute | solution.py:453
  9.2 5.6 %collective-permute-start.4 = (bf16[96,512]{1,0:T(8,128)(2,1)S(1)}, bf16[96,512]{1,0:T(8,128)(2,1)S(1)}, u32[]{:S(2)}, u32[]{:S(2)}) collective-permute-start(bf16[96,512]{1,0:T(8,128)(2,1)S(1)} %join.1.refs_0_), channel_id=1, source_target_pairs={{0,1},{1,0},{2,3},{3,2},{4,5},{5,4},{6,7},{7,6},{8,9},{9,8},{10,11... | collective-permute-start | bytes 294920 | tf_op jit(solution)/shard_map/ppermute | solution.py:453
  10.8 6.5 %collective-permute-start.5 = (bf16[96,512]{1,0:T(8,128)(2,1)S(1)}, bf16[96,512]{1,0:T(8,128)(2,1)S(1)}, u32[]{:S(2)}, u32[]{:S(2)}) collective-permute-start(bf16[96,512]{1,0:T(8,128)(2,1)S(1)} %join.1.refs_0_), channel_id=1, source_target_pairs={{0,2},{1,3},{2,0},{3,1},{4,6},{5,7},{6,4},{7,5},{8,10},{9,11},{10,... | collective-permute-start | bytes 294920 | tf_op jit(solution)/shard_map/ppermute | solution.py:453
  13.5 5.8 %collective-permute-start.6 = (bf16[96,512]{1,0:T(8,128)(2,1)S(1)}, bf16[96,512]{1,0:T(8,128)(2,1)S(1)}, u32[]{:S(2)}, u32[]{:S(2)}) collective-permute-start(bf16[96,512]{1,0:T(8,128)(2,1)S(1)} %join.1.refs_0_), channel_id=1, source_target_pairs={{0,3},{1,2},{2,1},{3,0},{4,7},{5,6},{6,5},{7,4},{8,11},{9,10},{10,... | collective-permute-start | bytes 294920 | tf_op jit(solution)/shard_map/ppermute | solution.py:453
  20.3 28.4 %copy-start.2 = (bf16[400,512]{1,0:T(8,128)(2,1)}, bf16[400,512]{1,0:T(8,128)(2,1)S(1)}, u32[]{:S(2)}) copy-start(bf16[400,512]{1,0:T(8,128)(2,1)S(1)} %get-tuple-element.32.refs_0_.refs_4_) | copy-start | bytes 1228804
  20.3 21.2 %collective-permute-start.7 = (bf16[400,512]{1,0:T(8,128)(2,1)S(1)}, bf16[400,512]{1,0:T(8,128)(2,1)S(1)}, u32[]{:S(2)}, u32[]{:S(2)}) collective-permute-start(bf16[400,512]{1,0:T(8,128)(2,1)S(1)} %get-tuple-element.32.refs_0_.refs_4_), channel_id=1, source_target_pairs={{0,8},{8,0},{16,24},{24,16},{32,40},{40,32},{48,56},{56,48},{64,72... | collective-permute-start | bytes 1228808 | tf_op jit(solution)/shard_map/ppermute | solution.py:453
  20.3 19.1 %collective-permute-start = (bf16[7,96,256]{2,1,0:T(8,128)(2,1)}, bf16[7,96,256]{2,1,0:T(8,128)(2,1)S(1)}, u32[]{:S(2)}, u32[]{:S(2)}) collective-permute-start(bf16[7,96,256]{2,1,0:T(8,128)(2,1)} %get-tuple-element.28), channel_id=1, source_target_pairs={{0,1},{1,0},{2,3},{3,2},{4,5},{5,4},{6,7},{7,6},{8,9},{9,8},{10,11... | collective-permute-start | bytes 1032200 | tf_op jit(solution)/shard_map/ppermute | solution.py:453
  20.3 13.4 %collective-permute-start.10 = (bf16[96,512]{1,0:T(8,128)(2,1)S(1)}, bf16[96,512]{1,0:T(8,128)(2,1)S(1)}, u32[]{:S(2)}, u32[]{:S(2)}) collective-permute-start(bf16[96,512]{1,0:T(8,128)(2,1)S(1)} %scale.1.refs_0_), channel_id=1, source_target_pairs={{0,2},{1,3},{2,0},{3,1},{4,6},{5,7},{6,4},{7,5},{8,10},{9,11},{10,... | collective-permute-start | bytes 294920 | tf_op jit(solution)/shard_map/ppermute | solution.py:453
  22.6 13.0 %collective-permute-start.11 = (bf16[96,512]{1,0:T(8,128)(2,1)S(1)}, bf16[96,512]{1,0:T(8,128)(2,1)S(1)}, u32[]{:S(2)}, u32[]{:S(2)}) collective-permute-start(bf16[96,512]{1,0:T(8,128)(2,1)S(1)} %scale.1.refs_0_), channel_id=1, source_target_pairs={{0,3},{1,2},{2,1},{3,0},{4,7},{5,6},{6,5},{7,4},{8,11},{9,10},{10,... | collective-permute-start | bytes 294920 | tf_op jit(solution)/shard_map/ppermute | solution.py:453
  25.1 10.5 %collective-permute-start.9 = (bf16[96,512]{1,0:T(8,128)(2,1)S(1)}, bf16[96,512]{1,0:T(8,128)(2,1)S(1)}, u32[]{:S(2)}, u32[]{:S(2)}) collective-permute-start(bf16[96,512]{1,0:T(8,128)(2,1)S(1)} %scale.1.refs_0_), channel_id=1, source_target_pairs={{0,1},{1,0},{2,3},{3,2},{4,5},{5,4},{6,7},{7,6},{8,9},{9,8},{10,11... | collective-permute-start | bytes 294920 | tf_op jit(solution)/shard_map/ppermute | solution.py:453
  33.7 27.2 %collective-permute-start.8 = (bf16[400,512]{1,0:T(8,128)(2,1)S(1)}, bf16[400,512]{1,0:T(8,128)(2,1)S(1)}, u32[]{:S(2)}, u32[]{:S(2)}) collective-permute-start(bf16[400,512]{1,0:T(8,128)(2,1)S(1)} %get-tuple-element.32.refs_0_.refs_4_), channel_id=1, source_target_pairs={{8,16},{24,32},{40,48},{56,64},{72,80},{88,96},{104,112},{16,8},{3... | collective-permute-start | bytes 1228808 | tf_op jit(solution)/shard_map/ppermute | solution.py:483
  35.7 36.4 %collective-permute-start.12 = (bf16[384,512]{1,0:T(8,128)(2,1)S(1)}, bf16[384,512]{1,0:T(8,128)(2,1)}, u32[]{:S(2)}, u32[]{:S(2)}) collective-permute-start(bf16[384,512]{1,0:T(8,128)(2,1)S(1)} %joinnoise.1.noise_0), channel_id=1, source_target_pairs={{0,8},{8,0},{16,24},{24,16},{32,40},{40,32},{48,56},{56,48},{64,72... | collective-permute-start | bytes 1179656 | tf_op jit(solution)/shard_map/ppermute | solution.py:453
  36.1 36.0 %collective-permute-start.13 = (bf16[384,512]{1,0:T(8,128)(2,1)S(1)}, bf16[384,512]{1,0:T(8,128)(2,1)}, u32[]{:S(2)}, u32[]{:S(2)}) collective-permute-start(bf16[384,512]{1,0:T(8,128)(2,1)S(1)} %joinnoise.1.noise_0), channel_id=1, source_target_pairs={{8,16},{24,32},{40,48},{56,64},{72,80},{88,96},{104,112},{16,8},{3... | collective-permute-start | bytes 1179656 | tf_op jit(solution)/shard_map/ppermute | solution.py:488
  40.2 12.4 %collective-permute-start.1 = (bf16[7,96,256]{2,1,0:T(8,128)(2,1)}, bf16[7,96,256]{2,1,0:T(8,128)(2,1)S(1)}, u32[]{:S(2)}, u32[]{:S(2)}) collective-permute-start(bf16[7,96,256]{2,1,0:T(8,128)(2,1)} %get-tuple-element.29), channel_id=1, source_target_pairs={{0,2},{1,3},{2,0},{3,1},{4,6},{5,7},{6,4},{7,5},{8,10},{9,11},{10,... | collective-permute-start | bytes 1032200 | tf_op jit(solution)/shard_map/ppermute | solution.py:453
  41.5 19.3 %copy-start.3 = (bf16[400,512]{1,0:T(8,128)(2,1)}, bf16[400,512]{1,0:T(8,128)(2,1)S(1)}, u32[]{:S(2)}) copy-start(bf16[400,512]{1,0:T(8,128)(2,1)S(1)} %collective-permute-done.7.refs_1_.refs_5_) | copy-start | bytes 1228804
  41.5 18.6 %collective-permute-start.2 = (bf16[7,96,256]{2,1,0:T(8,128)(2,1)}, bf16[7,96,256]{2,1,0:T(8,128)(2,1)S(1)}, u32[]{:S(2)}, u32[]{:S(2)}) collective-permute-start(bf16[7,96,256]{2,1,0:T(8,128)(2,1)} %get-tuple-element.30), channel_id=1, source_target_pairs={{0,3},{1,2},{2,1},{3,0},{4,7},{5,6},{6,5},{7,4},{8,11},{9,10},{10,... | collective-permute-start | bytes 1032200 | tf_op jit(solution)/shard_map/ppermute | solution.py:453
  42.8 29.3 %all-to-all-start = ((f32[16,1,128]{2,1,0:T(1,128)}), f32[16,1,128]{2,1,0:T(1,128)S(1)}, u32[]{:S(2)}, u32[]{:S(2)}) async-start(f32[16,1,128]{2,1,0:T(1,128)} %bitcast.8), calls=%async_computation | async-start | bytes 16384 | tf_op jit(solution)/shard_map/all_to_all | solution.py:457
  78.0 10.9 %collective-permute-start.17 = (bf16[4,96,256]{2,1,0:T(8,128)(2,1)S(1)}, bf16[4,96,256]{2,1,0:T(8,128)(2,1)S(1)}, u32[]{:S(2)}, u32[]{:S(2)}) collective-permute-start(bf16[4,96,256]{2,1,0:T(8,128)(2,1)S(1)} %get-tuple-element.48), channel_id=1, source_target_pairs={{0,1},{1,0},{2,3},{3,2},{4,5},{5,4},{6,7},{7,6},{8,9},{9,8},{10,11... | collective-permute-start | bytes 589832 | tf_op jit(solution)/shard_map/ppermute | solution.py:453
  78.1 13.6 %collective-permute-start.18 = (bf16[4,96,256]{2,1,0:T(8,128)(2,1)S(1)}, bf16[4,96,256]{2,1,0:T(8,128)(2,1)S(1)}, u32[]{:S(2)}, u32[]{:S(2)}) collective-permute-start(bf16[4,96,256]{2,1,0:T(8,128)(2,1)S(1)} %get-tuple-element.49), channel_id=1, source_target_pairs={{0,2},{1,3},{2,0},{3,1},{4,6},{5,7},{6,4},{7,5},{8,10},{9,11},{10,... | collective-permute-start | bytes 589832 | tf_op jit(solution)/shard_map/ppermute | solution.py:453
  81.7 16.0 %collective-permute-start.19 = (bf16[4,96,256]{2,1,0:T(8,128)(2,1)S(1)}, bf16[4,96,256]{2,1,0:T(8,128)(2,1)S(1)}, u32[]{:S(2)}, u32[]{:S(2)}) collective-permute-start(bf16[4,96,256]{2,1,0:T(8,128)(2,1)S(1)} %get-tuple-element.50), channel_id=1, source_target_pairs={{0,3},{1,2},{2,1},{3,0},{4,7},{5,6},{6,5},{7,4},{8,11},{9,10},{10,... | collective-permute-start | bytes 589832 | tf_op jit(solution)/shard_map/ppermute | solution.py:453
  85.2 13.4 %collective-permute-start.14 = (bf16[3,96,256]{2,1,0:T(8,128)(2,1)S(1)}, bf16[3,96,256]{2,1,0:T(8,128)(2,1)S(1)}, u32[]{:S(2)}, u32[]{:S(2)}) collective-permute-start(bf16[3,96,256]{2,1,0:T(8,128)(2,1)S(1)} %get-tuple-element.44), channel_id=1, source_target_pairs={{0,1},{1,0},{2,3},{3,2},{4,5},{5,4},{6,7},{7,6},{8,9},{9,8},{10,11... | collective-permute-start | bytes 442376 | tf_op jit(solution)/shard_map/ppermute | solution.py:453
  85.3 13.3 %collective-permute-start.15 = (bf16[3,96,256]{2,1,0:T(8,128)(2,1)S(1)}, bf16[3,96,256]{2,1,0:T(8,128)(2,1)S(1)}, u32[]{:S(2)}, u32[]{:S(2)}) collective-permute-start(bf16[3,96,256]{2,1,0:T(8,128)(2,1)S(1)} %get-tuple-element.45), channel_id=1, source_target_pairs={{0,2},{1,3},{2,0},{3,1},{4,6},{5,7},{6,4},{7,5},{8,10},{9,11},{10,... | collective-permute-start | bytes 442376 | tf_op jit(solution)/shard_map/ppermute | solution.py:453
  88.9 10.9 %collective-permute-start.16 = (bf16[3,96,256]{2,1,0:T(8,128)(2,1)S(1)}, bf16[3,96,256]{2,1,0:T(8,128)(2,1)S(1)}, u32[]{:S(2)}, u32[]{:S(2)}) collective-permute-start(bf16[3,96,256]{2,1,0:T(8,128)(2,1)S(1)} %get-tuple-element.46), channel_id=1, source_target_pairs={{0,3},{1,2},{2,1},{3,0},{4,7},{5,6},{6,5},{7,4},{8,11},{9,10},{10,... | collective-permute-start | bytes 442376 | tf_op jit(solution)/shard_map/ppermute | solution.py:453
  (17 other events, 95.7 us)

commit v8 on v7

--- a/solution.py
+++ b/solution.py
@@ -284,18 +284,22 @@
         pltpu.make_async_copy(far_states[s].at[:count], states.at[s], arrived.at[s])
         for s in range(peers)
     ]
+    light = [
+        pltpu.make_async_copy(packet.at[members:], packets.at[n, members:], near.at[n])
+        for n, packet in enumerate(far_packets)
+    ]
     late = [
-        pltpu.make_async_copy(packet, packets.at[n], near.at[n])
+        pltpu.make_async_copy(packet.at[:members], packets.at[n, :members], near.at[2 + n])
         for n, packet in enumerate(far_packets)
     ]
     onward = [
         pltpu.make_async_copy(far_states[s].at[count:], rest.at[s], passed.at[s])
         for s in range(peers)
     ]
-    for load in [*late, *loads, *onward]:
+    for load in [*light, *loads, *late, *onward]:
         load.start()
     anom_2[...] = far[:members].T
-    for load in late:
+    for load in light:
         load.wait()
     rows = packets[0, members:], packets[1, members:], far[members:]
     tapers(rows, offset, taper, members, tile_count)
@@ -304,7 +308,7 @@
     for l in range(count):
         state = [states[s, l] for s in range(peers)]
         gains(state, (anom_0, anom_2), taper, means.at[l], anomalies.at[l], gain.at[l])
-    for load in onward:
+    for load in [*late, *onward]:
         load.wait()
 
 
@@ -329,7 +333,7 @@
         scratch_shapes=[
             pltpu.VMEM((peers, count, own, width), BF16),
             pltpu.SemaphoreType.DMA((peers,)),
-            pltpu.SemaphoreType.DMA((2,)),
+            pltpu.SemaphoreType.DMA((4,)),
             pltpu.SemaphoreType.DMA((peers,)),
         ],
         compiler_params=params(8),

time: 102 us -> 102 us (level)
  no operation moved by 1% of the time
where the time goes in v8:
time: 102 us; the launch traced here: 101 us
  waiting for transfers between devices  36.5 us (36%)
  starting transfers between devices  36.2 us (35%)
  Pallas kernels  15.3 us (15%)
  local copies, waits for them, and re-layouts  11.7 us (11%)
    ppermute x18, waiting for transfers between devices, swapped(): return lax.ppermute(value, axis, pairs)  36.5 us
    ppermute x18, starting transfers between devices, swapped(): return lax.ppermute(value, axis, pairs)  25.4 us
    unnamed x40, local copies, waits for them, and re-layouts  11.7 us
    all_to_all x1, starting transfers between devices, exchanged(): return lax.all_to_all(blocks, axis, split_axis=0, concat_axis=0, tiled=True)  5.54 us
    pallas_call x1, Pallas kernels, start_gains(): pl.pallas_call(functools.partial(start_body, peers=peers, tile_count=tile...  4.72 us
    ppermute x1, starting transfers between devices, shards(): far_noise = lax.ppermute(noise, 'region', pairs)  3.34 us
    pallas_call x1, Pallas kernels, first_updates(): pl.pallas_call(first_body, in_specs=[whole()] * 9, out_specs=[whole()] *...  2.86 us
    pallas_call x1, Pallas kernels, second_updates(): pl.pallas_call(second_body, in_specs=[whole()] * 6, out_specs=[whole()] *...  2.4 us
  transfers between devices with their start and end apart: 21, of which 10 were waited for; matrix products, arithmetic and copies ran while one was open for 0% of the time, Pallas kernels for 8%

profile of v8, /device:TPU:96, one launch (start us, length us, event | category | flops | bytes accessed | tf_op | source)
XLA Modules:
  0.0 100.6 jit_solution(18430490583392514213)
XLA Ops:
  0.7 2.3 %pack.1 = (bf16[7,96,256]{2,1,0:T(8,128)(2,1)}, bf16[7,96,256]{2,1,0:T(8,128)(2,1)}, bf16[7,96,256]{2,1,0:T(8,128)(2,1)}, bf16[7,96,256]{2,1,0:T(8,128)(2,1)}, bf16[96,512]{1,0:T(8,128)(2,1)S(1)}) custom-call(s32[1]{0:T(128)} %bitcast.me, f32[7]{0:T(128)} %far_weights.1, bf16[7,96,1024]{2,1,0:T(8,128)(2,1)} %ensemble.1, s32[1,512]{1,0:T(1,128)} %bitcast.13), custom_call_target="tpu_custom_call" | custom-call | tf_op jit(solution)/shard_map/pack/pallas_call | solution.py:101
  3.0 3.3 %collective-permute-start.3 = (bf16[96,512]{1,0:T(8,128)(2,1)S(1)}, bf16[96,512]{1,0:T(8,128)(2,1)S(1)}, u32[]{:S(2)}, u32[]{:S(2)}) collective-permute-start(bf16[96,512]{1,0:T(8,128)(2,1)S(1)} %get-tuple-element.31.mine), channel_id=1, source_target_pairs={{0,4},{4,0},{1,5},{5,1},{2,6},{6,2},{3,7},{7,3},{8,12},{12,8},{9,1... | collective-permute-start | bytes 294920 | tf_op jit(solution)/shard_map/ppermute | solution.py:457
  6.3 2.9 %collective-permute-done.3.other = bf16[96,512]{1,0:T(8,128)(2,1)S(1)} collective-permute-done((bf16[96,512]{1,0:T(8,128)(2,1)S(1)}, bf16[96,512]{1,0:T(8,128)(2,1)S(1)}, u32[]{:S(2)}, u32[]{:S(2)}) %collective-permute-start.3) | collective-permute-done | bytes 98336 | tf_op jit(solution)/shard_map/ppermute | solution.py:457
  9.2 1.6 %collective-permute-start.4 = (bf16[96,512]{1,0:T(8,128)(2,1)S(1)}, bf16[96,512]{1,0:T(8,128)(2,1)S(1)}, u32[]{:S(2)}, u32[]{:S(2)}) collective-permute-start(bf16[96,512]{1,0:T(8,128)(2,1)S(1)} %join.1.refs_0_), channel_id=1, source_target_pairs={{0,1},{1,0},{2,3},{3,2},{4,5},{5,4},{6,7},{7,6},{8,9},{9,8},{10,11... | collective-permute-start | bytes 294920 | tf_op jit(solution)/shard_map/ppermute | solution.py:457
  10.8 2.7 %collective-permute-start.5 = (bf16[96,512]{1,0:T(8,128)(2,1)S(1)}, bf16[96,512]{1,0:T(8,128)(2,1)S(1)}, u32[]{:S(2)}, u32[]{:S(2)}) collective-permute-start(bf16[96,512]{1,0:T(8,128)(2,1)S(1)} %join.1.refs_0_), channel_id=1, source_target_pairs={{0,2},{1,3},{2,0},{3,1},{4,6},{5,7},{6,4},{7,5},{8,10},{9,11},{10,... | collective-permute-start | bytes 294920 | tf_op jit(solution)/shard_map/ppermute | solution.py:457
  14.8 2.4 %collective-permute-done.5.refs_2_ = bf16[96,512]{1,0:T(8,128)(2,1)S(1)} collective-permute-done((bf16[96,512]{1,0:T(8,128)(2,1)S(1)}, bf16[96,512]{1,0:T(8,128)(2,1)S(1)}, u32[]{:S(2)}, u32[]{:S(2)}) %collective-permute-start.5) | collective-permute-done | bytes 98336 | tf_op jit(solution)/shard_map/ppermute | solution.py:457
  17.3 2.1 %collective-permute-done.6.refs_3_ = bf16[96,512]{1,0:T(8,128)(2,1)S(1)} collective-permute-done((bf16[96,512]{1,0:T(8,128)(2,1)S(1)}, bf16[96,512]{1,0:T(8,128)(2,1)S(1)}, u32[]{:S(2)}, u32[]{:S(2)}) %collective-permute-start.6) | collective-permute-done | bytes 98336 | tf_op jit(solution)/shard_map/ppermute | solution.py:457
  20.3 2.2 %collective-permute-start.10 = (bf16[96,512]{1,0:T(8,128)(2,1)S(1)}, bf16[96,512]{1,0:T(8,128)(2,1)S(1)}, u32[]{:S(2)}, u32[]{:S(2)}) collective-permute-start(bf16[96,512]{1,0:T(8,128)(2,1)S(1)} %scale.1.refs_0_), channel_id=1, source_target_pairs={{0,2},{1,3},{2,0},{3,1},{4,6},{5,7},{6,4},{7,5},{8,10},{9,11},{10,... | collective-permute-start | bytes 294920 | tf_op jit(solution)/shard_map/ppermute | solution.py:457
  22.6 2.5 %collective-permute-start.11 = (bf16[96,512]{1,0:T(8,128)(2,1)S(1)}, bf16[96,512]{1,0:T(8,128)(2,1)S(1)}, u32[]{:S(2)}, u32[]{:S(2)}) collective-permute-start(bf16[96,512]{1,0:T(8,128)(2,1)S(1)} %scale.1.refs_0_), channel_id=1, source_target_pairs={{0,3},{1,2},{2,1},{3,0},{4,7},{5,6},{6,5},{7,4},{8,11},{9,10},{10,... | collective-permute-start | bytes 294920 | tf_op jit(solution)/shard_map/ppermute | solution.py:457
  25.1 8.6 %collective-permute-done.10.refs_2_ = bf16[96,512]{1,0:T(8,128)(2,1)S(1)} collective-permute-done((bf16[96,512]{1,0:T(8,128)(2,1)S(1)}, bf16[96,512]{1,0:T(8,128)(2,1)S(1)}, u32[]{:S(2)}, u32[]{:S(2)}) %collective-permute-start.10) | collective-permute-done | bytes 98336 | tf_op jit(solution)/shard_map/ppermute | solution.py:457
  33.7 1.9 %collective-permute-start.8 = (bf16[400,512]{1,0:T(8,128)(2,1)S(1)}, bf16[400,512]{1,0:T(8,128)(2,1)S(1)}, u32[]{:S(2)}, u32[]{:S(2)}) collective-permute-start(bf16[400,512]{1,0:T(8,128)(2,1)S(1)} %get-tuple-element.32.refs_0_.refs_4_), channel_id=1, source_target_pairs={{8,16},{24,32},{40,48},{56,64},{72,80},{88,96},{104,112},{16,8},{3... | collective-permute-start | bytes 1228808 | tf_op jit(solution)/shard_map/ppermute | solution.py:487
  36.1 3.3 %collective-permute-start.13 = (bf16[384,512]{1,0:T(8,128)(2,1)S(1)}, bf16[384,512]{1,0:T(8,128)(2,1)}, u32[]{:S(2)}, u32[]{:S(2)}) collective-permute-start(bf16[384,512]{1,0:T(8,128)(2,1)S(1)} %joinnoise.1.noise_0), channel_id=1, source_target_pairs={{8,16},{24,32},{40,48},{56,64},{72,80},{88,96},{104,112},{16,8},{3... | collective-permute-start | bytes 1179656 | tf_op jit(solution)/shard_map/ppermute | solution.py:492
  42.8 5.5 %all-to-all-start = ((f32[16,1,128]{2,1,0:T(1,128)}), f32[16,1,128]{2,1,0:T(1,128)S(1)}, u32[]{:S(2)}, u32[]{:S(2)}) async-start(f32[16,1,128]{2,1,0:T(1,128)} %bitcast.8), calls=%async_computation | async-start | bytes 16384 | tf_op jit(solution)/shard_map/all_to_all | solution.py:461
  48.7 3.9 %collective-permute-done.1.refs_2_ = bf16[7,96,256]{2,1,0:T(8,128)(2,1)S(1)} collective-permute-done((bf16[7,96,256]{2,1,0:T(8,128)(2,1)}, bf16[7,96,256]{2,1,0:T(8,128)(2,1)S(1)}, u32[]{:S(2)}, u32[]{:S(2)}) %collective-permute-start.1) | collective-permute-done | bytes 344096 | tf_op jit(solution)/shard_map/ppermute | solution.py:457
  53.3 6.8 %collective-permute-done.2.refs_3_ = bf16[7,96,256]{2,1,0:T(8,128)(2,1)S(1)} collective-permute-done((bf16[7,96,256]{2,1,0:T(8,128)(2,1)}, bf16[7,96,256]{2,1,0:T(8,128)(2,1)S(1)}, u32[]{:S(2)}, u32[]{:S(2)}) %collective-permute-start.2) | collective-permute-done | bytes 344096 | tf_op jit(solution)/shard_map/ppermute | solution.py:457
  62.8 4.7 %start.1 = (bf16[512,384]{1,0:T(8,128)(2,1)S(1)}, f32[1536,256]{1,0:T(8,128)S(1)}, f32[4,8,256]{2,1,0:T(8,128)S(1)}, bf16[4,384,256]{2,1,0:T(8,128)(2,1)S(1)}, b...) custom-call(s32[4]{0:T(128)S(1)} %pad_add_fusion.offset, ...), custom_call_target="tpu_custom_call" | custom-call | tf_op jit(solution)/shard_map/start/pallas_call | solution.py:320
  67.6 1.6 %copy-done = bf16[4,1536,256]{2,1,0:T(8,128)(2,1)} copy-done((bf16[4,1536,256]{2,1,0:T(8,128)(2,1)}, bf16[4,1536,256]{2,1,0:T(8,128)(2,1)S(1)}, u32[]{:S(2)}) %copy-start) | copy-done | bytes 3145752
  72.1 1.9 %copy-done.1 = bf16[4,1536,256]{2,1,0:T(8,128)(2,1)S(1)} copy-done((bf16[4,1536,256]{2,1,0:T(8,128)(2,1)S(1)}, bf16[4,1536,256]{2,1,0:T(8,128)(2,1)}, u32[]{:S(2)}) %copy-start.1) | copy-done | bytes 3145752
  75.1 2.9 %first.1 = (bf16[4,96,256]{2,1,0:T(8,128)(2,1)S(1)}, bf16[4,96,256]{2,1,0:T(8,128)(2,1)S(1)}, bf16[4,96,256]{2,1,0:T(8,128)(2,1)S(1)}, bf16[4,96,256]{2,1,0:T(8,...) custom-call(f32[4,8,256]{2,1,0:T(8,128)S(1)} %get-tuple-element.34.means, ...), custom_call_target="tpu_custom_call" | custom-call | tf_op jit(solution)/shard_map/first/pallas_call | solution.py:383
  78.1 3.6 %collective-permute-start.18 = (bf16[4,96,256]{2,1,0:T(8,128)(2,1)S(1)}, bf16[4,96,256]{2,1,0:T(8,128)(2,1)S(1)}, u32[]{:S(2)}, u32[]{:S(2)}) collective-permute-start(bf16[4,96,256]{2,1,0:T(8,128)(2,1)S(1)} %get-tuple-element.49), channel_id=1, source_target_pairs={{0,2},{1,3},{2,0},{3,1},{4,6},{5,7},{6,4},{7,5},{8,10},{9,11},{10,... | collective-permute-start | bytes 589832 | tf_op jit(solution)/shard_map/ppermute | solution.py:457
  82.8 2.4 %second.1 = (bf16[3,96,256]{2,1,0:T(8,128)(2,1)S(1)}, bf16[3,96,256]{2,1,0:T(8,128)(2,1)S(1)}, bf16[3,96,256]{2,1,0:T(8,128)(2,1)S(1)}, bf16[3,96,256]{2,1,0:T(8,128)(2,1)S(1)}) custom-call(bf16[4,3,96,256]{3,2,1,0:T(8,128)(2,1)S(1)} %copy-done.9, bf16[384,1536]{1,0:T(8,128)(2,1)S(1)} %get-tuple-element.39.perturbed, f32[8,128]{1,0:T(8,128)S(1)} %get-tuple-element.40.root, ...), custom_call_target="tpu_custom_call" | custom-call | tf_op jit(solution)/shard_map/second/pallas_call | solution.py:412
  85.3 3.6 %collective-permute-start.15 = (bf16[3,96,256]{2,1,0:T(8,128)(2,1)S(1)}, bf16[3,96,256]{2,1,0:T(8,128)(2,1)S(1)}, u32[]{:S(2)}, u32[]{:S(2)}) collective-permute-start(bf16[3,96,256]{2,1,0:T(8,128)(2,1)S(1)} %get-tuple-element.45), channel_id=1, source_target_pairs={{0,2},{1,3},{2,0},{3,1},{4,6},{5,7},{6,4},{7,5},{8,10},{9,11},{10,... | collective-permute-start | bytes 442376 | tf_op jit(solution)/shard_map/ppermute | solution.py:457
  90.0 1.7 %collective-permute-done.18.refs_2_ = bf16[4,96,256]{2,1,0:T(8,128)(2,1)S(1)} collective-permute-done((bf16[4,96,256]{2,1,0:T(8,128)(2,1)S(1)}, bf16[4,96,256]{2,1,0:T(8,128)(2,1)S(1)}, u32[]{:S(2)}, u32[]{:S(2)}) %collective-permute-start.18) | collective-permute-done | bytes 196640 | tf_op jit(solution)/shard_map/ppermute | solution.py:457
  91.7 6.0 %collective-permute-done.19.refs_3_ = bf16[4,96,256]{2,1,0:T(8,128)(2,1)S(1)} collective-permute-done((bf16[4,96,256]{2,1,0:T(8,128)(2,1)S(1)}, bf16[4,96,256]{2,1,0:T(8,128)(2,1)S(1)}, u32[]{:S(2)}, u32[]{:S(2)}) %collective-permute-start.19) | collective-permute-done | bytes 196640 | tf_op jit(solution)/shard_map/ppermute | solution.py:457
  (70 shorter events, 19.2 us)
Async XLA Ops:
  0.7 19.6 %copy-start.16 = (f32[96,512]{1,0:T(8,128)S(1)}, f32[96,512]{1,0:T(8,128)}, u32[]{:S(2)}) copy-start(f32[96,512]{1,0:T(8,128)} %noise.1) | copy-start | bytes 589828
  3.0 6.2 %collective-permute-start.3 = (bf16[96,512]{1,0:T(8,128)(2,1)S(1)}, bf16[96,512]{1,0:T(8,128)(2,1)S(1)}, u32[]{:S(2)}, u32[]{:S(2)}) collective-permute-start(bf16[96,512]{1,0:T(8,128)(2,1)S(1)} %get-tuple-element.31.mine), channel_id=1, source_target_pairs={{0,4},{4,0},{1,5},{5,1},{2,6},{6,2},{3,7},{7,3},{8,12},{12,8},{9,1... | collective-permute-start | bytes 294920 | tf_op jit(solution)/shard_map/ppermute | solution.py:457
  9.2 5.6 %collective-permute-start.4 = (bf16[96,512]{1,0:T(8,128)(2,1)S(1)}, bf16[96,512]{1,0:T(8,128)(2,1)S(1)}, u32[]{:S(2)}, u32[]{:S(2)}) collective-permute-start(bf16[96,512]{1,0:T(8,128)(2,1)S(1)} %join.1.refs_0_), channel_id=1, source_target_pairs={{0,1},{1,0},{2,3},{3,2},{4,5},{5,4},{6,7},{7,6},{8,9},{9,8},{10,11... | collective-permute-start | bytes 294920 | tf_op jit(solution)/shard_map/ppermute | solution.py:457
  10.8 6.5 %collective-permute-start.5 = (bf16[96,512]{1,0:T(8,128)(2,1)S(1)}, bf16[96,512]{1,0:T(8,128)(2,1)S(1)}, u32[]{:S(2)}, u32[]{:S(2)}) collective-permute-start(bf16[96,512]{1,0:T(8,128)(2,1)S(1)} %join.1.refs_0_), channel_id=1, source_target_pairs={{0,2},{1,3},{2,0},{3,1},{4,6},{5,7},{6,4},{7,5},{8,10},{9,11},{10,... | collective-permute-start | bytes 294920 | tf_op jit(solution)/shard_map/ppermute | solution.py:457
  13.5 5.8 %collective-permute-start.6 = (bf16[96,512]{1,0:T(8,128)(2,1)S(1)}, bf16[96,512]{1,0:T(8,128)(2,1)S(1)}, u32[]{:S(2)}, u32[]{:S(2)}) collective-permute-start(bf16[96,512]{1,0:T(8,128)(2,1)S(1)} %join.1.refs_0_), channel_id=1, source_target_pairs={{0,3},{1,2},{2,1},{3,0},{4,7},{5,6},{6,5},{7,4},{8,11},{9,10},{10,... | collective-permute-start | bytes 294920 | tf_op jit(solution)/shard_map/ppermute | solution.py:457
  20.3 28.4 %copy-start.2 = (bf16[400,512]{1,0:T(8,128)(2,1)}, bf16[400,512]{1,0:T(8,128)(2,1)S(1)}, u32[]{:S(2)}) copy-start(bf16[400,512]{1,0:T(8,128)(2,1)S(1)} %get-tuple-element.32.refs_0_.refs_4_) | copy-start | bytes 1228804
  20.3 21.2 %collective-permute-start.7 = (bf16[400,512]{1,0:T(8,128)(2,1)S(1)}, bf16[400,512]{1,0:T(8,128)(2,1)S(1)}, u32[]{:S(2)}, u32[]{:S(2)}) collective-permute-start(bf16[400,512]{1,0:T(8,128)(2,1)S(1)} %get-tuple-element.32.refs_0_.refs_4_), channel_id=1, source_target_pairs={{0,8},{8,0},{16,24},{24,16},{32,40},{40,32},{48,56},{56,48},{64,72... | collective-permute-start | bytes 1228808 | tf_op jit(solution)/shard_map/ppermute | solution.py:457
  20.3 19.1 %collective-permute-start = (bf16[7,96,256]{2,1,0:T(8,128)(2,1)}, bf16[7,96,256]{2,1,0:T(8,128)(2,1)S(1)}, u32[]{:S(2)}, u32[]{:S(2)}) collective-permute-start(bf16[7,96,256]{2,1,0:T(8,128)(2,1)} %get-tuple-element.28), channel_id=1, source_target_pairs={{0,1},{1,0},{2,3},{3,2},{4,5},{5,4},{6,7},{7,6},{8,9},{9,8},{10,11... | collective-permute-start | bytes 1032200 | tf_op jit(solution)/shard_map/ppermute | solution.py:457
  20.3 13.4 %collective-permute-start.10 = (bf16[96,512]{1,0:T(8,128)(2,1)S(1)}, bf16[96,512]{1,0:T(8,128)(2,1)S(1)}, u32[]{:S(2)}, u32[]{:S(2)}) collective-permute-start(bf16[96,512]{1,0:T(8,128)(2,1)S(1)} %scale.1.refs_0_), channel_id=1, source_target_pairs={{0,2},{1,3},{2,0},{3,1},{4,6},{5,7},{6,4},{7,5},{8,10},{9,11},{10,... | collective-permute-start | bytes 294920 | tf_op jit(solution)/shard_map/ppermute | solution.py:457
  22.6 13.0 %collective-permute-start.11 = (bf16[96,512]{1,0:T(8,128)(2,1)S(1)}, bf16[96,512]{1,0:T(8,128)(2,1)S(1)}, u32[]{:S(2)}, u32[]{:S(2)}) collective-permute-start(bf16[96,512]{1,0:T(8,128)(2,1)S(1)} %scale.1.refs_0_), channel_id=1, source_target_pairs={{0,3},{1,2},{2,1},{3,0},{4,7},{5,6},{6,5},{7,4},{8,11},{9,10},{10,... | collective-permute-start | bytes 294920 | tf_op jit(solution)/shard_map/ppermute | solution.py:457
  25.1 10.5 %collective-permute-start.9 = (bf16[96,512]{1,0:T(8,128)(2,1)S(1)}, bf16[96,512]{1,0:T(8,128)(2,1)S(1)}, u32[]{:S(2)}, u32[]{:S(2)}) collective-permute-start(bf16[96,512]{1,0:T(8,128)(2,1)S(1)} %scale.1.refs_0_), channel_id=1, source_target_pairs={{0,1},{1,0},{2,3},{3,2},{4,5},{5,4},{6,7},{7,6},{8,9},{9,8},{10,11... | collective-permute-start | bytes 294920 | tf_op jit(solution)/shard_map/ppermute | solution.py:457
  33.7 27.2 %collective-permute-start.8 = (bf16[400,512]{1,0:T(8,128)(2,1)S(1)}, bf16[400,512]{1,0:T(8,128)(2,1)S(1)}, u32[]{:S(2)}, u32[]{:S(2)}) collective-permute-start(bf16[400,512]{1,0:T(8,128)(2,1)S(1)} %get-tuple-element.32.refs_0_.refs_4_), channel_id=1, source_target_pairs={{8,16},{24,32},{40,48},{56,64},{72,80},{88,96},{104,112},{16,8},{3... | collective-permute-start | bytes 1228808 | tf_op jit(solution)/shard_map/ppermute | solution.py:487
  35.7 36.4 %collective-permute-start.12 = (bf16[384,512]{1,0:T(8,128)(2,1)S(1)}, bf16[384,512]{1,0:T(8,128)(2,1)}, u32[]{:S(2)}, u32[]{:S(2)}) collective-permute-start(bf16[384,512]{1,0:T(8,128)(2,1)S(1)} %joinnoise.1.noise_0), channel_id=1, source_target_pairs={{0,8},{8,0},{16,24},{24,16},{32,40},{40,32},{48,56},{56,48},{64,72... | collective-permute-start | bytes 1179656 | tf_op jit(solution)/shard_map/ppermute | solution.py:457
  36.1 36.0 %collective-permute-start.13 = (bf16[384,512]{1,0:T(8,128)(2,1)S(1)}, bf16[384,512]{1,0:T(8,128)(2,1)}, u32[]{:S(2)}, u32[]{:S(2)}) collective-permute-start(bf16[384,512]{1,0:T(8,128)(2,1)S(1)} %joinnoise.1.noise_0), channel_id=1, source_target_pairs={{8,16},{24,32},{40,48},{56,64},{72,80},{88,96},{104,112},{16,8},{3... | collective-permute-start | bytes 1179656 | tf_op jit(solution)/shard_map/ppermute | solution.py:492
  40.2 12.4 %collective-permute-start.1 = (bf16[7,96,256]{2,1,0:T(8,128)(2,1)}, bf16[7,96,256]{2,1,0:T(8,128)(2,1)S(1)}, u32[]{:S(2)}, u32[]{:S(2)}) collective-permute-start(bf16[7,96,256]{2,1,0:T(8,128)(2,1)} %get-tuple-element.29), channel_id=1, source_target_pairs={{0,2},{1,3},{2,0},{3,1},{4,6},{5,7},{6,4},{7,5},{8,10},{9,11},{10,... | collective-permute-start | bytes 1032200 | tf_op jit(solution)/shard_map/ppermute | solution.py:457
  41.5 19.3 %copy-start.3 = (bf16[400,512]{1,0:T(8,128)(2,1)}, bf16[400,512]{1,0:T(8,128)(2,1)S(1)}, u32[]{:S(2)}) copy-start(bf16[400,512]{1,0:T(8,128)(2,1)S(1)} %collective-permute-done.7.refs_1_.refs_5_) | copy-start | bytes 1228804
  41.5 18.6 %collective-permute-start.2 = (bf16[7,96,256]{2,1,0:T(8,128)(2,1)}, bf16[7,96,256]{2,1,0:T(8,128)(2,1)S(1)}, u32[]{:S(2)}, u32[]{:S(2)}) collective-permute-start(bf16[7,96,256]{2,1,0:T(8,128)(2,1)} %get-tuple-element.30), channel_id=1, source_target_pairs={{0,3},{1,2},{2,1},{3,0},{4,7},{5,6},{6,5},{7,4},{8,11},{9,10},{10,... | collective-permute-start | bytes 1032200 | tf_op jit(solution)/shard_map/ppermute | solution.py:457
  42.8 29.3 %all-to-all-start = ((f32[16,1,128]{2,1,0:T(1,128)}), f32[16,1,128]{2,1,0:T(1,128)S(1)}, u32[]{:S(2)}, u32[]{:S(2)}) async-start(f32[16,1,128]{2,1,0:T(1,128)} %bitcast.8), calls=%async_computation | async-start | bytes 16384 | tf_op jit(solution)/shard_map/all_to_all | solution.py:461
  78.0 10.9 %collective-permute-start.17 = (bf16[4,96,256]{2,1,0:T(8,128)(2,1)S(1)}, bf16[4,96,256]{2,1,0:T(8,128)(2,1)S(1)}, u32[]{:S(2)}, u32[]{:S(2)}) collective-permute-start(bf16[4,96,256]{2,1,0:T(8,128)(2,1)S(1)} %get-tuple-element.48), channel_id=1, source_target_pairs={{0,1},{1,0},{2,3},{3,2},{4,5},{5,4},{6,7},{7,6},{8,9},{9,8},{10,11... | collective-permute-start | bytes 589832 | tf_op jit(solution)/shard_map/ppermute | solution.py:457
  78.1 13.6 %collective-permute-start.18 = (bf16[4,96,256]{2,1,0:T(8,128)(2,1)S(1)}, bf16[4,96,256]{2,1,0:T(8,128)(2,1)S(1)}, u32[]{:S(2)}, u32[]{:S(2)}) collective-permute-start(bf16[4,96,256]{2,1,0:T(8,128)(2,1)S(1)} %get-tuple-element.49), channel_id=1, source_target_pairs={{0,2},{1,3},{2,0},{3,1},{4,6},{5,7},{6,4},{7,5},{8,10},{9,11},{10,... | collective-permute-start | bytes 589832 | tf_op jit(solution)/shard_map/ppermute | solution.py:457
  81.7 16.0 %collective-permute-start.19 = (bf16[4,96,256]{2,1,0:T(8,128)(2,1)S(1)}, bf16[4,96,256]{2,1,0:T(8,128)(2,1)S(1)}, u32[]{:S(2)}, u32[]{:S(2)}) collective-permute-start(bf16[4,96,256]{2,1,0:T(8,128)(2,1)S(1)} %get-tuple-element.50), channel_id=1, source_target_pairs={{0,3},{1,2},{2,1},{3,0},{4,7},{5,6},{6,5},{7,4},{8,11},{9,10},{10,... | collective-permute-start | bytes 589832 | tf_op jit(solution)/shard_map/ppermute | solution.py:457
  85.2 13.4 %collective-permute-start.14 = (bf16[3,96,256]{2,1,0:T(8,128)(2,1)S(1)}, bf16[3,96,256]{2,1,0:T(8,128)(2,1)S(1)}, u32[]{:S(2)}, u32[]{:S(2)}) collective-permute-start(bf16[3,96,256]{2,1,0:T(8,128)(2,1)S(1)} %get-tuple-element.44), channel_id=1, source_target_pairs={{0,1},{1,0},{2,3},{3,2},{4,5},{5,4},{6,7},{7,6},{8,9},{9,8},{10,11... | collective-permute-start | bytes 442376 | tf_op jit(solution)/shard_map/ppermute | solution.py:457
  85.3 13.3 %collective-permute-start.15 = (bf16[3,96,256]{2,1,0:T(8,128)(2,1)S(1)}, bf16[3,96,256]{2,1,0:T(8,128)(2,1)S(1)}, u32[]{:S(2)}, u32[]{:S(2)}) collective-permute-start(bf16[3,96,256]{2,1,0:T(8,128)(2,1)S(1)} %get-tuple-element.45), channel_id=1, source_target_pairs={{0,2},{1,3},{2,0},{3,1},{4,6},{5,7},{6,4},{7,5},{8,10},{9,11},{10,... | collective-permute-start | bytes 442376 | tf_op jit(solution)/shard_map/ppermute | solution.py:457
  88.9 10.9 %collective-permute-start.16 = (bf16[3,96,256]{2,1,0:T(8,128)(2,1)S(1)}, bf16[3,96,256]{2,1,0:T(8,128)(2,1)S(1)}, u32[]{:S(2)}, u32[]{:S(2)}) collective-permute-start(bf16[3,96,256]{2,1,0:T(8,128)(2,1)S(1)} %get-tuple-element.46), channel_id=1, source_target_pairs={{0,3},{1,2},{2,1},{3,0},{4,7},{5,6},{6,5},{7,4},{8,11},{9,10},{10,... | collective-permute-start | bytes 442376 | tf_op jit(solution)/shard_map/ppermute | solution.py:457
  (17 other events, 95.7 us)

commit v9 on v7

--- a/solution.py
+++ b/solution.py
@@ -63,7 +63,9 @@
         )
         for s in range(peers)
     ]
-    stores = [pltpu.make_async_copy(buffer.at[s], blocks[s], left.at[s]) for s in range(peers)]
+    stores = [
+        pltpu.make_async_copy(buffer.at[s], blocks[s - 1], left.at[s]) for s in range(1, peers)
+    ]
     light = [
         pltpu.make_async_copy(far_weights, weights, arrived.at[peers]),
         pltpu.make_async_copy(far_tiles, tiles, arrived.at[peers + 1]),
@@ -79,7 +81,8 @@
         ).astype(BF16)
     for s in range(peers):
         loads[s].wait()
-        stores[s].start()
+        if s:
+            stores[s - 1].start()
         mixed = weights[0] * buffer[s, 0].astype(F32)
         for l in range(1, var_count):
             mixed = mixed + weights[l] * buffer[s, l].astype(F32)
@@ -101,8 +104,8 @@
     return pl.pallas_call(
         pack_body,
         in_specs=[scalars()] + [anywhere()] * 3,
-        out_specs=[anywhere()] * peers + [whole()],
-        out_shape=[pltpu.HBM((var_count, own, width), BF16)] * peers + [shape_of((own, obs))],
+        out_specs=[anywhere()] * (peers - 1) + [whole()],
+        out_shape=[pltpu.HBM((var_count, own, width), BF16)] * (peers - 1) + [shape_of((own, obs))],
         scratch_shapes=[
             pltpu.SMEM((var_count,), F32),
             pltpu.VMEM((1, obs), jnp.int32),
@@ -280,6 +283,9 @@
     states, arrived, near, passed = refs[peers + 11 :]
     members = anomalies.shape[1]
     count = gain.shape[0]
+    width = states.shape[3]
+    own_tiles = far_states[0].at[:, :, pl.ds(pl.multiple_of(offset[0], width), width)]
+    far_states = [own_tiles, *far_states[1:]]
     loads = [
         pltpu.make_async_copy(far_states[s].at[:count], states.at[s], arrived.at[s])
         for s in range(peers)
@@ -309,7 +315,7 @@
 
 
 def start_gains(offset, states, packets, anom_0, count, tile_count):
-    var_count, own, width = states[0].shape
+    var_count, own, width = states[1].shape
     peers = len(states)
     members = own * peers
     rows, obs = packets[0].shape
@@ -481,7 +487,7 @@
     packet, sums = stats(me, predicted, values, error, tiles, regions)
     near = swapped(packet, "region", 1)
     far = lax.ppermute(packet, "region", pairs)
-    states = traded(blocks, (1, 3, 2))
+    states = traded([ensemble, *blocks], (1, 3, 2))
     all_sums = exchanged(sums, "region")
     noise = join_noise(noises)
     near_noise = swapped(noise, "region", 1)

time: 102 us -> 100 us (0.980)
  the two profiles are of different devices: /device:TPU:96 before, /device:TPU:24 now
where the time goes in v9:
time: 100 us; the launch traced here: 99.8 us
  starting transfers between devices  38 us (38%)
  waiting for transfers between devices  33.8 us (34%)
  Pallas kernels  15.3 us (15%)
  local copies, waits for them, and re-layouts  11.7 us (12%)
    ppermute x18, waiting for transfers between devices, swapped(): return lax.ppermute(value, axis, pairs)  33.8 us
    ppermute x18, starting transfers between devices, swapped(): return lax.ppermute(value, axis, pairs)  22.6 us
    unnamed x40, local copies, waits for them, and re-layouts  11.7 us
    ppermute x1, starting transfers between devices, shards(): far_noise = lax.ppermute(noise, 'region', pairs)  5.38 us
    ppermute x1, starting transfers between devices, shards(): far = lax.ppermute(packet, 'region', pairs)  5.09 us
    all_to_all x1, starting transfers between devices, exchanged(): return lax.all_to_all(blocks, axis, split_axis=0, concat_axis=0, tiled=True)  4.88 us
    pallas_call x1, Pallas kernels, start_gains(): pl.pallas_call(functools.partial(start_body, peers=peers, tile_count=tile...  4.7 us
    pallas_call x1, Pallas kernels, first_updates(): pl.pallas_call(first_body, in_specs=[whole()] * 9, out_specs=[whole()] *...  2.87 us
  transfers between devices with their start and end apart: 21, of which 11 were waited for; matrix products, arithmetic and copies ran while one was open for 0% of the time, Pallas kernels for 8%

profile of v9, /device:TPU:24, one launch (start us, length us, event | category | flops | bytes accessed | tf_op | source)
XLA Modules:
  0.0 99.8 jit_solution(15629838969076440926)
XLA Ops:
  0.7 2.3 %pack.1 = (bf16[7,96,256]{2,1,0:T(8,128)(2,1)}, bf16[7,96,256]{2,1,0:T(8,128)(2,1)}, bf16[7,96,256]{2,1,0:T(8,128)(2,1)}, bf16[96,512]{1,0:T(8,128)(2,1)S(1)}) custom-call(s32[1]{0:T(128)} %bitcast.me, f32[7]{0:T(128)} %far_weights.1, bf16[7,96,1024]{2,1,0:T(8,128)(2,1)} %refs_0_.1, s32[1,512]{1,0:T(1,128)} %bitcast.13), custom_call_target="tpu_custom_call" | custom-call | tf_op jit(solution)/shard_map/pack/pallas_call | solution.py:104
  4.3 4.9 %collective-permute-done.3.other = bf16[96,512]{1,0:T(8,128)(2,1)S(1)} collective-permute-done((bf16[96,512]{1,0:T(8,128)(2,1)S(1)}, bf16[96,512]{1,0:T(8,128)(2,1)S(1)}, u32[]{:S(2)}, u32[]{:S(2)}) %collective-permute-start.3) | collective-permute-done | bytes 98336 | tf_op jit(solution)/shard_map/ppermute | solution.py:459
  9.3 2.8 %collective-permute-start.6 = (bf16[96,512]{1,0:T(8,128)(2,1)S(1)}, bf16[96,512]{1,0:T(8,128)(2,1)S(1)}, u32[]{:S(2)}, u32[]{:S(2)}) collective-permute-start(bf16[96,512]{1,0:T(8,128)(2,1)S(1)} %join.1.refs_0_), channel_id=1, source_target_pairs={{0,3},{1,2},{2,1},{3,0},{4,7},{5,6},{6,5},{7,4},{8,11},{9,10},{10,... | collective-permute-start | bytes 294920 | tf_op jit(solution)/shard_map/ppermute | solution.py:459
  13.4 2.8 %collective-permute-done.6.refs_3_ = bf16[96,512]{1,0:T(8,128)(2,1)S(1)} collective-permute-done((bf16[96,512]{1,0:T(8,128)(2,1)S(1)}, bf16[96,512]{1,0:T(8,128)(2,1)S(1)}, u32[]{:S(2)}, u32[]{:S(2)}) %collective-permute-start.6) | collective-permute-done | bytes 98336 | tf_op jit(solution)/shard_map/ppermute | solution.py:459
  16.2 2.0 %collective-permute-done.5.refs_2_ = bf16[96,512]{1,0:T(8,128)(2,1)S(1)} collective-permute-done((bf16[96,512]{1,0:T(8,128)(2,1)S(1)}, bf16[96,512]{1,0:T(8,128)(2,1)S(1)}, u32[]{:S(2)}, u32[]{:S(2)}) %collective-permute-start.5) | collective-permute-done | bytes 98336 | tf_op jit(solution)/shard_map/ppermute | solution.py:459
  19.5 2.3 %collective-permute-start.11 = (bf16[96,512]{1,0:T(8,128)(2,1)S(1)}, bf16[96,512]{1,0:T(8,128)(2,1)S(1)}, u32[]{:S(2)}, u32[]{:S(2)}) collective-permute-start(bf16[96,512]{1,0:T(8,128)(2,1)S(1)} %scale.1.refs_0_), channel_id=1, source_target_pairs={{0,3},{1,2},{2,1},{3,0},{4,7},{5,6},{6,5},{7,4},{8,11},{9,10},{10,... | collective-permute-start | bytes 294920 | tf_op jit(solution)/shard_map/ppermute | solution.py:459
  23.7 2.0 %collective-permute-done.11.refs_3_ = bf16[96,512]{1,0:T(8,128)(2,1)S(1)} collective-permute-done((bf16[96,512]{1,0:T(8,128)(2,1)S(1)}, bf16[96,512]{1,0:T(8,128)(2,1)S(1)}, u32[]{:S(2)}, u32[]{:S(2)}) %collective-permute-start.11) | collective-permute-done | bytes 98336 | tf_op jit(solution)/shard_map/ppermute | solution.py:459
  25.8 5.1 %collective-permute-start.8 = (bf16[400,512]{1,0:T(8,128)(2,1)S(1)}, bf16[400,512]{1,0:T(8,128)(2,1)S(1)}, u32[]{:S(2)}, u32[]{:S(2)}) collective-permute-start(bf16[400,512]{1,0:T(8,128)(2,1)S(1)} %get-tuple-element.30.refs_0_.refs_4_), channel_id=1, source_target_pairs={{8,16},{24,32},{40,48},{56,64},{72,80},{88,96},{104,112},{16,8},{3... | collective-permute-start | bytes 1228808 | tf_op jit(solution)/shard_map/ppermute | solution.py:489
  30.9 2.6 %collective-permute-done.10.refs_2_ = bf16[96,512]{1,0:T(8,128)(2,1)S(1)} collective-permute-done((bf16[96,512]{1,0:T(8,128)(2,1)S(1)}, bf16[96,512]{1,0:T(8,128)(2,1)S(1)}, u32[]{:S(2)}, u32[]{:S(2)}) %collective-permute-start.10) | collective-permute-done | bytes 98336 | tf_op jit(solution)/shard_map/ppermute | solution.py:459
  34.1 5.4 %collective-permute-start.13 = (bf16[384,512]{1,0:T(8,128)(2,1)S(1)}, bf16[384,512]{1,0:T(8,128)(2,1)}, u32[]{:S(2)}, u32[]{:S(2)}) collective-permute-start(bf16[384,512]{1,0:T(8,128)(2,1)S(1)} %joinnoise.1.noise_0), channel_id=1, source_target_pairs={{8,16},{24,32},{40,48},{56,64},{72,80},{88,96},{104,112},{16,8},{3... | collective-permute-start | bytes 1179656 | tf_op jit(solution)/shard_map/ppermute | solution.py:494
  40.3 2.0 %collective-permute-start.1 = (bf16[7,96,256]{2,1,0:T(8,128)(2,1)}, bf16[7,96,256]{2,1,0:T(8,128)(2,1)S(1)}, u32[]{:S(2)}, u32[]{:S(2)}) collective-permute-start(bf16[7,96,256]{2,1,0:T(8,128)(2,1)} %get-tuple-element.27), channel_id=1, source_target_pairs={{0,2},{1,3},{2,0},{3,1},{4,6},{5,7},{6,4},{7,5},{8,10},{9,11},{10,... | collective-permute-start | bytes 1032200 | tf_op jit(solution)/shard_map/ppermute | solution.py:459
  43.3 4.9 %all-to-all-start = ((f32[16,1,128]{2,1,0:T(1,128)}), f32[16,1,128]{2,1,0:T(1,128)S(1)}, u32[]{:S(2)}, u32[]{:S(2)}) async-start(f32[16,1,128]{2,1,0:T(1,128)} %bitcast.8), calls=%async_computation | async-start | bytes 16384 | tf_op jit(solution)/shard_map/all_to_all | solution.py:463
  48.6 4.0 %collective-permute-done.1.refs_2_ = bf16[7,96,256]{2,1,0:T(8,128)(2,1)S(1)} collective-permute-done((bf16[7,96,256]{2,1,0:T(8,128)(2,1)}, bf16[7,96,256]{2,1,0:T(8,128)(2,1)S(1)}, u32[]{:S(2)}, u32[]{:S(2)}) %collective-permute-start.1) | collective-permute-done | bytes 344096 | tf_op jit(solution)/shard_map/ppermute | solution.py:459
  53.3 6.5 %collective-permute-done.2.refs_3_ = bf16[7,96,256]{2,1,0:T(8,128)(2,1)S(1)} collective-permute-done((bf16[7,96,256]{2,1,0:T(8,128)(2,1)}, bf16[7,96,256]{2,1,0:T(8,128)(2,1)S(1)}, u32[]{:S(2)}, u32[]{:S(2)}) %collective-permute-start.2) | collective-permute-done | bytes 344096 | tf_op jit(solution)/shard_map/ppermute | solution.py:459
  62.6 4.7 %start.1 = (bf16[512,384]{1,0:T(8,128)(2,1)S(1)}, f32[1536,256]{1,0:T(8,128)S(1)}, f32[4,8,256]{2,1,0:T(8,128)S(1)}, bf16[4,384,256]{2,1,0:T(8,128)(2,1)S(1)}, b...) custom-call(s32[4]{0:T(128)S(1)} %pad_add_fusion.offset, ...), custom_call_target="tpu_custom_call" | custom-call | tf_op jit(solution)/shard_map/start/pallas_call | solution.py:322
  67.3 1.6 %copy-done = bf16[4,1536,256]{2,1,0:T(8,128)(2,1)} copy-done((bf16[4,1536,256]{2,1,0:T(8,128)(2,1)}, bf16[4,1536,256]{2,1,0:T(8,128)(2,1)S(1)}, u32[]{:S(2)}) %copy-start) | copy-done | bytes 3145752
  71.9 1.9 %copy-done.1 = bf16[4,1536,256]{2,1,0:T(8,128)(2,1)S(1)} copy-done((bf16[4,1536,256]{2,1,0:T(8,128)(2,1)S(1)}, bf16[4,1536,256]{2,1,0:T(8,128)(2,1)}, u32[]{:S(2)}) %copy-start.1) | copy-done | bytes 3145752
  74.9 2.9 %first.1 = (bf16[4,96,256]{2,1,0:T(8,128)(2,1)S(1)}, bf16[4,96,256]{2,1,0:T(8,128)(2,1)S(1)}, bf16[4,96,256]{2,1,0:T(8,128)(2,1)S(1)}, bf16[4,96,256]{2,1,0:T(8,...) custom-call(f32[4,8,256]{2,1,0:T(8,128)S(1)} %get-tuple-element.32.means, ...), custom_call_target="tpu_custom_call" | custom-call | tf_op jit(solution)/shard_map/first/pallas_call | solution.py:385
  78.2 2.7 %collective-permute-start.18 = (bf16[4,96,256]{2,1,0:T(8,128)(2,1)S(1)}, bf16[4,96,256]{2,1,0:T(8,128)(2,1)S(1)}, u32[]{:S(2)}, u32[]{:S(2)}) collective-permute-start(bf16[4,96,256]{2,1,0:T(8,128)(2,1)S(1)} %get-tuple-element.47), channel_id=1, source_target_pairs={{0,2},{1,3},{2,0},{3,1},{4,6},{5,7},{6,4},{7,5},{8,10},{9,11},{10,... | collective-permute-start | bytes 589832 | tf_op jit(solution)/shard_map/ppermute | solution.py:459
  80.9 1.6 %collective-permute-start.19 = (bf16[4,96,256]{2,1,0:T(8,128)(2,1)S(1)}, bf16[4,96,256]{2,1,0:T(8,128)(2,1)S(1)}, u32[]{:S(2)}, u32[]{:S(2)}) collective-permute-start(bf16[4,96,256]{2,1,0:T(8,128)(2,1)S(1)} %get-tuple-element.48), channel_id=1, source_target_pairs={{0,3},{1,2},{2,1},{3,0},{4,7},{5,6},{6,5},{7,4},{8,11},{9,10},{10,... | collective-permute-start | bytes 589832 | tf_op jit(solution)/shard_map/ppermute | solution.py:459
  82.5 2.4 %second.1 = (bf16[3,96,256]{2,1,0:T(8,128)(2,1)S(1)}, bf16[3,96,256]{2,1,0:T(8,128)(2,1)S(1)}, bf16[3,96,256]{2,1,0:T(8,128)(2,1)S(1)}, bf16[3,96,256]{2,1,0:T(8,128)(2,1)S(1)}) custom-call(bf16[4,3,96,256]{3,2,1,0:T(8,128)(2,1)S(1)} %copy-done.9, bf16[384,1536]{1,0:T(8,128)(2,1)S(1)} %get-tuple-element.37.perturbed, f32[8,128]{1,0:T(8,128)S(1)} %get-tuple-element.38.root, ...), custom_call_target="tpu_custom_call" | custom-call | tf_op jit(solution)/shard_map/second/pallas_call | solution.py:414
  85.0 3.1 %collective-permute-start.15 = (bf16[3,96,256]{2,1,0:T(8,128)(2,1)S(1)}, bf16[3,96,256]{2,1,0:T(8,128)(2,1)S(1)}, u32[]{:S(2)}, u32[]{:S(2)}) collective-permute-start(bf16[3,96,256]{2,1,0:T(8,128)(2,1)S(1)} %get-tuple-element.43), channel_id=1, source_target_pairs={{0,2},{1,3},{2,0},{3,1},{4,6},{5,7},{6,4},{7,5},{8,10},{9,11},{10,... | collective-permute-start | bytes 442376 | tf_op jit(solution)/shard_map/ppermute | solution.py:459
  88.1 1.6 %collective-permute-start.16 = (bf16[3,96,256]{2,1,0:T(8,128)(2,1)S(1)}, bf16[3,96,256]{2,1,0:T(8,128)(2,1)S(1)}, u32[]{:S(2)}, u32[]{:S(2)}) collective-permute-start(bf16[3,96,256]{2,1,0:T(8,128)(2,1)S(1)} %get-tuple-element.44), channel_id=1, source_target_pairs={{0,3},{1,2},{2,1},{3,0},{4,7},{5,6},{6,5},{7,4},{8,11},{9,10},{10,... | collective-permute-start | bytes 442376 | tf_op jit(solution)/shard_map/ppermute | solution.py:459
  90.9 5.9 %collective-permute-done.19.refs_3_ = bf16[4,96,256]{2,1,0:T(8,128)(2,1)S(1)} collective-permute-done((bf16[4,96,256]{2,1,0:T(8,128)(2,1)S(1)}, bf16[4,96,256]{2,1,0:T(8,128)(2,1)S(1)}, u32[]{:S(2)}, u32[]{:S(2)}) %collective-permute-start.19) | collective-permute-done | bytes 196640 | tf_op jit(solution)/shard_map/ppermute | solution.py:459
  (70 shorter events, 20.7 us)
Async XLA Ops:
  0.7 18.8 %copy-start.16 = (f32[96,512]{1,0:T(8,128)S(1)}, f32[96,512]{1,0:T(8,128)}, u32[]{:S(2)}) copy-start(f32[96,512]{1,0:T(8,128)} %noise.1) | copy-start | bytes 589828
  3.0 6.2 %collective-permute-start.3 = (bf16[96,512]{1,0:T(8,128)(2,1)S(1)}, bf16[96,512]{1,0:T(8,128)(2,1)S(1)}, u32[]{:S(2)}, u32[]{:S(2)}) collective-permute-start(bf16[96,512]{1,0:T(8,128)(2,1)S(1)} %get-tuple-element.29.mine), channel_id=1, source_target_pairs={{0,4},{4,0},{1,5},{5,1},{2,6},{6,2},{3,7},{7,3},{8,12},{12,8},{9,1... | collective-permute-start | bytes 294920 | tf_op jit(solution)/shard_map/ppermute | solution.py:459
  9.3 7.0 %collective-permute-start.6 = (bf16[96,512]{1,0:T(8,128)(2,1)S(1)}, bf16[96,512]{1,0:T(8,128)(2,1)S(1)}, u32[]{:S(2)}, u32[]{:S(2)}) collective-permute-start(bf16[96,512]{1,0:T(8,128)(2,1)S(1)} %join.1.refs_0_), channel_id=1, source_target_pairs={{0,3},{1,2},{2,1},{3,0},{4,7},{5,6},{6,5},{7,4},{8,11},{9,10},{10,... | collective-permute-start | bytes 294920 | tf_op jit(solution)/shard_map/ppermute | solution.py:459
  12.1 6.1 %collective-permute-start.5 = (bf16[96,512]{1,0:T(8,128)(2,1)S(1)}, bf16[96,512]{1,0:T(8,128)(2,1)S(1)}, u32[]{:S(2)}, u32[]{:S(2)}) collective-permute-start(bf16[96,512]{1,0:T(8,128)(2,1)S(1)} %join.1.refs_0_), channel_id=1, source_target_pairs={{0,2},{1,3},{2,0},{3,1},{4,6},{5,7},{6,4},{7,5},{8,10},{9,11},{10,... | collective-permute-start | bytes 294920 | tf_op jit(solution)/shard_map/ppermute | solution.py:459
  12.9 5.3 %collective-permute-start.4 = (bf16[96,512]{1,0:T(8,128)(2,1)S(1)}, bf16[96,512]{1,0:T(8,128)(2,1)S(1)}, u32[]{:S(2)}, u32[]{:S(2)}) collective-permute-start(bf16[96,512]{1,0:T(8,128)(2,1)S(1)} %join.1.refs_0_), channel_id=1, source_target_pairs={{0,1},{1,0},{2,3},{3,2},{4,5},{5,4},{6,7},{7,6},{8,9},{9,8},{10,11... | collective-permute-start | bytes 294920 | tf_op jit(solution)/shard_map/ppermute | solution.py:459
  19.2 29.4 %copy-start.2 = (bf16[400,512]{1,0:T(8,128)(2,1)}, bf16[400,512]{1,0:T(8,128)(2,1)S(1)}, u32[]{:S(2)}) copy-start(bf16[400,512]{1,0:T(8,128)(2,1)S(1)} %get-tuple-element.30.refs_0_.refs_4_) | copy-start | bytes 1228804
  19.2 23.2 %collective-permute-start.7 = (bf16[400,512]{1,0:T(8,128)(2,1)S(1)}, bf16[400,512]{1,0:T(8,128)(2,1)S(1)}, u32[]{:S(2)}, u32[]{:S(2)}) collective-permute-start(bf16[400,512]{1,0:T(8,128)(2,1)S(1)} %get-tuple-element.30.refs_0_.refs_4_), channel_id=1, source_target_pairs={{0,8},{8,0},{16,24},{24,16},{32,40},{40,32},{48,56},{56,48},{64,72... | collective-permute-start | bytes 1228808 | tf_op jit(solution)/shard_map/ppermute | solution.py:459
  19.2 20.4 %collective-permute-start = (bf16[7,96,256]{2,1,0:T(8,128)(2,1)}, bf16[7,96,256]{2,1,0:T(8,128)(2,1)S(1)}, u32[]{:S(2)}, u32[]{:S(2)}) collective-permute-start(bf16[7,96,256]{2,1,0:T(8,128)(2,1)} %get-tuple-element.26), channel_id=1, source_target_pairs={{0,1},{1,0},{2,3},{3,2},{4,5},{5,4},{6,7},{7,6},{8,9},{9,8},{10,11... | collective-permute-start | bytes 1032200 | tf_op jit(solution)/shard_map/ppermute | solution.py:459
  19.5 6.2 %collective-permute-start.11 = (bf16[96,512]{1,0:T(8,128)(2,1)S(1)}, bf16[96,512]{1,0:T(8,128)(2,1)S(1)}, u32[]{:S(2)}, u32[]{:S(2)}) collective-permute-start(bf16[96,512]{1,0:T(8,128)(2,1)S(1)} %scale.1.refs_0_), channel_id=1, source_target_pairs={{0,3},{1,2},{2,1},{3,0},{4,7},{5,6},{6,5},{7,4},{8,11},{9,10},{10,... | collective-permute-start | bytes 294920 | tf_op jit(solution)/shard_map/ppermute | solution.py:459
  21.9 11.6 %collective-permute-start.10 = (bf16[96,512]{1,0:T(8,128)(2,1)S(1)}, bf16[96,512]{1,0:T(8,128)(2,1)S(1)}, u32[]{:S(2)}, u32[]{:S(2)}) collective-permute-start(bf16[96,512]{1,0:T(8,128)(2,1)S(1)} %scale.1.refs_0_), channel_id=1, source_target_pairs={{0,2},{1,3},{2,0},{3,1},{4,6},{5,7},{6,4},{7,5},{8,10},{9,11},{10,... | collective-permute-start | bytes 294920 | tf_op jit(solution)/shard_map/ppermute | solution.py:459
  23.4 10.7 %collective-permute-start.9 = (bf16[96,512]{1,0:T(8,128)(2,1)S(1)}, bf16[96,512]{1,0:T(8,128)(2,1)S(1)}, u32[]{:S(2)}, u32[]{:S(2)}) collective-permute-start(bf16[96,512]{1,0:T(8,128)(2,1)S(1)} %scale.1.refs_0_), channel_id=1, source_target_pairs={{0,1},{1,0},{2,3},{3,2},{4,5},{5,4},{6,7},{7,6},{8,9},{9,8},{10,11... | collective-permute-start | bytes 294920 | tf_op jit(solution)/shard_map/ppermute | solution.py:459
  25.8 34.9 %collective-permute-start.8 = (bf16[400,512]{1,0:T(8,128)(2,1)S(1)}, bf16[400,512]{1,0:T(8,128)(2,1)S(1)}, u32[]{:S(2)}, u32[]{:S(2)}) collective-permute-start(bf16[400,512]{1,0:T(8,128)(2,1)S(1)} %get-tuple-element.30.refs_0_.refs_4_), channel_id=1, source_target_pairs={{8,16},{24,32},{40,48},{56,64},{72,80},{88,96},{104,112},{16,8},{3... | collective-permute-start | bytes 1228808 | tf_op jit(solution)/shard_map/ppermute | solution.py:489
  34.1 37.7 %collective-permute-start.13 = (bf16[384,512]{1,0:T(8,128)(2,1)S(1)}, bf16[384,512]{1,0:T(8,128)(2,1)}, u32[]{:S(2)}, u32[]{:S(2)}) collective-permute-start(bf16[384,512]{1,0:T(8,128)(2,1)S(1)} %joinnoise.1.noise_0), channel_id=1, source_target_pairs={{8,16},{24,32},{40,48},{56,64},{72,80},{88,96},{104,112},{16,8},{3... | collective-permute-start | bytes 1179656 | tf_op jit(solution)/shard_map/ppermute | solution.py:494
  39.5 32.4 %collective-permute-start.12 = (bf16[384,512]{1,0:T(8,128)(2,1)S(1)}, bf16[384,512]{1,0:T(8,128)(2,1)}, u32[]{:S(2)}, u32[]{:S(2)}) collective-permute-start(bf16[384,512]{1,0:T(8,128)(2,1)S(1)} %joinnoise.1.noise_0), channel_id=1, source_target_pairs={{0,8},{8,0},{16,24},{24,16},{32,40},{40,32},{48,56},{56,48},{64,72... | collective-permute-start | bytes 1179656 | tf_op jit(solution)/shard_map/ppermute | solution.py:459
  40.3 12.3 %collective-permute-start.1 = (bf16[7,96,256]{2,1,0:T(8,128)(2,1)}, bf16[7,96,256]{2,1,0:T(8,128)(2,1)S(1)}, u32[]{:S(2)}, u32[]{:S(2)}) collective-permute-start(bf16[7,96,256]{2,1,0:T(8,128)(2,1)} %get-tuple-element.27), channel_id=1, source_target_pairs={{0,2},{1,3},{2,0},{3,1},{4,6},{5,7},{6,4},{7,5},{8,10},{9,11},{10,... | collective-permute-start | bytes 1032200 | tf_op jit(solution)/shard_map/ppermute | solution.py:459
  42.3 18.3 %copy-start.3 = (bf16[400,512]{1,0:T(8,128)(2,1)}, bf16[400,512]{1,0:T(8,128)(2,1)S(1)}, u32[]{:S(2)}) copy-start(bf16[400,512]{1,0:T(8,128)(2,1)S(1)} %collective-permute-done.7.refs_1_.refs_5_) | copy-start | bytes 1228804
  42.3 17.5 %collective-permute-start.2 = (bf16[7,96,256]{2,1,0:T(8,128)(2,1)}, bf16[7,96,256]{2,1,0:T(8,128)(2,1)S(1)}, u32[]{:S(2)}, u32[]{:S(2)}) collective-permute-start(bf16[7,96,256]{2,1,0:T(8,128)(2,1)} %get-tuple-element.28), channel_id=1, source_target_pairs={{0,3},{1,2},{2,1},{3,0},{4,7},{5,6},{6,5},{7,4},{8,11},{9,10},{10,... | collective-permute-start | bytes 1032200 | tf_op jit(solution)/shard_map/ppermute | solution.py:459
  43.3 28.5 %all-to-all-start = ((f32[16,1,128]{2,1,0:T(1,128)}), f32[16,1,128]{2,1,0:T(1,128)S(1)}, u32[]{:S(2)}, u32[]{:S(2)}) async-start(f32[16,1,128]{2,1,0:T(1,128)} %bitcast.8), calls=%async_computation | async-start | bytes 16384 | tf_op jit(solution)/shard_map/all_to_all | solution.py:463
  77.8 10.3 %collective-permute-start.17 = (bf16[4,96,256]{2,1,0:T(8,128)(2,1)S(1)}, bf16[4,96,256]{2,1,0:T(8,128)(2,1)S(1)}, u32[]{:S(2)}, u32[]{:S(2)}) collective-permute-start(bf16[4,96,256]{2,1,0:T(8,128)(2,1)S(1)} %get-tuple-element.46), channel_id=1, source_target_pairs={{0,1},{1,0},{2,3},{3,2},{4,5},{5,4},{6,7},{7,6},{8,9},{9,8},{10,11... | collective-permute-start | bytes 589832 | tf_op jit(solution)/shard_map/ppermute | solution.py:459
  78.2 12.7 %collective-permute-start.18 = (bf16[4,96,256]{2,1,0:T(8,128)(2,1)S(1)}, bf16[4,96,256]{2,1,0:T(8,128)(2,1)S(1)}, u32[]{:S(2)}, u32[]{:S(2)}) collective-permute-start(bf16[4,96,256]{2,1,0:T(8,128)(2,1)S(1)} %get-tuple-element.47), channel_id=1, source_target_pairs={{0,2},{1,3},{2,0},{3,1},{4,6},{5,7},{6,4},{7,5},{8,10},{9,11},{10,... | collective-permute-start | bytes 589832 | tf_op jit(solution)/shard_map/ppermute | solution.py:459
  80.9 15.9 %collective-permute-start.19 = (bf16[4,96,256]{2,1,0:T(8,128)(2,1)S(1)}, bf16[4,96,256]{2,1,0:T(8,128)(2,1)S(1)}, u32[]{:S(2)}, u32[]{:S(2)}) collective-permute-start(bf16[4,96,256]{2,1,0:T(8,128)(2,1)S(1)} %get-tuple-element.48), channel_id=1, source_target_pairs={{0,3},{1,2},{2,1},{3,0},{4,7},{5,6},{6,5},{7,4},{8,11},{9,10},{10,... | collective-permute-start | bytes 589832 | tf_op jit(solution)/shard_map/ppermute | solution.py:459
  84.9 12.8 %collective-permute-start.14 = (bf16[3,96,256]{2,1,0:T(8,128)(2,1)S(1)}, bf16[3,96,256]{2,1,0:T(8,128)(2,1)S(1)}, u32[]{:S(2)}, u32[]{:S(2)}) collective-permute-start(bf16[3,96,256]{2,1,0:T(8,128)(2,1)S(1)} %get-tuple-element.42), channel_id=1, source_target_pairs={{0,1},{1,0},{2,3},{3,2},{4,5},{5,4},{6,7},{7,6},{8,9},{9,8},{10,11... | collective-permute-start | bytes 442376 | tf_op jit(solution)/shard_map/ppermute | solution.py:459
  85.0 12.7 %collective-permute-start.15 = (bf16[3,96,256]{2,1,0:T(8,128)(2,1)S(1)}, bf16[3,96,256]{2,1,0:T(8,128)(2,1)S(1)}, u32[]{:S(2)}, u32[]{:S(2)}) collective-permute-start(bf16[3,96,256]{2,1,0:T(8,128)(2,1)S(1)} %get-tuple-element.43), channel_id=1, source_target_pairs={{0,2},{1,3},{2,0},{3,1},{4,6},{5,7},{6,4},{7,5},{8,10},{9,11},{10,... | collective-permute-start | bytes 442376 | tf_op jit(solution)/shard_map/ppermute | solution.py:459
  88.1 10.8 %collective-permute-start.16 = (bf16[3,96,256]{2,1,0:T(8,128)(2,1)S(1)}, bf16[3,96,256]{2,1,0:T(8,128)(2,1)S(1)}, u32[]{:S(2)}, u32[]{:S(2)}) collective-permute-start(bf16[3,96,256]{2,1,0:T(8,128)(2,1)S(1)} %get-tuple-element.44), channel_id=1, source_target_pairs={{0,3},{1,2},{2,1},{3,0},{4,7},{5,6},{6,5},{7,4},{8,11},{9,10},{10,... | collective-permute-start | bytes 442376 | tf_op jit(solution)/shard_map/ppermute | solution.py:459
  (17 other events, 92.2 us)
